TPU v7x, 256 devices: a whole 4x4x8 slice. The times are simulated.
256 devices in a mesh: gx: 8 (over x, core), gy: 4 (over y), gz: 8 (over z).
Axes of the slice: x: 4, y: 4, z: 8, core: 2. Of those that a mesh axis runs over, the one named last changes fastest.
Arguments:
- offset: float32 [3, 8, 8, 16, 1024], P(None, None, 'gx', 'gy', 'gz'), may hold values from 0.05 to 0.95, as said below
- velocity: float32 [3, 8, 8, 16, 1024], P(None, None, 'gx', 'gy', 'gz'), may hold values from -11 to 11
- occupancy: int32 [8, 16, 1024], P('gx', 'gy', 'gz'), may hold values from 1 to 8
- noise: bfloat16 [14, 8, 8, 8, 16, 1024], P(None, None, None, 'gx', 'gy', 'gz'), may hold values from -4 to 4
Outputs:
- interaction_push_per_bead: float32 [3, 8, 8, 16, 1024], P(None, None, 'gx', 'gy', 'gz')
- stress_matrix: float32 [3, 3], replicated
- thermal_level: float32 [1], replicated
Inputs may be any that keep to these rules, and one draw needn't show every extreme that they name: `offset`: two beads of the grid are never closer than 0.1. `occupancy`: at most 8 beads a cell, in its first slots.
All inputs are finite; a program needn't handle non-finite values.
Results may differ from a plain program's by a relative error of at most 0.0003.
Values may be sent and summed in bfloat16 or wider, within the bound.
No kernel may reach another device: no remote copies, remote signals or barrier semaphores. Data moves between devices by JAX's collectives and lax.ppermute only.
A program may use at most 64 MiB of HBM per device.

v0:
```python
import jax
import jax.numpy as jnp
from jax import lax
from jax.experimental import pallas as pl
from jax.experimental.pallas import tpu as pltpu
from jax.sharding import PartitionSpec as P

AXES = ("gx", "gy", "gz")
ROWS = 4
LANES = 128
SLOTS = 8
FAR = 100.0
NOISE_SCALE = 15.0
REST = 25.0 / 15.0
DRAG = 4.5 / 15.0
HALF_ROOT = 0.7071067811865476


def tile_index(dx, dy, dz):
    if dz == 1:
        return 5 + (dy + 1) * 3 + (dx + 1)
    return {(0, 0): 0, (1, 0): 1, (-1, 1): 2, (0, 1): 3, (1, 1): 4}[(dx, dy)]


COLUMN_TILES = {
    0: [(0, 0), (1, 0), (-1, 1), (0, 1), (1, 1)],
    1: [(0, 0), (1, 0), (-1, 1), (0, 1), (1, 1)],
    -1: [(1, 0), (-1, 1), (0, 1), (1, 1)],
}
PRODUCTS = [(0, 0), (0, 1), (0, 2), (1, 1), (1, 2), (2, 2)]


def lane_iota():
    return lax.broadcasted_iota(jnp.int32, (SLOTS, LANES), 1)


def slot_iota():
    return lax.broadcasted_iota(jnp.int32, (SLOTS, LANES), 0)


def row_of(ref, *index):
    *lead, s = index
    return jnp.broadcast_to(ref[(*lead, pl.ds(s, 1), slice(None))], (SLOTS, LANES))


def pack_kernel(off_ref, vel_ref, occ_ref, v_ref, ownx_ref, z_ref):
    lane = lane_iota()
    slot = slot_iota()
    z = jnp.zeros((SLOTS, LANES), jnp.float32)
    for y in range(ROWS):
        live = slot < jnp.broadcast_to(occ_ref[pl.ds(y, 1), :], (SLOTS, LANES))
        for c in range(6):
            if c < 3:
                val = off_ref[c, pl.ds(y, SLOTS, stride=ROWS), :]
                if c == 0:
                    ownx_ref[y] = jnp.where(live, val, FAR)
                    val = jnp.where(live, val, -FAR)
            else:
                val = vel_ref[c - 3, pl.ds(y, SLOTS, stride=ROWS), :] * DRAG
            v_ref[y * 6 + c] = val
            at = (y + 1) * 6 + c
            z = jnp.where(lane == at, pltpu.roll(val, at, 1), z)
    z_ref[...] = z


def widen_kernel(v_ref, zr_ref, ym_ref, yp_ref, m_ref):
    lane = lane_iota()
    for c in range(6):
        m_ref[c] = ym_ref[c]
        m_ref[30 + c] = yp_ref[c]
        for y in range(ROWS):
            m_ref[(y + 1) * 6 + c] = v_ref[y * 6 + c]
    z = jnp.where(lane < 6, pltpu.roll(ym_ref[6], LANES - 24, 1), zr_ref[...])
    z = jnp.where((lane >= 30) & (lane < 36), pltpu.roll(yp_ref[6], 24, 1), z)
    m_ref[36] = z


def next_plane(m_ref, dx, up_ref):
    lane = lane_iota()
    z = m_ref[36]
    for row in range(6):
        for c in range(6):
            at = row * 6 + c
            val = pltpu.roll(m_ref[at], LANES - 1, 1)
            val = jnp.where(lane == LANES - 1, pltpu.roll(z, LANES - 1 - at, 1), val)
            if c == 2:
                val = val + 1.0
            up_ref[at] = val


def row_pairs(y, columns, own_ref, ownx_ref, th_ref, rl_refs, ru_refs, vir):
    slot = slot_iota()
    d = [[None] * 3 for _ in range(SLOTS)]
    for dx, level_ref, up_ref in columns:
        for dy, dz in COLUMN_TILES[dx]:
            k = tile_index(dx, dy, dz)
            src = up_ref if dz else level_ref
            base = (y + 1 + dy) * 6
            oth = [src[base + c] for c in range(6)]
            if dx:
                oth[0] = oth[0] + float(dx)
            if dy:
                oth[1] = oth[1] + float(dy)
            r = [None] * 3
            for s in range(SLOTS):
                if k == 0 and s == SLOTS - 1:
                    continue
                own = [row_of(ownx_ref, y, s)] + [row_of(own_ref, (y + 1) * 6 + c, s) for c in range(1, 6)]
                sep = [own[a] - oth[a] for a in range(3)]
                rel = [own[3 + a] - oth[3 + a] for a in range(3)]
                dist2 = sep[0] * sep[0] + sep[1] * sep[1] + sep[2] * sep[2]
                u = jnp.maximum(lax.rsqrt(dist2) - 1.0, 0.0)
                dot = sep[0] * rel[0] + sep[1] * rel[1] + sep[2] * rel[2]
                theta = th_ref[pl.ds(k * 256 + s * 32 + y, SLOTS, stride=ROWS), :]
                if k == 0:
                    theta = (theta + th_ref[pl.ds(s * ROWS + y, SLOTS, stride=32), :]) * HALF_ROOT
                fr = u * ((theta + REST) - u * dot)
                if k == 0:
                    fr = jnp.where(slot > s, fr, 0.0)
                for a in range(3):
                    f = fr * sep[a]
                    d[s][a] = f if d[s][a] is None else d[s][a] + f
                    r[a] = f if r[a] is None else r[a] + f
            ref = (ru_refs if dz else rl_refs)[dx]
            at = (y + 1 + dy) * 3
            for a in range(3):
                ref[at + a] = ref[at + a] + r[a]
            vir = [t - oth[a] * r[b] for t, (a, b) in zip(vir, PRODUCTS)]
    for s in range(SLOTS):
        own = [row_of(ownx_ref, y, s)] + [row_of(own_ref, (y + 1) * 6 + c, s) for c in range(1, 3)]
        vir = [t + own[a] * d[s][b] for t, (a, b) in zip(vir, PRODUCTS)]
    return d, vir


def settle(rl_ref, ru_ref, out_ref):
    lane = lane_iota()
    z = jnp.zeros((SLOTS, LANES), jnp.float32)
    for at in range(18):
        up = ru_ref[at]
        z = jnp.where(lane == at, pltpu.roll(up, at + 1, 1), z)
        out_ref[1 + at] = rl_ref[at] + jnp.where(lane == 0, 0.0, pltpu.roll(up, 1, 1))
    out_ref[0] = z
    out_ref[19] = z


def own_column_kernel(m_ref, ownx_ref, th_ref, d_ref, r_ref, acc_ref, up_ref, rl_ref, ru_ref):
    next_plane(m_ref, 0, up_ref)
    zero = jnp.zeros((18, SLOTS, LANES), jnp.float32)
    rl_ref[...] = zero
    ru_ref[...] = zero
    acc_ref[...] = jnp.zeros((16, SLOTS, LANES), jnp.float32)

    @pl.loop(0, ROWS)
    def _(y):
        vir = [acc_ref[i] for i in range(6)]
        d, vir = row_pairs(y, [(0, m_ref, up_ref)], m_ref, ownx_ref, th_ref, {0: rl_ref}, {0: ru_ref}, vir)
        for i in range(6):
            acc_ref[i] = vir[i]
        for s in range(SLOTS):
            for a in range(3):
                part = d[s][a]
                d_ref[y * 3 + a, pl.ds(s, 1), :] = jnp.sum(part, axis=0, keepdims=True)
        base = (y + 1) * 6
        live = jnp.where(m_ref[base] > -0.5 * FAR, 1.0, 0.0)
        vel = [m_ref[base + 3 + a] for a in range(3)]
        for i, (a, b) in enumerate(PRODUCTS):
            acc_ref[6 + i] = acc_ref[6 + i] + live * vel[a] * vel[b]
        acc_ref[12] = acc_ref[12] + live

    settle(rl_ref, ru_ref, r_ref)


def side_columns_kernel(
    m_ref, ownx_ref, th_ref, xm_ref, xp_ref, d0_ref, acc0_ref,
    d_ref, rm_ref, rp_ref, tally_ref,
    um_ref, up_ref, rlm_ref, rum_ref, rlp_ref, rup_ref, acc_ref,
):
    next_plane(xm_ref, -1, um_ref)
    next_plane(xp_ref, 1, up_ref)
    zero = jnp.zeros((18, SLOTS, LANES), jnp.float32)
    for ref in (rlm_ref, rum_ref, rlp_ref, rup_ref):
        ref[...] = zero
    acc_ref[...] = acc0_ref[...]

    @pl.loop(0, ROWS)
    def _(y):
        vir = [acc_ref[i] for i in range(6)]
        d, vir = row_pairs(
            y, [(1, xp_ref, up_ref), (-1, xm_ref, um_ref)], m_ref, ownx_ref, th_ref,
            {1: rlp_ref, -1: rlm_ref}, {1: rup_ref, -1: rum_ref}, vir,
        )
        for i in range(6):
            acc_ref[i] = vir[i]
        for s in range(SLOTS):
            for a in range(3):
                at = (y * 3 + a, pl.ds(s, 1), slice(None))
                d_ref[at] = d0_ref[at] + jnp.sum(d[s][a], axis=0, keepdims=True)

    settle(rlm_ref, rum_ref, rm_ref)
    settle(rlp_ref, rup_ref, rp_ref)
    lane = lax.broadcasted_iota(jnp.int32, (16, LANES), 1)
    line = lax.broadcasted_iota(jnp.int32, (16, LANES), 0)
    sums = jnp.sum(jnp.sum(acc_ref[...], axis=1), axis=1, keepdims=True)
    tally = jnp.sum(jnp.where(lane == line, sums, 0.0), axis=0, keepdims=True)
    tally_ref[...] = jnp.broadcast_to(tally, tally_ref.shape)


def last_plane_kernel(sz_ref, ym_ref, yp_ref, z_ref):
    lane = lane_iota()
    z = sz_ref[...]
    z = z + jnp.where((lane >= 3) & (lane < 6), pltpu.roll(ym_ref[...], LANES - 12, 1), 0.0)
    z = z + jnp.where((lane >= 12) & (lane < 15), pltpu.roll(yp_ref[...], 12, 1), 0.0)
    z_ref[...] = z


def finish_kernel(d_ref, s_ref, ym_ref, yp_ref, z_ref, f_ref):
    lane = lane_iota()
    for y in range(ROWS):
        for a in range(3):
            at = (y + 1) * 3 + a
            back = s_ref[1 + at]
            if y == 0:
                back = back + ym_ref[a]
            if y == ROWS - 1:
                back = back + yp_ref[1 + a]
            back = back + jnp.where(lane == 0, pltpu.roll(z_ref[...], LANES - at, 1), 0.0)
            f_ref[a, pl.ds(y, SLOTS, stride=ROWS), :] = NOISE_SCALE * (d_ref[y * 3 + a] - back)


def f32(*shape):
    return jax.ShapeDtypeStruct(shape, jnp.float32)


def vmem(*shape):
    return pltpu.VMEM(shape, jnp.float32)


def call(kernel, out_shape, scratch=()):
    return pl.pallas_call(kernel, out_shape=out_shape, scratch_shapes=list(scratch), name=kernel.__name__)


def shifted(shard, axis, by):
    count = lax.axis_size(axis)
    return lax.ppermute(shard, axis, [(i, (i + by) % count) for i in range(count)])


def per_device(offset, velocity, occupancy, noise):
    off = offset.reshape(3, SLOTS * ROWS, LANES)
    vel = velocity.reshape(3, SLOTS * ROWS, LANES)
    occ = occupancy.reshape(ROWS, LANES)
    theta = noise.reshape(14 * SLOTS * SLOTS * ROWS, LANES).astype(jnp.float32)
    v, ownx, z = call(pack_kernel, (f32(24, SLOTS, LANES), f32(ROWS, SLOTS, LANES), f32(SLOTS, LANES)))(off, vel, occ)
    zr = shifted(z, "gz", -1)
    from_ym = shifted(jnp.concatenate([v[18:24], zr[None]]), "gy", 1)
    from_yp = shifted(jnp.concatenate([v[0:6], zr[None]]), "gy", -1)
    m = call(widen_kernel, f32(37, SLOTS, LANES))(v, zr, from_ym, from_yp)
    from_xm = shifted(m, "gx", 1)
    from_xp = shifted(m, "gx", -1)
    tile = (SLOTS, LANES)
    d0, r0, acc0 = call(
        own_column_kernel,
        (f32(12, *tile), f32(20, *tile), f32(16, *tile)),
        [vmem(36, *tile), vmem(18, *tile), vmem(18, *tile)],
    )(m, ownx, theta)
    devices = lax.axis_size(AXES)
    d, rm, rp, tally = call(
        side_columns_kernel,
        (f32(12, *tile), f32(20, *tile), f32(20, *tile), f32(devices, LANES)),
        [vmem(36, *tile)] * 2 + [vmem(18, *tile)] * 4 + [vmem(16, *tile)],
    )(m, ownx, theta, from_xm, from_xp, d0, acc0)
    s = r0 + shifted(rp, "gx", 1) + shifted(rm, "gx", -1)
    back_ym = shifted(s[16:20], "gy", 1)
    back_yp = shifted(s[0:4], "gy", -1)
    home = call(last_plane_kernel, f32(*tile))(s[0], back_ym[3], back_yp[0])
    arrived = shifted(home, "gz", 1)
    force = call(finish_kernel, f32(3, SLOTS * ROWS, LANES))(d, s, back_ym, back_yp, arrived)
    tallies = lax.all_to_all(tally, AXES, 0, 0, tiled=True)
    total = jnp.sum(tallies, axis=0)
    virial = NOISE_SCALE * total[0:6]
    kinetic = total[6:12] / (DRAG * DRAG)
    count = total[12]
    cells = ROWS * LANES * devices
    stress = (kinetic + virial) / cells
    order = [PRODUCTS.index((min(a, b), max(a, b))) for a in range(3) for b in range(3)]
    stress_matrix = jnp.stack([stress[i] for i in order]).reshape(3, 3)
    thermal_level = jnp.reshape((kinetic[0] + kinetic[3] + kinetic[5]) / (3.0 * count - 3.0), (1,))
    return force.reshape(offset.shape), stress_matrix, thermal_level


def solution(mesh):
    spec = P(None, None, *AXES)
    return jax.shard_map(
        per_device,
        mesh=mesh,
        in_specs=(spec, spec, P(*AXES), P(None, None, None, *AXES)),
        out_specs=(spec, P(), P()),
        check_vma=False,
    )
```

profile of v0, /device:TPU:1, one launch (start us, length us, event | category | flops | bytes accessed | tf_op | source)
XLA Modules:
  0.0 67.5 jit_solution(11669161960334417725)
XLA Ops:
  0.6 1.5 %pack_kernel.1 = (f32[24,8,128]{2,1,0:T(8,128)}, f32[4,8,128]{2,1,0:T(8,128)}, f32[8,128]{1,0:T(8,128)}) custom-call(f32[3,32,128]{2,1,0:T(8,128)} %bitcast.21, f32[3,32,128]{2,1,0:T(8,128)} %bitcast.22, s32[4,128]{1,0:T(4,128)} %bitcast.26), custom_call_target="tpu_custom_call" | custom-call | tf_op jit(solution)/shard_map/pack_kernel/pallas_call | solution.py:252
  2.1 6.4 %collective-permute-start = (f32[8,128]{1,0:T(8,128)}, f32[8,128]{1,0:T(8,128)S(1)}, u32[]{:S(2)}, u32[]{:S(2)}) collective-permute-start(f32[8,128]{1,0:T(8,128)} %get-tuple-element.14), channel_id=1, source_target_pairs={{0,7},{1,0},{2,1},{3,2},{4,3},{5,4},{6,5},{7,6},{8,15},{9,8},{10,9... | collective-permute-start | bytes 12296 | tf_op jit(solution)/shard_map/ppermute | solution.py:244
  8.5 0.8 %fusion = (f32[6,8,128]{2,1,0:T(8,128)S(1)}, f32[6,8,128]{2,1,0:T(8,128)S(1)}) fusion(f32[24,8,128]{2,1,0:T(8,128)} %get-tuple-element.13.v_ref), kind=kLoop, calls=%fused_computation.8 | loop fusion | bytes 98304 | tf_op jit(solution)/shard_map/slice | solution.py:255
  9.3 0.2 collective-permute-done.zr_ref
  9.5 2.7 %collective-permute-start.2 = (f32[7,8,128]{2,1,0:T(8,128)S(1)}, f32[7,8,128]{2,1,0:T(8,128)S(1)}, u32[]{:S(2)}, u32[]{:S(2)}) collective-permute-start(f32[7,8,128]{2,1,0:T(8,128)S(1)} %get-tuple-element.33), channel_id=1, source_target_pairs={{0,24},{8,0},{16,8},{24,16},{1,25},{9,1},{17,9},{25,17},{2,26},{10... | collective-permute-start | bytes 86024 | tf_op jit(solution)/shard_map/ppermute | solution.py:244
  12.2 0.0 collective-permute-start.1
  12.2 1.0 %collective-permute-done.2.yp_ref = f32[7,8,128]{2,1,0:T(8,128)S(1)} collective-permute-done((f32[7,8,128]{2,1,0:T(8,128)S(1)}, f32[7,8,128]{2,1,0:T(8,128)S(1)}, u32[]{:S(2)}, u32[]{:S(2)}) %collective-permute-start.2) | collective-permute-done | bytes 28704 | tf_op jit(solution)/shard_map/ppermute | solution.py:244
  13.2 2.9 %collective-permute-done.1.ym_ref = f32[7,8,128]{2,1,0:T(8,128)S(1)} collective-permute-done((f32[7,8,128]{2,1,0:T(8,128)S(1)}, f32[7,8,128]{2,1,0:T(8,128)S(1)}, u32[]{:S(2)}, u32[]{:S(2)}) %collective-permute-start.1) | collective-permute-done | bytes 28704 | tf_op jit(solution)/shard_map/ppermute | solution.py:244
  16.2 0.0 copy-done.4
  16.2 0.6 copy-done.5
  16.8 1.6 %widen_kernel.1.m_ref = f32[37,8,128]{2,1,0:T(8,128)} custom-call(f32[24,8,128]{2,1,0:T(8,128)} %get-tuple-element.13.v_ref, f32[8,128]{1,0:T(8,128)} %copy-done.8, f32[7,8,128]{2,1,0:T(8,128)} %copy-done.5, f32[7,8,128]{2,1,0:T(8,128)} %copy-done.4), custom_call_target="tpu_custom_call" | custom-call | tf_op jit(solution)/shard_map/widen_kernel/pallas_call | solution.py:256
  18.4 3.0 %collective-permute-start.4 = (f32[37,8,128]{2,1,0:T(8,128)}, f32[37,8,128]{2,1,0:T(8,128)S(1)}, u32[]{:S(2)}, u32[]{:S(2)}) collective-permute-start(f32[37,8,128]{2,1,0:T(8,128)} %widen_kernel.1.m_ref), channel_id=1, source_target_pairs={{0,224},{32,0},{64,32},{96,64},{128,96},{160,128},{192,160},{224,1... | collective-permute-start | bytes 454664 | tf_op jit(solution)/shard_map/ppermute | solution.py:244
  21.4 1.1 %collective-permute-start.3 = (f32[37,8,128]{2,1,0:T(8,128)}, f32[37,8,128]{2,1,0:T(8,128)S(1)}, u32[]{:S(2)}, u32[]{:S(2)}) collective-permute-start(f32[37,8,128]{2,1,0:T(8,128)} %widen_kernel.1.m_ref), channel_id=1, source_target_pairs={{0,32},{32,64},{64,96},{96,128},{128,160},{160,192},{192,224},{224... | collective-permute-start | bytes 454664 | tf_op jit(solution)/shard_map/ppermute | solution.py:244
  22.5 2.5 %convert.1.th_ref = f32[3584,128]{1,0:T(8,128)} convert(bf16[3584,128]{1,0:T(8,128)(2,1)} %bitcast.19) | non-fusion elementwise | flops 458752 | bytes 2752512 | tf_op jit(solution)/shard_map/convert_element_type | solution.py:251
  25.0 3.4 %own_column_kernel.1 = (f32[12,8,128]{2,1,0:T(8,128)}, f32[20,8,128]{2,1,0:T(8,128)}, f32[16,8,128]{2,1,0:T(8,128)}) custom-call(f32[37,8,128]{2,1,0:T(8,128)} %widen_kernel.1.m_ref, f32[4,8,128]{2,1,0:T(8,128)} %get-tuple-element.15.ownx_ref, f32[3584,128]{1,0:T(8,128)} %convert.1.th_ref), custom_call_target="tpu_custom_call" | custom-call | tf_op jit(solution)/shard_map/own_column_kernel/pallas_call | solution.py:260
  28.5 0.0 collective-permute-done.4.xp_ref
  28.5 0.0 collective-permute-done.3.xm_ref
  28.5 0.6 copy-done.1
  29.1 0.1 copy-done.2
  29.2 4.3 %side_columns_kernel.1 = (f32[12,8,128]{2,1,0:T(8,128)}, f32[20,8,128]{2,1,0:T(8,128)}, f32[20,8,128]{2,1,0:T(8,128)}, f32[256,128]{1,0:T(8,128)}) custom-call(f32[37,8,128]{2,1,0:T(8,128)} %widen_kernel.1.m_ref, f32[4,8,128]{2,1,0:T(8,128)} %get-tuple-element.15.ownx_ref, f32[3584,128]{1,0:T(8,128)} %convert.1.th_ref, f32[37,8,128]{2,1,0:T(8,128)} %copy-done.2, ...), custom_call_target="tpu_custom_call" | custom-call | tf_op jit(solution)/shard_map/side_columns_kernel/pallas_call | solution.py:266
  33.5 0.5 collective-permute-start.5
  34.0 0.0 collective-permute-start.6
  34.0 8.7 %all-to-all-start = ((f32[256,1,128]{2,1,0:T(1,128)}), f32[256,1,128]{2,1,0:T(1,128)S(1)}, u32[]{:S(2)}, u32[]{:S(2)}) async-start(f32[256,1,128]{2,1,0:T(1,128)} %bitcast.20), calls=%async_computation | async-start | bytes 262144 | tf_op jit(solution)/shard_map/all_to_all | solution.py:277
  42.7 0.0 collective-permute-done.5
  42.7 0.0 collective-permute-done.6
  42.8 0.0 copy-done.3
  42.8 2.7 %collective-permute-start.8 = (f32[4,8,128]{2,1,0:T(8,128)S(1)}, f32[4,8,128]{2,1,0:T(8,128)S(1)}, u32[]{:S(2)}, u32[]{:S(2)}) collective-permute-start(f32[4,8,128]{2,1,0:T(8,128)S(1)} %get-tuple-element.31), channel_id=1, source_target_pairs={{0,24},{8,0},{16,8},{24,16},{1,25},{9,1},{17,9},{25,17},{2,26},{10... | collective-permute-start | bytes 49160 | tf_op jit(solution)/shard_map/ppermute | solution.py:244
  45.5 0.6 slice_bitcast_fusion.2.sz_ref
  46.1 0.0 collective-permute-start.7
  46.1 0.3 collective-permute-done.8.yp_ref
  46.4 0.6 slice_bitcast_fusion.yp_ref
  47.0 3.2 %collective-permute-done.7.ym_ref = f32[4,8,128]{2,1,0:T(8,128)S(1)} collective-permute-done((f32[4,8,128]{2,1,0:T(8,128)S(1)}, f32[4,8,128]{2,1,0:T(8,128)S(1)}, u32[]{:S(2)}, u32[]{:S(2)}) %collective-permute-start.7) | collective-permute-done | bytes 16416 | tf_op jit(solution)/shard_map/ppermute | solution.py:244
  50.2 0.6 slice_bitcast_fusion.1.ym_ref
  50.8 1.4 %last_plane_kernel.1 = f32[8,128]{1,0:T(8,128)} custom-call(f32[8,128]{1,0:T(8,128)} %slice_bitcast_fusion.2.sz_ref, f32[8,128]{1,0:T(8,128)} %slice_bitcast_fusion.1.ym_ref, f32[8,128]{1,0:T(8,128)} %slice_bitcast_fusion.yp_ref), custom_call_target="tpu_custom_call" | custom-call | tf_op jit(solution)/shard_map/last_plane_kernel/pallas_call | solution.py:274
  52.2 1.5 %collective-permute-start.9 = (f32[8,128]{1,0:T(8,128)}, f32[8,128]{1,0:T(8,128)S(1)}, u32[]{:S(2)}, u32[]{:S(2)}) collective-permute-start(f32[8,128]{1,0:T(8,128)} %last_plane_kernel.1), channel_id=1, source_target_pairs={{0,1},{1,2},{2,3},{3,4},{4,5},{5,6},{6,7},{7,0},{8,9},{9,10},{10,1... | collective-permute-start | bytes 12296 | tf_op jit(solution)/shard_map/ppermute | solution.py:244
  53.6 4.1 %collective-permute-done.9.z_ref = f32[8,128]{1,0:T(8,128)S(1)} collective-permute-done((f32[8,128]{1,0:T(8,128)}, f32[8,128]{1,0:T(8,128)S(1)}, u32[]{:S(2)}, u32[]{:S(2)}) %collective-permute-start.9) | collective-permute-done | bytes 4128 | tf_op jit(solution)/shard_map/ppermute | solution.py:244
  57.7 0.0 copy-done
  57.7 0.0 copy-done.7
  57.7 0.6 copy-done.9
  58.3 1.6 %finish_kernel.1 = f32[3,32,128]{2,1,0:T(8,128)} custom-call(f32[12,8,128]{2,1,0:T(8,128)} %get-tuple-element.18.d_ref, f32[20,8,128]{2,1,0:T(8,128)} %copy-done, f32[4,8,128]{2,1,0:T(8,128)} %copy-done.7, f32[4,8,128]{2,1,0:T(8,128)} %copy-done.6, f32[8,128]{1,0:T(8,128)} %copy-done.9), custom_call_target="tpu_custom_call" | custom-call | tf_op jit(solution)/shard_map/finish_kernel/pallas_call | solution.py:276
  59.9 0.0 all-to-all-done
  59.9 0.3 reduce_sum.9
  60.2 0.7 slice.78
  60.8 0.1 slice_multiply_fusion
  60.9 0.1 fusion.3
  61.0 0.7 %fusion.2 = (f32[1]{0:T(128)}, f32[1]{0:T(128)}, f32[1]{0:T(128)}, f32[1]{0:T(128)}, f32[1]{0:T(128)}) fusion(f32[6]{0:T(128)S(1)} %get-tuple-element.38, f32[6]{0:T(128)S(1)} %get-tuple-element.39), kind=kLoop, calls=%fused_computation.10 | loop fusion | bytes 40 | tf_op jit(solution)/shard_map/slice | solution.py:286
  61.6 1.4 %stack.4 = f32[9]{0:T(128)S(1)} concatenate(f32[3]{0:T(128)S(1)} %bitcast.24, f32[1]{0:T(128)} %get-tuple-element.44, f32[2]{0:T(128)S(1)} %get-tuple-element.41, f32[1]{0:T(128)} %get-tuple-element.45, f32[2]{0:T(128)S(1)} %get-tuple-element.40), dimensions={0} | concatenate | bytes 72 | tf_op jit(solution)/shard_map/stack | solution.py:285
  63.1 0.7 reshape.39
  (15 shorter events, 0.0 us)
Async XLA Ops:
  2.1 7.4 %collective-permute-start = (f32[8,128]{1,0:T(8,128)}, f32[8,128]{1,0:T(8,128)S(1)}, u32[]{:S(2)}, u32[]{:S(2)}) collective-permute-start(f32[8,128]{1,0:T(8,128)} %get-tuple-element.14), channel_id=1, source_target_pairs={{0,7},{1,0},{2,1},{3,2},{4,3},{5,4},{6,5},{7,6},{8,15},{9,8},{10,9... | collective-permute-start | bytes 12296 | tf_op jit(solution)/shard_map/ppermute | solution.py:244
  9.5 6.7 %copy-start.8 = (f32[8,128]{1,0:T(8,128)}, f32[8,128]{1,0:T(8,128)S(1)}, u32[]{:S(2)}) copy-start(f32[8,128]{1,0:T(8,128)S(1)} %collective-permute-done.zr_ref) | copy-start | bytes 12292
  9.5 3.7 %collective-permute-start.2 = (f32[7,8,128]{2,1,0:T(8,128)S(1)}, f32[7,8,128]{2,1,0:T(8,128)S(1)}, u32[]{:S(2)}, u32[]{:S(2)}) collective-permute-start(f32[7,8,128]{2,1,0:T(8,128)S(1)} %get-tuple-element.33), channel_id=1, source_target_pairs={{0,24},{8,0},{16,8},{24,16},{1,25},{9,1},{17,9},{25,17},{2,26},{10... | collective-permute-start | bytes 86024 | tf_op jit(solution)/shard_map/ppermute | solution.py:244
  12.2 3.9 %collective-permute-start.1 = (f32[7,8,128]{2,1,0:T(8,128)S(1)}, f32[7,8,128]{2,1,0:T(8,128)S(1)}, u32[]{:S(2)}, u32[]{:S(2)}) collective-permute-start(f32[7,8,128]{2,1,0:T(8,128)S(1)} %get-tuple-element.34), channel_id=1, source_target_pairs={{0,8},{8,16},{16,24},{24,0},{1,9},{9,17},{17,25},{25,1},{2,10},{10... | collective-permute-start | bytes 86024 | tf_op jit(solution)/shard_map/ppermute | solution.py:244
  13.2 3.0 %copy-start.4 = (f32[7,8,128]{2,1,0:T(8,128)}, f32[7,8,128]{2,1,0:T(8,128)S(1)}, u32[]{:S(2)}) copy-start(f32[7,8,128]{2,1,0:T(8,128)S(1)} %collective-permute-done.2.yp_ref) | copy-start | bytes 86020
  16.2 0.6 copy-start.5
  18.4 10.0 %collective-permute-start.4 = (f32[37,8,128]{2,1,0:T(8,128)}, f32[37,8,128]{2,1,0:T(8,128)S(1)}, u32[]{:S(2)}, u32[]{:S(2)}) collective-permute-start(f32[37,8,128]{2,1,0:T(8,128)} %widen_kernel.1.m_ref), channel_id=1, source_target_pairs={{0,224},{32,0},{64,32},{96,64},{128,96},{160,128},{192,160},{224,1... | collective-permute-start | bytes 454664 | tf_op jit(solution)/shard_map/ppermute | solution.py:244
  21.4 7.1 %collective-permute-start.3 = (f32[37,8,128]{2,1,0:T(8,128)}, f32[37,8,128]{2,1,0:T(8,128)S(1)}, u32[]{:S(2)}, u32[]{:S(2)}) collective-permute-start(f32[37,8,128]{2,1,0:T(8,128)} %widen_kernel.1.m_ref), channel_id=1, source_target_pairs={{0,32},{32,64},{64,96},{96,128},{128,160},{160,192},{192,224},{224... | collective-permute-start | bytes 454664 | tf_op jit(solution)/shard_map/ppermute | solution.py:244
  28.5 14.3 %copy-start.3 = (f32[20,8,128]{2,1,0:T(8,128)S(1)}, f32[20,8,128]{2,1,0:T(8,128)}, u32[]{:S(2)}) copy-start(f32[20,8,128]{2,1,0:T(8,128)} %get-tuple-element.19) | copy-start | bytes 245764
  28.5 0.6 copy-start.1
  28.5 0.7 %copy-start.2 = (f32[37,8,128]{2,1,0:T(8,128)}, f32[37,8,128]{2,1,0:T(8,128)S(1)}, u32[]{:S(2)}) copy-start(f32[37,8,128]{2,1,0:T(8,128)S(1)} %collective-permute-done.3.xm_ref) | copy-start | bytes 454660
  33.5 9.2 %collective-permute-start.5 = (f32[20,8,128]{2,1,0:T(8,128)}, f32[20,8,128]{2,1,0:T(8,128)S(1)}, u32[]{:S(2)}, u32[]{:S(2)}) collective-permute-start(f32[20,8,128]{2,1,0:T(8,128)} %get-tuple-element.20), channel_id=1, source_target_pairs={{0,32},{32,64},{64,96},{96,128},{128,160},{160,192},{192,224},{224... | collective-permute-start | bytes 245768 | tf_op jit(solution)/shard_map/ppermute | solution.py:244
  34.0 8.7 %collective-permute-start.6 = (f32[20,8,128]{2,1,0:T(8,128)}, f32[20,8,128]{2,1,0:T(8,128)S(1)}, u32[]{:S(2)}, u32[]{:S(2)}) collective-permute-start(f32[20,8,128]{2,1,0:T(8,128)} %get-tuple-element.21), channel_id=1, source_target_pairs={{0,224},{32,0},{64,32},{96,64},{128,96},{160,128},{192,160},{224,1... | collective-permute-start | bytes 245768 | tf_op jit(solution)/shard_map/ppermute | solution.py:244
  34.0 25.9 %all-to-all-start = ((f32[256,1,128]{2,1,0:T(1,128)}), f32[256,1,128]{2,1,0:T(1,128)S(1)}, u32[]{:S(2)}, u32[]{:S(2)}) async-start(f32[256,1,128]{2,1,0:T(1,128)} %bitcast.20), calls=%async_computation | async-start | bytes 262144 | tf_op jit(solution)/shard_map/all_to_all | solution.py:277
  42.8 14.9 %copy-start = (f32[20,8,128]{2,1,0:T(8,128)}, f32[20,8,128]{2,1,0:T(8,128)S(1)}, u32[]{:S(2)}) copy-start(f32[20,8,128]{2,1,0:T(8,128)S(1)} %add_add_fusion.s_ref) | copy-start | bytes 245764
  42.8 3.6 %collective-permute-start.8 = (f32[4,8,128]{2,1,0:T(8,128)S(1)}, f32[4,8,128]{2,1,0:T(8,128)S(1)}, u32[]{:S(2)}, u32[]{:S(2)}) collective-permute-start(f32[4,8,128]{2,1,0:T(8,128)S(1)} %get-tuple-element.31), channel_id=1, source_target_pairs={{0,24},{8,0},{16,8},{24,16},{1,25},{9,1},{17,9},{25,17},{2,26},{10... | collective-permute-start | bytes 49160 | tf_op jit(solution)/shard_map/ppermute | solution.py:244
  46.1 4.1 %collective-permute-start.7 = (f32[4,8,128]{2,1,0:T(8,128)S(1)}, f32[4,8,128]{2,1,0:T(8,128)S(1)}, u32[]{:S(2)}, u32[]{:S(2)}) collective-permute-start(f32[4,8,128]{2,1,0:T(8,128)S(1)} %get-tuple-element.32), channel_id=1, source_target_pairs={{0,8},{8,16},{16,24},{24,0},{1,9},{9,17},{17,25},{25,1},{2,10},{10... | collective-permute-start | bytes 49160 | tf_op jit(solution)/shard_map/ppermute | solution.py:244
  46.4 11.3 %copy-start.6 = (f32[4,8,128]{2,1,0:T(8,128)}, f32[4,8,128]{2,1,0:T(8,128)S(1)}, u32[]{:S(2)}) copy-start(f32[4,8,128]{2,1,0:T(8,128)S(1)} %collective-permute-done.8.yp_ref) | copy-start | bytes 49156
  50.2 7.5 %copy-start.7 = (f32[4,8,128]{2,1,0:T(8,128)}, f32[4,8,128]{2,1,0:T(8,128)S(1)}, u32[]{:S(2)}) copy-start(f32[4,8,128]{2,1,0:T(8,128)S(1)} %collective-permute-done.7.ym_ref) | copy-start | bytes 49156
  52.2 5.5 %collective-permute-start.9 = (f32[8,128]{1,0:T(8,128)}, f32[8,128]{1,0:T(8,128)S(1)}, u32[]{:S(2)}, u32[]{:S(2)}) collective-permute-start(f32[8,128]{1,0:T(8,128)} %last_plane_kernel.1), channel_id=1, source_target_pairs={{0,1},{1,2},{2,3},{3,4},{4,5},{5,6},{6,7},{7,0},{8,9},{9,10},{10,1... | collective-permute-start | bytes 12296 | tf_op jit(solution)/shard_map/ppermute | solution.py:244
  57.7 0.6 copy-start.9
where the time goes:
time: 68.8 us; the launch traced here: 67.5 us
  starting transfers between devices  26.6 us (39%)
  Pallas kernels  13.8 us (20%)
  waiting for transfers between devices  11.7 us (17%)
  local copies, waits for them, and re-layouts  7.96 us (12%)
  between operations  4.48 us (7%)
  other arithmetic  2.93 us (4%)
    ppermute x10, starting transfers between devices, shifted(): lax.ppermute(shard, axis, [(i, (i + by) % count) for i in range(count)])  17.9 us
    ppermute x10, waiting for transfers between devices, shifted(): lax.ppermute(shard, axis, [(i, (i + by) % count) for i in range(count)])  11.7 us
    all_to_all x1, starting transfers between devices, per_device(): tallies = lax.all_to_all(tally, AXES, 0, 0, tiled=True)  8.71 us
    pallas_call x1, Pallas kernels, per_device(): call(side_columns_kernel, (f32(12, *tile), f32(20, *tile), f32(20, *tile)...  4.32 us
    pallas_call x1, Pallas kernels, per_device(): call(own_column_kernel, (f32(12, *tile), f32(20, *tile), f32(16, *tile)),...  3.43 us
    convert_element_type x1, other arithmetic, per_device(): theta = noise.reshape(14 * SLOTS * SLOTS * ROWS, LANES).astype(jnp.float32)  2.55 us
    unnamed x20, local copies, waits for them, and re-layouts  1.89 us
    squeeze x3, local copies, waits for them, and re-layouts, per_device(): home = call(last_plane_kernel, f32(*tile))(s[0], back_ym[3], back_yp[0])  1.8 us
  transfers between devices with their start and end apart: 11, of which 6 were waited for; matrix products, arithmetic and copies ran while one was open for 8% of the time, Pallas kernels for 9%

commit v1 on v0

--- a/solution.py
+++ b/solution.py
@@ -1,3 +1,5 @@
+import functools
+
 import jax
 import jax.numpy as jnp
 from jax import lax
@@ -61,6 +63,15 @@
             at = (y + 1) * 6 + c
             z = jnp.where(lane == at, pltpu.roll(val, at, 1), z)
     z_ref[...] = z
+
+
+def convert_kernel(noise_ref, th_ref, ready_ref):
+    ready_ref[...] = jnp.zeros_like(ready_ref)
+
+    @pl.loop(0, th_ref.shape[0] // 256)
+    def _(i):
+        at = pl.ds(pl.multiple_of(i * 256, 256), 256)
+        th_ref[at, :] = noise_ref[at, :].astype(jnp.float32)
 
 
 def widen_kernel(v_ref, zr_ref, ym_ref, yp_ref, m_ref):
@@ -198,18 +209,24 @@
 
     settle(rlm_ref, rum_ref, rm_ref)
     settle(rlp_ref, rup_ref, rp_ref)
+    acc = [acc_ref[i] for i in range(13)]
+    sums = [NOISE_SCALE * acc[i] + acc[6 + i] * (1.0 / (DRAG * DRAG)) for i in range(6)]
+    lines = [sums[PRODUCTS.index((min(a, b), max(a, b)))] for a in range(3) for b in range(3)]
+    lines += [(acc[6] + acc[9] + acc[11]) * (1.0 / (DRAG * DRAG)), acc[12]]
     lane = lax.broadcasted_iota(jnp.int32, (16, LANES), 1)
     line = lax.broadcasted_iota(jnp.int32, (16, LANES), 0)
-    sums = jnp.sum(jnp.sum(acc_ref[...], axis=1), axis=1, keepdims=True)
-    tally = jnp.sum(jnp.where(lane == line, sums, 0.0), axis=0, keepdims=True)
+    lines = [jnp.sum(x, axis=0, keepdims=True) for x in lines]
+    held = jnp.concatenate(lines + [jnp.zeros((16 - len(lines), LANES), jnp.float32)], axis=0)
+    held = jnp.where(lane == line, jnp.sum(held, axis=1, keepdims=True), 0.0)
+    tally = jnp.sum(held, axis=0, keepdims=True)
     tally_ref[...] = jnp.broadcast_to(tally, tally_ref.shape)
 
 
-def last_plane_kernel(sz_ref, ym_ref, yp_ref, z_ref):
-    lane = lane_iota()
-    z = sz_ref[...]
-    z = z + jnp.where((lane >= 3) & (lane < 6), pltpu.roll(ym_ref[...], LANES - 12, 1), 0.0)
-    z = z + jnp.where((lane >= 12) & (lane < 15), pltpu.roll(yp_ref[...], 12, 1), 0.0)
+def last_plane_kernel(s_ref, ym_ref, yp_ref, z_ref):
+    lane = lane_iota()
+    z = s_ref[0]
+    z = z + jnp.where((lane >= 3) & (lane < 6), pltpu.roll(ym_ref[3], LANES - 12, 1), 0.0)
+    z = z + jnp.where((lane >= 12) & (lane < 15), pltpu.roll(yp_ref[0], 12, 1), 0.0)
     z_ref[...] = z
 
 
@@ -227,16 +244,41 @@
             f_ref[a, pl.ds(y, SLOTS, stride=ROWS), :] = NOISE_SCALE * (d_ref[y * 3 + a] - back)
 
 
+def report_kernel(cells, tallies_ref, stress_ref, level_ref):
+    total = jnp.broadcast_to(jnp.sum(tallies_ref[...], axis=0, keepdims=True), (SLOTS, LANES))
+    slot = slot_iota()
+    stress = jnp.where(slot == 1, pltpu.roll(total, LANES - 3, 1), total)
+    stress = jnp.where(slot == 2, pltpu.roll(total, LANES - 6, 1), stress) * (1.0 / cells)
+    stress_ref[...] = stress[0:3, 0:3]
+    level = pltpu.roll(total, LANES - 9, 1) / (3.0 * pltpu.roll(total, LANES - 10, 1) - 3.0)
+    level_ref[...] = level[0:1, 0:1]
+
+
 def f32(*shape):
-    return jax.ShapeDtypeStruct(shape, jnp.float32)
+    return pltpu.VMEM(shape, jnp.float32)
 
 
 def vmem(*shape):
     return pltpu.VMEM(shape, jnp.float32)
 
 
-def call(kernel, out_shape, scratch=()):
-    return pl.pallas_call(kernel, out_shape=out_shape, scratch_shapes=list(scratch), name=kernel.__name__)
+def call(kernel, out_shape, scratch=(), hold=True):
+    space = pl.BlockSpec(memory_space=pltpu.VMEM)
+
+    def run(*args):
+        if hold:
+            args = [pltpu.with_memory_space_constraint(a, pltpu.VMEM) for a in args]
+        return pl.pallas_call(
+            kernel,
+            out_shape=out_shape,
+            in_specs=[space for _ in args],
+            out_specs=jax.tree.map(lambda _: space, out_shape),
+            scratch_shapes=list(scratch),
+            compiler_params=pltpu.CompilerParams(vmem_limit_bytes=16 << 20),
+            name=getattr(kernel, "func", kernel).__name__,
+        )(*args)
+
+    return run
 
 
 def shifted(shard, axis, by):
@@ -248,15 +290,17 @@
     off = offset.reshape(3, SLOTS * ROWS, LANES)
     vel = velocity.reshape(3, SLOTS * ROWS, LANES)
     occ = occupancy.reshape(ROWS, LANES)
-    theta = noise.reshape(14 * SLOTS * SLOTS * ROWS, LANES).astype(jnp.float32)
-    v, ownx, z = call(pack_kernel, (f32(24, SLOTS, LANES), f32(ROWS, SLOTS, LANES), f32(SLOTS, LANES)))(off, vel, occ)
-    zr = shifted(z, "gz", -1)
+    tile = (SLOTS, LANES)
+    lines = 14 * SLOTS * SLOTS * ROWS
+    theta, ready = call(convert_kernel, (f32(lines, LANES), f32(*tile)), hold=False)(noise.reshape(lines, LANES))
+    v, ownx, z = call(pack_kernel, (f32(24, *tile), f32(ROWS, *tile), f32(*tile)), hold=False)(off, vel, occ)
+    zr, ready = lax.optimization_barrier((shifted(z, "gz", -1), ready))
+    zr = zr + ready
     from_ym = shifted(jnp.concatenate([v[18:24], zr[None]]), "gy", 1)
     from_yp = shifted(jnp.concatenate([v[0:6], zr[None]]), "gy", -1)
-    m = call(widen_kernel, f32(37, SLOTS, LANES))(v, zr, from_ym, from_yp)
+    m = call(widen_kernel, f32(37, *tile))(v, zr, from_ym, from_yp)
     from_xm = shifted(m, "gx", 1)
     from_xp = shifted(m, "gx", -1)
-    tile = (SLOTS, LANES)
     d0, r0, acc0 = call(
         own_column_kernel,
         (f32(12, *tile), f32(20, *tile), f32(16, *tile)),
@@ -271,20 +315,16 @@
     s = r0 + shifted(rp, "gx", 1) + shifted(rm, "gx", -1)
     back_ym = shifted(s[16:20], "gy", 1)
     back_yp = shifted(s[0:4], "gy", -1)
-    home = call(last_plane_kernel, f32(*tile))(s[0], back_ym[3], back_yp[0])
+    home = call(last_plane_kernel, f32(*tile))(s, back_ym, back_yp)
     arrived = shifted(home, "gz", 1)
-    force = call(finish_kernel, f32(3, SLOTS * ROWS, LANES))(d, s, back_ym, back_yp, arrived)
+    force_shape = jax.ShapeDtypeStruct((3, SLOTS * ROWS, LANES), jnp.float32)
+    force = call(finish_kernel, force_shape)(d, s, back_ym, back_yp, arrived)
     tallies = lax.all_to_all(tally, AXES, 0, 0, tiled=True)
-    total = jnp.sum(tallies, axis=0)
-    virial = NOISE_SCALE * total[0:6]
-    kinetic = total[6:12] / (DRAG * DRAG)
-    count = total[12]
-    cells = ROWS * LANES * devices
-    stress = (kinetic + virial) / cells
-    order = [PRODUCTS.index((min(a, b), max(a, b))) for a in range(3) for b in range(3)]
-    stress_matrix = jnp.stack([stress[i] for i in order]).reshape(3, 3)
-    thermal_level = jnp.reshape((kinetic[0] + kinetic[3] + kinetic[5]) / (3.0 * count - 3.0), (1,))
-    return force.reshape(offset.shape), stress_matrix, thermal_level
+    stress, level = call(
+        functools.partial(report_kernel, float(ROWS * LANES * devices)),
+        (jax.ShapeDtypeStruct((3, 3), jnp.float32), jax.ShapeDtypeStruct((1, 1), jnp.float32)),
+    )(tallies)
+    return force.reshape(offset.shape), stress, level.reshape(1)
 
 
 def solution(mesh):

time: 68.8 us -> 51.9 us (0.75)
  Pallas kernels: 13.8 us -> 5.57 us
  local copies, waits for them, and re-layouts: 7.96 us -> 3.46 us
  between operations: 4.48 us -> 0.74 us
  other arithmetic: 2.93 us -> 0.03 us
  waiting for transfers between devices: 11.7 us -> 13.9 us
  starting transfers between devices: 26.6 us -> 27.4 us
    pallas_call x6 -> x8, Pallas kernels: 13.8 us -> 5.57 us  [run(): pl.pallas_call(kernel, out_shape=out_shape, in_specs=[space for _ in args...]
    convert_element_type x1 -> x0, other arithmetic: 2.55 us -> none  [per_device(): theta = noise.reshape(14 * SLOTS * SLOTS * ROWS, LANES).astype(jnp.float32)]
    ppermute x10, waiting for transfers between devices: 11.7 us -> 13.9 us  [shifted(): lax.ppermute(shard, axis, [(i, (i + by) % count) for i in range(count)])]
    squeeze x3 -> x0, local copies, waits for them, and re-layouts: 1.8 us -> none  [per_device(): home = call(last_plane_kernel, f32(*tile))(s[0], back_ym[3], back_yp[0])]
    ppermute x10, starting transfers between devices: 17.9 us -> 19.4 us  [shifted(): lax.ppermute(shard, axis, [(i, (i + by) % count) for i in range(count)])]
    unnamed x20 -> x8, local copies, waits for them, and re-layouts: 1.89 us -> 3.45 us
    slice x3 -> x0, local copies, waits for them, and re-layouts: 1.42 us -> none  [the longest x1 0.68 us: per_device(): kinetic[5]]
    another operation x1 -> x0, local copies, waits for them, and re-layouts: 1.42 us -> none  [per_device(): stress_matrix = jnp.stack([stress[i] for i in order]).reshape(3, 3)]
  transfers between devices with their start and end apart: 11 -> 11, of which waited for: 6 -> 6; matrix products, arithmetic and copies ran while one was open for 8% -> 0% of each run, Pallas kernels for 9% -> 4%
where the time goes in v1:
time: 51.9 us; the launch traced here: 51.1 us
  starting transfers between devices  27.4 us (53%)
  waiting for transfers between devices  13.9 us (27%)
  Pallas kernels  5.57 us (11%)
  local copies, waits for them, and re-layouts  3.46 us (7%)
  between operations  0.74 us (1%)
    ppermute x10, starting transfers between devices, shifted(): lax.ppermute(shard, axis, [(i, (i + by) % count) for i in range(count)])  19.4 us
    ppermute x10, waiting for transfers between devices, shifted(): lax.ppermute(shard, axis, [(i, (i + by) % count) for i in range(count)])  13.9 us
    all_to_all x1, starting transfers between devices, per_device(): tallies = lax.all_to_all(tally, AXES, 0, 0, tiled=True)  7.97 us
    pallas_call x8, Pallas kernels, run(): pl.pallas_call(kernel, out_shape=out_shape, in_specs=[space for _ in args...  5.57 us
    unnamed x8, local copies, waits for them, and re-layouts  3.45 us
  transfers between devices with their start and end apart: 11, of which 6 were waited for; matrix products, arithmetic and copies ran while one was open for 0% of the time, Pallas kernels for 4%

profile of v1, /device:TPU:1, one launch (start us, length us, event | category | flops | bytes accessed | tf_op | source)
XLA Modules:
  0.0 51.1 jit_solution(3375206289259320690)
XLA Ops:
  0.6 0.0 copy-start.1
  0.6 0.8 %copy-done.1 = f32[3,8,1,4,128]{4,3,2,1,0:T(4,128)S(1)} copy-done((f32[3,8,1,4,128]{4,3,2,1,0:T(4,128)S(1)}, f32[3,8,1,4,128]{4,3,2,1,0:T(4,128)}, u32[]{:S(2)}) %copy-start.1) | copy-done | bytes 49176
  1.4 0.0 copy-start.2
  1.4 0.8 %copy-done.2 = f32[3,8,1,4,128]{4,3,2,1,0:T(4,128)S(1)} copy-done((f32[3,8,1,4,128]{4,3,2,1,0:T(4,128)S(1)}, f32[3,8,1,4,128]{4,3,2,1,0:T(4,128)}, u32[]{:S(2)}) %copy-start.2) | copy-done | bytes 49176
  2.2 0.0 copy-start.3
  2.2 0.7 %copy-done.3 = s32[1,4,128]{2,1,0:T(4,128)S(1)} copy-done((s32[1,4,128]{2,1,0:T(4,128)S(1)}, s32[1,4,128]{2,1,0:T(4,128)}, u32[]{:S(2)}) %copy-start.3) | copy-done | bytes 2072
  2.9 0.1 pack_kernel.1
  3.0 6.5 %collective-permute-start = (f32[8,128]{1,0:T(8,128)S(1)}, f32[8,128]{1,0:T(8,128)S(1)}, u32[]{:S(2)}, u32[]{:S(2)}) collective-permute-start(f32[8,128]{1,0:T(8,128)S(1)} %get-tuple-element.20), channel_id=1, source_target_pairs={{0,7},{1,0},{2,1},{3,2},{4,3},{5,4},{6,5},{7,6},{8,15},{9,8},{10,9... | collective-permute-start | bytes 12296 | tf_op jit(solution)/shard_map/ppermute | solution.py:286
  9.5 0.0 copy-start
  9.5 1.2 %copy-done = bf16[14,8,8,1,4,128]{5,4,3,2,1,0:T(4,128)(2,1)S(1)} copy-done((bf16[14,8,8,1,4,128]{5,4,3,2,1,0:T(4,128)(2,1)S(1)}, bf16[14,8,8,1,4,128]{5,4,3,2,1,0:T(4,128)(2,1)}, u32[]{:S(2)}) %copy-start) | copy-done | bytes 917528
  10.7 0.2 convert_kernel.1
  10.8 0.0 collective-permute-done
  10.9 2.8 %collective-permute-start.2 = (f32[7,8,128]{2,1,0:T(8,128)S(1)}, f32[7,8,128]{2,1,0:T(8,128)S(1)}, u32[]{:S(2)}, u32[]{:S(2)}) collective-permute-start(f32[7,8,128]{2,1,0:T(8,128)S(1)} %get-tuple-element.45), channel_id=1, source_target_pairs={{0,24},{8,0},{16,8},{24,16},{1,25},{9,1},{17,9},{25,17},{2,26},{10... | collective-permute-start | bytes 86024 | tf_op jit(solution)/shard_map/ppermute | solution.py:286
  13.7 0.0 collective-permute-start.1
  13.7 1.0 %collective-permute-done.2.yp_ref = f32[7,8,128]{2,1,0:T(8,128)S(1)} collective-permute-done((f32[7,8,128]{2,1,0:T(8,128)S(1)}, f32[7,8,128]{2,1,0:T(8,128)S(1)}, u32[]{:S(2)}, u32[]{:S(2)}) %collective-permute-start.2) | collective-permute-done | bytes 28704 | tf_op jit(solution)/shard_map/ppermute | solution.py:286
  14.7 2.9 %collective-permute-done.1.ym_ref = f32[7,8,128]{2,1,0:T(8,128)S(1)} collective-permute-done((f32[7,8,128]{2,1,0:T(8,128)S(1)}, f32[7,8,128]{2,1,0:T(8,128)S(1)}, u32[]{:S(2)}, u32[]{:S(2)}) %collective-permute-start.1) | collective-permute-done | bytes 28704 | tf_op jit(solution)/shard_map/ppermute | solution.py:286
  17.6 0.1 widen_kernel.1.m_ref
  17.7 2.4 %collective-permute-start.4 = (f32[37,8,128]{2,1,0:T(8,128)S(1)}, f32[37,8,128]{2,1,0:T(8,128)S(1)}, u32[]{:S(2)}, u32[]{:S(2)}) collective-permute-start(f32[37,8,128]{2,1,0:T(8,128)S(1)} %widen_kernel.1.m_ref), channel_id=1, source_target_pairs={{0,224},{32,0},{64,32},{96,64},{128,96},{160,128},{192,160},{224,1... | collective-permute-start | bytes 454664 | tf_op jit(solution)/shard_map/ppermute | solution.py:286
  20.1 1.1 %collective-permute-start.3 = (f32[37,8,128]{2,1,0:T(8,128)S(1)}, f32[37,8,128]{2,1,0:T(8,128)S(1)}, u32[]{:S(2)}, u32[]{:S(2)}) collective-permute-start(f32[37,8,128]{2,1,0:T(8,128)S(1)} %widen_kernel.1.m_ref), channel_id=1, source_target_pairs={{0,32},{32,64},{64,96},{96,128},{128,160},{160,192},{192,224},{224... | collective-permute-start | bytes 454664 | tf_op jit(solution)/shard_map/ppermute | solution.py:286
  21.2 1.2 %own_column_kernel.1 = (f32[12,8,128]{2,1,0:T(8,128)S(1)}, f32[20,8,128]{2,1,0:T(8,128)S(1)}, f32[16,8,128]{2,1,0:T(8,128)S(1)}) custom-call(f32[37,8,128]{2,1,0:T(8,128)S(1)} %widen_kernel.1.m_ref, f32[4,8,128]{2,1,0:T(8,128)S(1)} %get-tuple-element.24.ownx_ref, f32[3584,128]{1,0:T(8,128)S(1)} %get-tuple-element.25.th_ref), custom_call_target="tpu_custom_call" | custom-call | tf_op jit(solution)/shard_map/own_column_kernel/pallas_call | solution.py:271
  22.4 1.7 %collective-permute-done.4.xp_ref = f32[37,8,128]{2,1,0:T(8,128)S(1)} collective-permute-done((f32[37,8,128]{2,1,0:T(8,128)S(1)}, f32[37,8,128]{2,1,0:T(8,128)S(1)}, u32[]{:S(2)}, u32[]{:S(2)}) %collective-permute-start.4) | collective-permute-done | bytes 151584 | tf_op jit(solution)/shard_map/ppermute | solution.py:286
  24.1 0.0 collective-permute-done.3.xm_ref
  24.1 2.6 %side_columns_kernel.1 = (f32[12,8,128]{2,1,0:T(8,128)S(1)}, f32[20,8,128]{2,1,0:T(8,128)S(1)}, f32[20,8,128]{2,1,0:T(8,128)S(1)}, f32[256,128]{1,0:T(8,128)}) custom-call(f32[37,8,128]{2,1,0:T(8,128)S(1)} %widen_kernel.1.m_ref, f32[4,8,128]{2,1,0:T(8,128)S(1)} %get-tuple-element.24.ownx_ref, f32[3584,128]{1,0:T(8,128)S(1)} %get-tuple-element.25.th_ref, ...), custom_call_target="tpu_custom_call" | custom-call | tf_op jit(solution)/shard_map/side_columns_kernel/pallas_call | solution.py:271
  26.6 1.7 %collective-permute-start.5 = (f32[20,8,128]{2,1,0:T(8,128)S(1)}, f32[20,8,128]{2,1,0:T(8,128)S(1)}, u32[]{:S(2)}, u32[]{:S(2)}) collective-permute-start(f32[20,8,128]{2,1,0:T(8,128)S(1)} %get-tuple-element.30), channel_id=1, source_target_pairs={{0,32},{32,64},{64,96},{96,128},{128,160},{160,192},{192,224},{224... | collective-permute-start | bytes 245768 | tf_op jit(solution)/shard_map/ppermute | solution.py:286
  28.4 0.6 %collective-permute-start.6 = (f32[20,8,128]{2,1,0:T(8,128)S(1)}, f32[20,8,128]{2,1,0:T(8,128)S(1)}, u32[]{:S(2)}, u32[]{:S(2)}) collective-permute-start(f32[20,8,128]{2,1,0:T(8,128)S(1)} %get-tuple-element.31), channel_id=1, source_target_pairs={{0,224},{32,0},{64,32},{96,64},{128,96},{160,128},{192,160},{224,1... | collective-permute-start | bytes 245768 | tf_op jit(solution)/shard_map/ppermute | solution.py:286
  29.0 8.0 %all-to-all-start = ((f32[256,1,128]{2,1,0:T(1,128)}), f32[256,1,128]{2,1,0:T(1,128)S(1)}, u32[]{:S(2)}, u32[]{:S(2)}) async-start(f32[256,1,128]{2,1,0:T(1,128)} %bitcast.8), calls=%async_computation | async-start | bytes 262144 | tf_op jit(solution)/shard_map/all_to_all | solution.py:322
  37.0 0.0 collective-permute-done.5
  37.0 0.0 collective-permute-done.6
  37.0 2.8 %collective-permute-start.8 = (f32[4,8,128]{2,1,0:T(8,128)S(1)}, f32[4,8,128]{2,1,0:T(8,128)S(1)}, u32[]{:S(2)}, u32[]{:S(2)}) collective-permute-start(f32[4,8,128]{2,1,0:T(8,128)S(1)} %get-tuple-element.43), channel_id=1, source_target_pairs={{0,24},{8,0},{16,8},{24,16},{1,25},{9,1},{17,9},{25,17},{2,26},{10... | collective-permute-start | bytes 49160 | tf_op jit(solution)/shard_map/ppermute | solution.py:286
  39.9 0.0 collective-permute-start.7
  39.9 0.9 %collective-permute-done.8.yp_ref = f32[4,8,128]{2,1,0:T(8,128)S(1)} collective-permute-done((f32[4,8,128]{2,1,0:T(8,128)S(1)}, f32[4,8,128]{2,1,0:T(8,128)S(1)}, u32[]{:S(2)}, u32[]{:S(2)}) %collective-permute-start.8) | collective-permute-done | bytes 16416 | tf_op jit(solution)/shard_map/ppermute | solution.py:286
  40.7 3.2 %collective-permute-done.7.ym_ref = f32[4,8,128]{2,1,0:T(8,128)S(1)} collective-permute-done((f32[4,8,128]{2,1,0:T(8,128)S(1)}, f32[4,8,128]{2,1,0:T(8,128)S(1)}, u32[]{:S(2)}, u32[]{:S(2)}) %collective-permute-start.7) | collective-permute-done | bytes 16416 | tf_op jit(solution)/shard_map/ppermute | solution.py:286
  44.0 0.1 last_plane_kernel.1
  44.0 1.5 %collective-permute-start.9 = (f32[8,128]{1,0:T(8,128)S(1)}, f32[8,128]{1,0:T(8,128)S(1)}, u32[]{:S(2)}, u32[]{:S(2)}) collective-permute-start(f32[8,128]{1,0:T(8,128)S(1)} %last_plane_kernel.1), channel_id=1, source_target_pairs={{0,1},{1,2},{2,3},{3,4},{4,5},{5,6},{6,7},{7,0},{8,9},{9,10},{10,1... | collective-permute-start | bytes 12296 | tf_op jit(solution)/shard_map/ppermute | solution.py:286
  45.5 4.2 %collective-permute-done.9.z_ref = f32[8,128]{1,0:T(8,128)S(1)} collective-permute-done((f32[8,128]{1,0:T(8,128)S(1)}, f32[8,128]{1,0:T(8,128)S(1)}, u32[]{:S(2)}, u32[]{:S(2)}) %collective-permute-start.9) | collective-permute-done | bytes 4128 | tf_op jit(solution)/shard_map/ppermute | solution.py:286
  49.7 0.7 %finish_kernel.1 = f32[3,32,128]{2,1,0:T(8,128)} custom-call(f32[12,8,128]{2,1,0:T(8,128)S(1)} %get-tuple-element.28.d_ref, f32[20,8,128]{2,1,0:T(8,128)S(1)} %add_add_fusion.s_ref, f32[4,8,128]{2,1,0:T(8,128)S(1)} %collective-permute-done.7.ym_ref, f32[4,8,128]{2,1,0:T(8,128)S(1)} %collective-permute-done.8.yp_ref, f32[8,128]{1,0:T(8,128)S(1)} %collective-permute-done.9.z_ref), custom_call_target="tpu_custom_call" | custom-call | tf_op jit(solution)/shard_map/finish_kernel/pallas_call | solution.py:271
  50.4 0.0 all-to-all-done
  50.4 0.7 %report_kernel.1 = (f32[3,3]{1,0:T(4,128)}, f32[1,1]{1,0:T(1,128)}) custom-call(f32[256,128]{1,0:T(8,128)S(1)} %bitcast.14), custom_call_target="tpu_custom_call" | custom-call | tf_op jit(solution)/shard_map/report_kernel/pallas_call | solution.py:271
  (5 shorter events, 0.0 us)
Async XLA Ops:
  0.6 0.8 %copy-start.1 = (f32[3,8,1,4,128]{4,3,2,1,0:T(4,128)S(1)}, f32[3,8,1,4,128]{4,3,2,1,0:T(4,128)}, u32[]{:S(2)}) copy-start(f32[3,8,1,4,128]{4,3,2,1,0:T(4,128)} %param.4) | copy-start | bytes 147460
  1.4 0.8 %copy-start.2 = (f32[3,8,1,4,128]{4,3,2,1,0:T(4,128)S(1)}, f32[3,8,1,4,128]{4,3,2,1,0:T(4,128)}, u32[]{:S(2)}) copy-start(f32[3,8,1,4,128]{4,3,2,1,0:T(4,128)} %param.5) | copy-start | bytes 147460
  2.2 0.7 %copy-start.3 = (s32[1,4,128]{2,1,0:T(4,128)S(1)}, s32[1,4,128]{2,1,0:T(4,128)}, u32[]{:S(2)}) copy-start(s32[1,4,128]{2,1,0:T(4,128)} %param.6) | copy-start | bytes 6148
  3.0 7.8 %collective-permute-start = (f32[8,128]{1,0:T(8,128)S(1)}, f32[8,128]{1,0:T(8,128)S(1)}, u32[]{:S(2)}, u32[]{:S(2)}) collective-permute-start(f32[8,128]{1,0:T(8,128)S(1)} %get-tuple-element.20), channel_id=1, source_target_pairs={{0,7},{1,0},{2,1},{3,2},{4,3},{5,4},{6,5},{7,6},{8,15},{9,8},{10,9... | collective-permute-start | bytes 12296 | tf_op jit(solution)/shard_map/ppermute | solution.py:286
  9.5 1.2 %copy-start = (bf16[14,8,8,1,4,128]{5,4,3,2,1,0:T(4,128)(2,1)S(1)}, bf16[14,8,8,1,4,128]{5,4,3,2,1,0:T(4,128)(2,1)}, u32[]{:S(2)}) copy-start(bf16[14,8,8,1,4,128]{5,4,3,2,1,0:T(4,128)(2,1)} %param.7) | copy-start | bytes 2752516
  10.9 3.8 %collective-permute-start.2 = (f32[7,8,128]{2,1,0:T(8,128)S(1)}, f32[7,8,128]{2,1,0:T(8,128)S(1)}, u32[]{:S(2)}, u32[]{:S(2)}) collective-permute-start(f32[7,8,128]{2,1,0:T(8,128)S(1)} %get-tuple-element.45), channel_id=1, source_target_pairs={{0,24},{8,0},{16,8},{24,16},{1,25},{9,1},{17,9},{25,17},{2,26},{10... | collective-permute-start | bytes 86024 | tf_op jit(solution)/shard_map/ppermute | solution.py:286
  13.7 3.9 %collective-permute-start.1 = (f32[7,8,128]{2,1,0:T(8,128)S(1)}, f32[7,8,128]{2,1,0:T(8,128)S(1)}, u32[]{:S(2)}, u32[]{:S(2)}) collective-permute-start(f32[7,8,128]{2,1,0:T(8,128)S(1)} %get-tuple-element.46), channel_id=1, source_target_pairs={{0,8},{8,16},{16,24},{24,0},{1,9},{9,17},{17,25},{25,1},{2,10},{10... | collective-permute-start | bytes 86024 | tf_op jit(solution)/shard_map/ppermute | solution.py:286
  17.7 6.4 %collective-permute-start.4 = (f32[37,8,128]{2,1,0:T(8,128)S(1)}, f32[37,8,128]{2,1,0:T(8,128)S(1)}, u32[]{:S(2)}, u32[]{:S(2)}) collective-permute-start(f32[37,8,128]{2,1,0:T(8,128)S(1)} %widen_kernel.1.m_ref), channel_id=1, source_target_pairs={{0,224},{32,0},{64,32},{96,64},{128,96},{160,128},{192,160},{224,1... | collective-permute-start | bytes 454664 | tf_op jit(solution)/shard_map/ppermute | solution.py:286
  20.1 4.0 %collective-permute-start.3 = (f32[37,8,128]{2,1,0:T(8,128)S(1)}, f32[37,8,128]{2,1,0:T(8,128)S(1)}, u32[]{:S(2)}, u32[]{:S(2)}) collective-permute-start(f32[37,8,128]{2,1,0:T(8,128)S(1)} %widen_kernel.1.m_ref), channel_id=1, source_target_pairs={{0,32},{32,64},{64,96},{96,128},{128,160},{160,192},{192,224},{224... | collective-permute-start | bytes 454664 | tf_op jit(solution)/shard_map/ppermute | solution.py:286
  26.6 10.3 %collective-permute-start.5 = (f32[20,8,128]{2,1,0:T(8,128)S(1)}, f32[20,8,128]{2,1,0:T(8,128)S(1)}, u32[]{:S(2)}, u32[]{:S(2)}) collective-permute-start(f32[20,8,128]{2,1,0:T(8,128)S(1)} %get-tuple-element.30), channel_id=1, source_target_pairs={{0,32},{32,64},{64,96},{96,128},{128,160},{160,192},{192,224},{224... | collective-permute-start | bytes 245768 | tf_op jit(solution)/shard_map/ppermute | solution.py:286
  28.4 8.6 %collective-permute-start.6 = (f32[20,8,128]{2,1,0:T(8,128)S(1)}, f32[20,8,128]{2,1,0:T(8,128)S(1)}, u32[]{:S(2)}, u32[]{:S(2)}) collective-permute-start(f32[20,8,128]{2,1,0:T(8,128)S(1)} %get-tuple-element.31), channel_id=1, source_target_pairs={{0,224},{32,0},{64,32},{96,64},{128,96},{160,128},{192,160},{224,1... | collective-permute-start | bytes 245768 | tf_op jit(solution)/shard_map/ppermute | solution.py:286
  29.0 21.4 %all-to-all-start = ((f32[256,1,128]{2,1,0:T(1,128)}), f32[256,1,128]{2,1,0:T(1,128)S(1)}, u32[]{:S(2)}, u32[]{:S(2)}) async-start(f32[256,1,128]{2,1,0:T(1,128)} %bitcast.8), calls=%async_computation | async-start | bytes 262144 | tf_op jit(solution)/shard_map/all_to_all | solution.py:322
  37.0 3.7 %collective-permute-start.8 = (f32[4,8,128]{2,1,0:T(8,128)S(1)}, f32[4,8,128]{2,1,0:T(8,128)S(1)}, u32[]{:S(2)}, u32[]{:S(2)}) collective-permute-start(f32[4,8,128]{2,1,0:T(8,128)S(1)} %get-tuple-element.43), channel_id=1, source_target_pairs={{0,24},{8,0},{16,8},{24,16},{1,25},{9,1},{17,9},{25,17},{2,26},{10... | collective-permute-start | bytes 49160 | tf_op jit(solution)/shard_map/ppermute | solution.py:286
  39.9 4.1 %collective-permute-start.7 = (f32[4,8,128]{2,1,0:T(8,128)S(1)}, f32[4,8,128]{2,1,0:T(8,128)S(1)}, u32[]{:S(2)}, u32[]{:S(2)}) collective-permute-start(f32[4,8,128]{2,1,0:T(8,128)S(1)} %get-tuple-element.44), channel_id=1, source_target_pairs={{0,8},{8,16},{16,24},{24,0},{1,9},{9,17},{17,25},{25,1},{2,10},{10... | collective-permute-start | bytes 49160 | tf_op jit(solution)/shard_map/ppermute | solution.py:286
  44.0 5.6 %collective-permute-start.9 = (f32[8,128]{1,0:T(8,128)S(1)}, f32[8,128]{1,0:T(8,128)S(1)}, u32[]{:S(2)}, u32[]{:S(2)}) collective-permute-start(f32[8,128]{1,0:T(8,128)S(1)} %last_plane_kernel.1), channel_id=1, source_target_pairs={{0,1},{1,2},{2,3},{3,4},{4,5},{5,6},{6,7},{7,0},{8,9},{9,10},{10,1... | collective-permute-start | bytes 12296 | tf_op jit(solution)/shard_map/ppermute | solution.py:286

commit v2 on v1

--- a/solution.py
+++ b/solution.py
@@ -16,6 +16,7 @@
 REST = 25.0 / 15.0
 DRAG = 4.5 / 15.0
 HALF_ROOT = 0.7071067811865476
+BACK = 16
 
 
 def tile_index(dx, dy, dz):
@@ -45,7 +46,15 @@
     return jnp.broadcast_to(ref[(*lead, pl.ds(s, 1), slice(None))], (SLOTS, LANES))
 
 
-def pack_kernel(off_ref, vel_ref, occ_ref, v_ref, ownx_ref, z_ref):
+def pack_kernel(off_hbm, vel_hbm, occ_hbm, v_ref, ownx_ref, z_ref, off_ref, vel_ref, occ_ref, sems):
+    copies = [
+        pltpu.make_async_copy(src, dst, sems.at[i])
+        for i, (src, dst) in enumerate([(off_hbm, off_ref), (vel_hbm, vel_ref), (occ_hbm, occ_ref)])
+    ]
+    for copy in copies:
+        copy.start()
+    for copy in copies:
+        copy.wait()
     lane = lane_iota()
     slot = slot_iota()
     z = jnp.zeros((SLOTS, LANES), jnp.float32)
@@ -65,9 +74,7 @@
     z_ref[...] = z
 
 
-def convert_kernel(noise_ref, th_ref, ready_ref):
-    ready_ref[...] = jnp.zeros_like(ready_ref)
-
+def convert_kernel(noise_ref, th_ref):
     @pl.loop(0, th_ref.shape[0] // 256)
     def _(i):
         at = pl.ds(pl.multiple_of(i * 256, 256), 256)
@@ -149,12 +156,24 @@
     for at in range(18):
         up = ru_ref[at]
         z = jnp.where(lane == at, pltpu.roll(up, at + 1, 1), z)
-        out_ref[1 + at] = rl_ref[at] + jnp.where(lane == 0, 0.0, pltpu.roll(up, 1, 1))
-    out_ref[0] = z
-    out_ref[19] = z
-
-
-def own_column_kernel(m_ref, ownx_ref, th_ref, d_ref, r_ref, acc_ref, up_ref, rl_ref, ru_ref):
+        out_ref[at] = rl_ref[at] + jnp.where(lane == 0, 0.0, pltpu.roll(up, 1, 1))
+    return z
+
+
+def send_past(z, sizes, at, dx, tally, rows_ref):
+    lane = lax.broadcasted_iota(jnp.int32, (1, LANES), 1)
+    column = (at[0] + (dx + sizes[0])) % sizes[0] * sizes[1]
+    for dy, row, count, place in [(-1, 0, 1, 3), (0, 1, 4, 0), (1, 5, 1, 0)]:
+        line = tally
+        for t in range(SLOTS):
+            to = BACK + t * 12 + place * 3
+            moved = pltpu.roll(z[t : t + 1, :], (to - row * 3) % LANES, 1)
+            line = jnp.where((lane >= to) & (lane < to + 3 * count), moved, line)
+        dest = (column + (at[1] + (dy + sizes[1])) % sizes[1]) * sizes[2] + (at[2] + 1) % sizes[2]
+        rows_ref[pl.ds(dest, 1), :] = line
+
+
+def own_column_kernel(m_ref, ownx_ref, th_ref, d_ref, r_ref, z_ref, acc_ref, up_ref, rl_ref, ru_ref):
     next_plane(m_ref, 0, up_ref)
     zero = jnp.zeros((18, SLOTS, LANES), jnp.float32)
     rl_ref[...] = zero
@@ -178,11 +197,11 @@
             acc_ref[6 + i] = acc_ref[6 + i] + live * vel[a] * vel[b]
         acc_ref[12] = acc_ref[12] + live
 
-    settle(rl_ref, ru_ref, r_ref)
+    z_ref[...] = settle(rl_ref, ru_ref, r_ref)
 
 
 def side_columns_kernel(
-    m_ref, ownx_ref, th_ref, xm_ref, xp_ref, d0_ref, acc0_ref,
+    sizes, here_ref, m_ref, ownx_ref, th_ref, xm_ref, xp_ref, d0_ref, z0_ref, acc0_ref,
     d_ref, rm_ref, rp_ref, tally_ref,
     um_ref, up_ref, rlm_ref, rum_ref, rlp_ref, rup_ref, acc_ref,
 ):
@@ -207,8 +226,7 @@
                 at = (y * 3 + a, pl.ds(s, 1), slice(None))
                 d_ref[at] = d0_ref[at] + jnp.sum(d[s][a], axis=0, keepdims=True)
 
-    settle(rlm_ref, rum_ref, rm_ref)
-    settle(rlp_ref, rup_ref, rp_ref)
+    planes = [settle(rlm_ref, rum_ref, rm_ref), z0_ref[...], settle(rlp_ref, rup_ref, rp_ref)]
     acc = [acc_ref[i] for i in range(13)]
     sums = [NOISE_SCALE * acc[i] + acc[6 + i] * (1.0 / (DRAG * DRAG)) for i in range(6)]
     lines = [sums[PRODUCTS.index((min(a, b), max(a, b)))] for a in range(3) for b in range(3)]
@@ -220,38 +238,33 @@
     held = jnp.where(lane == line, jnp.sum(held, axis=1, keepdims=True), 0.0)
     tally = jnp.sum(held, axis=0, keepdims=True)
     tally_ref[...] = jnp.broadcast_to(tally, tally_ref.shape)
-
-
-def last_plane_kernel(s_ref, ym_ref, yp_ref, z_ref):
-    lane = lane_iota()
-    z = s_ref[0]
-    z = z + jnp.where((lane >= 3) & (lane < 6), pltpu.roll(ym_ref[3], LANES - 12, 1), 0.0)
-    z = z + jnp.where((lane >= 12) & (lane < 15), pltpu.roll(yp_ref[0], 12, 1), 0.0)
-    z_ref[...] = z
-
-
-def finish_kernel(d_ref, s_ref, ym_ref, yp_ref, z_ref, f_ref):
-    lane = lane_iota()
-    for y in range(ROWS):
-        for a in range(3):
-            at = (y + 1) * 3 + a
-            back = s_ref[1 + at]
-            if y == 0:
-                back = back + ym_ref[a]
-            if y == ROWS - 1:
-                back = back + yp_ref[1 + a]
-            back = back + jnp.where(lane == 0, pltpu.roll(z_ref[...], LANES - at, 1), 0.0)
-            f_ref[a, pl.ds(y, SLOTS, stride=ROWS), :] = NOISE_SCALE * (d_ref[y * 3 + a] - back)
-
-
-def report_kernel(cells, tallies_ref, stress_ref, level_ref):
+    at = (here_ref[0] // (sizes[1] * sizes[2]), here_ref[0] // sizes[2] % sizes[1], here_ref[0] % sizes[2])
+    for dx, z in zip((-1, 0, 1), planes):
+        send_past(z, sizes, at, dx, tally, tally_ref)
+
+
+def finish_kernel(cells, d_ref, s_ref, ym_ref, yp_ref, tallies_ref, f_ref, stress_ref, level_ref):
+    lane = lane_iota()
+    slot = slot_iota()
     total = jnp.broadcast_to(jnp.sum(tallies_ref[...], axis=0, keepdims=True), (SLOTS, LANES))
-    slot = slot_iota()
     stress = jnp.where(slot == 1, pltpu.roll(total, LANES - 3, 1), total)
     stress = jnp.where(slot == 2, pltpu.roll(total, LANES - 6, 1), stress) * (1.0 / cells)
     stress_ref[...] = stress[0:3, 0:3]
     level = pltpu.roll(total, LANES - 9, 1) / (3.0 * pltpu.roll(total, LANES - 10, 1) - 3.0)
     level_ref[...] = level[0:1, 0:1]
+    z = pltpu.roll(total, LANES - BACK, 1)
+    for t in range(1, SLOTS):
+        z = jnp.where(slot == t, pltpu.roll(total, LANES - BACK - t * 12, 1), z)
+    for y in range(ROWS):
+        for a in range(3):
+            at = (y + 1) * 3 + a
+            back = s_ref[at]
+            if y == 0:
+                back = back + ym_ref[a]
+            if y == ROWS - 1:
+                back = back + yp_ref[a]
+            back = back + jnp.where(lane == 0, pltpu.roll(z, (LANES - y * 3 - a) % LANES, 1), 0.0)
+            f_ref[a, pl.ds(y, SLOTS, stride=ROWS), :] = NOISE_SCALE * (d_ref[y * 3 + a] - back)
 
 
 def f32(*shape):
@@ -262,16 +275,19 @@
     return pltpu.VMEM(shape, jnp.float32)
 
 
-def call(kernel, out_shape, scratch=(), hold=True):
+def call(kernel, out_shape, scratch=(), source=None, scalars=0):
     space = pl.BlockSpec(memory_space=pltpu.VMEM)
 
     def run(*args):
-        if hold:
-            args = [pltpu.with_memory_space_constraint(a, pltpu.VMEM) for a in args]
+        specs = [pl.BlockSpec(memory_space=source or pltpu.VMEM) for _ in args]
+        specs[:scalars] = [pl.BlockSpec(memory_space=pltpu.SMEM)] * scalars
+        if source is not pltpu.VMEM:
+            held = [pltpu.with_memory_space_constraint(a, source or pltpu.VMEM) for a in args[scalars:]]
+            args = (*args[:scalars], *held)
         return pl.pallas_call(
             kernel,
             out_shape=out_shape,
-            in_specs=[space for _ in args],
+            in_specs=specs,
             out_specs=jax.tree.map(lambda _: space, out_shape),
             scratch_shapes=list(scratch),
             compiler_params=pltpu.CompilerParams(vmem_limit_bytes=16 << 20),
@@ -279,6 +295,19 @@
         )(*args)
 
     return run
+
+
+def swapped(shard, axis, first):
+    count = lax.axis_size(axis)
+    pairs = [((first + i) % count, (first + i + 1) % count) for i in range(0, count, 2)]
+    return lax.ppermute(shard, axis, pairs + [(j, i) for i, j in pairs])
+
+
+def both_sides(low, high, axis):
+    even = lax.axis_index(axis) % 2 == 0
+    inner = swapped(jnp.where(even, high, low), axis, 0)
+    outer = swapped(jnp.where(even, low, high), axis, 1)
+    return jnp.where(even, outer, inner), jnp.where(even, inner, outer)
 
 
 def shifted(shard, axis, by):
@@ -292,38 +321,40 @@
     occ = occupancy.reshape(ROWS, LANES)
     tile = (SLOTS, LANES)
     lines = 14 * SLOTS * SLOTS * ROWS
-    theta, ready = call(convert_kernel, (f32(lines, LANES), f32(*tile)), hold=False)(noise.reshape(lines, LANES))
-    v, ownx, z = call(pack_kernel, (f32(24, *tile), f32(ROWS, *tile), f32(*tile)), hold=False)(off, vel, occ)
-    zr, ready = lax.optimization_barrier((shifted(z, "gz", -1), ready))
-    zr = zr + ready
-    from_ym = shifted(jnp.concatenate([v[18:24], zr[None]]), "gy", 1)
-    from_yp = shifted(jnp.concatenate([v[0:6], zr[None]]), "gy", -1)
+    theta = call(convert_kernel, f32(lines, LANES), source=pltpu.VMEM)(noise.reshape(lines, LANES))
+    v, ownx, z = call(
+        pack_kernel,
+        (f32(24, *tile), f32(ROWS, *tile), f32(*tile)),
+        [vmem(*off.shape), vmem(*off.shape), pltpu.VMEM(occ.shape, jnp.int32), pltpu.SemaphoreType.DMA((3,))],
+        source=pltpu.HBM,
+    )(off, vel, occ)
+    zr = shifted(z, "gz", -1)
+    low, high = (jnp.concatenate([part, zr[None]]) for part in (v[0:6], v[18:24]))
+    from_ym, from_yp = both_sides(low, high, "gy")
     m = call(widen_kernel, f32(37, *tile))(v, zr, from_ym, from_yp)
     from_xm = shifted(m, "gx", 1)
     from_xp = shifted(m, "gx", -1)
-    d0, r0, acc0 = call(
+    d0, r0, z0, acc0 = call(
         own_column_kernel,
-        (f32(12, *tile), f32(20, *tile), f32(16, *tile)),
+        (f32(12, *tile), f32(18, *tile), f32(*tile), f32(16, *tile)),
         [vmem(36, *tile), vmem(18, *tile), vmem(18, *tile)],
     )(m, ownx, theta)
-    devices = lax.axis_size(AXES)
+    sizes = tuple(lax.axis_size(axis) for axis in AXES)
+    devices = sizes[0] * sizes[1] * sizes[2]
+    here = jnp.reshape(lax.axis_index(AXES).astype(jnp.int32), (1,))
     d, rm, rp, tally = call(
-        side_columns_kernel,
-        (f32(12, *tile), f32(20, *tile), f32(20, *tile), f32(devices, LANES)),
+        functools.partial(side_columns_kernel, sizes),
+        (f32(12, *tile), f32(18, *tile), f32(18, *tile), f32(devices, LANES)),
         [vmem(36, *tile)] * 2 + [vmem(18, *tile)] * 4 + [vmem(16, *tile)],
-    )(m, ownx, theta, from_xm, from_xp, d0, acc0)
+        scalars=1,
+    )(here, m, ownx, theta, from_xm, from_xp, d0, z0, acc0)
     s = r0 + shifted(rp, "gx", 1) + shifted(rm, "gx", -1)
-    back_ym = shifted(s[16:20], "gy", 1)
-    back_yp = shifted(s[0:4], "gy", -1)
-    home = call(last_plane_kernel, f32(*tile))(s, back_ym, back_yp)
-    arrived = shifted(home, "gz", 1)
-    force_shape = jax.ShapeDtypeStruct((3, SLOTS * ROWS, LANES), jnp.float32)
-    force = call(finish_kernel, force_shape)(d, s, back_ym, back_yp, arrived)
+    back_ym, back_yp = both_sides(s[0:3], s[15:18], "gy")
     tallies = lax.all_to_all(tally, AXES, 0, 0, tiled=True)
-    stress, level = call(
-        functools.partial(report_kernel, float(ROWS * LANES * devices)),
-        (jax.ShapeDtypeStruct((3, 3), jnp.float32), jax.ShapeDtypeStruct((1, 1), jnp.float32)),
-    )(tallies)
+    force, stress, level = call(
+        functools.partial(finish_kernel, float(ROWS * LANES * devices)),
+        tuple(jax.ShapeDtypeStruct(x, jnp.float32) for x in (off.shape, (3, 3), (1, 1))),
+    )(d, s, back_ym, back_yp, tallies)
     return force.reshape(offset.shape), stress, level.reshape(1)
 
 

time: 51.9 us -> 49.8 us (0.960); the launches traced: 51.1 us -> 49.5 us
  local copies, waits for them, and re-layouts: 3.46 us -> 1.18 us
  starting transfers between devices: 27.4 us -> 28.6 us
  waiting for transfers between devices: 13.9 us -> 13.1 us
    ppermute x10 -> x5, waiting for transfers between devices: 13.9 us -> 1.37 us  [shifted(): lax.ppermute(shard, axis, [(i, (i + by) % count) for i in range(count)])]
    all_to_all x1, waiting for transfers between devices: 0.01 us -> 7.48 us  [per_device(): tallies = lax.all_to_all(tally, AXES, 0, 0, tiled=True)]
    ppermute x10 -> x5, starting transfers between devices: 19.4 us -> 12.1 us  [shifted(): lax.ppermute(shard, axis, [(i, (i + by) % count) for i in range(count)])]
    ppermute x0 -> x4, starting transfers between devices: none -> 6.43 us  [swapped(): return lax.ppermute(shard, axis, pairs + [(j, i) for i, j in pairs])]
    ppermute x0 -> x4, waiting for transfers between devices: none -> 4.29 us  [swapped(): return lax.ppermute(shard, axis, pairs + [(j, i) for i, j in pairs])]
    unnamed x8 -> x2, local copies, waits for them, and re-layouts: 3.45 us -> 1.18 us
    all_to_all x1, starting transfers between devices: 7.97 us -> 10.1 us  [per_device(): tallies = lax.all_to_all(tally, AXES, 0, 0, tiled=True)]
    pallas_call x8 -> x6, Pallas kernels: 5.57 us -> 5.85 us  [run(): pl.pallas_call(kernel, out_shape=out_shape, in_specs=specs, out_specs=jax...]
  transfers between devices with their start and end apart: 11 -> 10, of which waited for: 6 -> 5; matrix products, arithmetic and copies ran while one was open for 0% -> 0% of each run, Pallas kernels for 4% -> 3%
where the time goes in v2:
time: 49.8 us; the launch traced here: 49.5 us
  starting transfers between devices  28.6 us (57%)
  waiting for transfers between devices  13.1 us (26%)
  Pallas kernels  5.85 us (12%)
  local copies, waits for them, and re-layouts  1.18 us (2%)
  between operations  0.71 us (1%)
    ppermute x5, starting transfers between devices, shifted(): lax.ppermute(shard, axis, [(i, (i + by) % count) for i in range(count)])  12.1 us
    all_to_all x1, starting transfers between devices, per_device(): tallies = lax.all_to_all(tally, AXES, 0, 0, tiled=True)  10.1 us
    all_to_all x1, waiting for transfers between devices, per_device(): tallies = lax.all_to_all(tally, AXES, 0, 0, tiled=True)  7.48 us
    ppermute x4, starting transfers between devices, swapped(): return lax.ppermute(shard, axis, pairs + [(j, i) for i, j in pairs])  6.43 us
    pallas_call x6, Pallas kernels, run(): pl.pallas_call(kernel, out_shape=out_shape, in_specs=specs, out_specs=jax...  5.85 us
    ppermute x4, waiting for transfers between devices, swapped(): return lax.ppermute(shard, axis, pairs + [(j, i) for i, j in pairs])  4.29 us
    ppermute x5, waiting for transfers between devices, shifted(): lax.ppermute(shard, axis, [(i, (i + by) % count) for i in range(count)])  1.37 us
    unnamed x2, local copies, waits for them, and re-layouts  1.18 us
  transfers between devices with their start and end apart: 10, of which 5 were waited for; matrix products, arithmetic and copies ran while one was open for 0% of the time, Pallas kernels for 3%

profile of v2, /device:TPU:1, one launch (start us, length us, event | category | flops | bytes accessed | tf_op | source)
XLA Modules:
  0.0 49.5 jit_solution(15057218000917569521)
XLA Ops:
  0.6 0.9 %pack_kernel.1 = (f32[24,8,128]{2,1,0:T(8,128)S(1)}, f32[4,8,128]{2,1,0:T(8,128)S(1)}, f32[8,128]{1,0:T(8,128)S(1)}) custom-call(f32[3,32,128]{2,1,0:T(8,128)} %bitcast.17, f32[3,32,128]{2,1,0:T(8,128)} %bitcast.18, s32[4,128]{1,0:T(4,128)} %bitcast.19), custom_call_target="tpu_custom_call" | custom-call | tf_op jit(solution)/shard_map/pack_kernel/pallas_call | solution.py:287
  1.6 6.5 %collective-permute-start = (f32[8,128]{1,0:T(8,128)S(1)}, f32[8,128]{1,0:T(8,128)S(1)}, u32[]{:S(2)}, u32[]{:S(2)}) collective-permute-start(f32[8,128]{1,0:T(8,128)S(1)} %get-tuple-element.18), channel_id=1, source_target_pairs={{0,7},{1,0},{2,1},{3,2},{4,3},{5,4},{6,5},{7,6},{8,15},{9,8},{10,9... | collective-permute-start | bytes 12296 | tf_op jit(solution)/shard_map/ppermute | solution.py:315
  8.1 0.8 %collective-permute-done.zr_ref = f32[8,128]{1,0:T(8,128)S(1)} collective-permute-done((f32[8,128]{1,0:T(8,128)S(1)}, f32[8,128]{1,0:T(8,128)S(1)}, u32[]{:S(2)}, u32[]{:S(2)}) %collective-permute-start) | collective-permute-done | bytes 4128 | tf_op jit(solution)/shard_map/ppermute | solution.py:315
  8.8 1.3 %collective-permute-start.2 = (f32[7,8,128]{2,1,0:T(8,128)S(1)}, f32[7,8,128]{2,1,0:T(8,128)S(1)}, u32[]{:S(2)}, u32[]{:S(2)}) collective-permute-start(f32[7,8,128]{2,1,0:T(8,128)S(1)} %get-tuple-element.43), channel_id=1, source_target_pairs={{0,8},{16,24},{8,0},{24,16},{1,9},{17,25},{9,1},{25,17},{2,10},{18... | collective-permute-start | bytes 86024 | tf_op jit(solution)/shard_map/ppermute | solution.py:303
  10.1 1.9 %collective-permute-start.1 = (f32[7,8,128]{2,1,0:T(8,128)S(1)}, f32[7,8,128]{2,1,0:T(8,128)S(1)}, u32[]{:S(2)}, u32[]{:S(2)}) collective-permute-start(f32[7,8,128]{2,1,0:T(8,128)S(1)} %get-tuple-element.44), channel_id=1, source_target_pairs={{8,16},{24,0},{16,8},{0,24},{9,17},{25,1},{17,9},{1,25},{10,18},{2... | collective-permute-start | bytes 86024 | tf_op jit(solution)/shard_map/ppermute | solution.py:303
  12.0 0.0 collective-permute-done.2
  12.0 2.0 %collective-permute-done.1 = f32[7,8,128]{2,1,0:T(8,128)S(1)} collective-permute-done((f32[7,8,128]{2,1,0:T(8,128)S(1)}, f32[7,8,128]{2,1,0:T(8,128)S(1)}, u32[]{:S(2)}, u32[]{:S(2)}) %collective-permute-start.1) | collective-permute-done | bytes 28704 | tf_op jit(solution)/shard_map/ppermute | solution.py:303
  14.1 0.1 widen_kernel.1.m_ref
  14.1 3.0 %collective-permute-start.4 = (f32[37,8,128]{2,1,0:T(8,128)S(1)}, f32[37,8,128]{2,1,0:T(8,128)S(1)}, u32[]{:S(2)}, u32[]{:S(2)}) collective-permute-start(f32[37,8,128]{2,1,0:T(8,128)S(1)} %widen_kernel.1.m_ref), channel_id=1, source_target_pairs={{0,224},{32,0},{64,32},{96,64},{128,96},{160,128},{192,160},{224,1... | collective-permute-start | bytes 454664 | tf_op jit(solution)/shard_map/ppermute | solution.py:315
  17.1 1.1 %collective-permute-start.3 = (f32[37,8,128]{2,1,0:T(8,128)S(1)}, f32[37,8,128]{2,1,0:T(8,128)S(1)}, u32[]{:S(2)}, u32[]{:S(2)}) collective-permute-start(f32[37,8,128]{2,1,0:T(8,128)S(1)} %widen_kernel.1.m_ref), channel_id=1, source_target_pairs={{0,32},{32,64},{64,96},{96,128},{128,160},{160,192},{192,224},{224... | collective-permute-start | bytes 454664 | tf_op jit(solution)/shard_map/ppermute | solution.py:315
  18.2 0.0 copy-start
  18.2 1.2 %copy-done = bf16[14,8,8,1,4,128]{5,4,3,2,1,0:T(4,128)(2,1)S(1)} copy-done((bf16[14,8,8,1,4,128]{5,4,3,2,1,0:T(4,128)(2,1)S(1)}, bf16[14,8,8,1,4,128]{5,4,3,2,1,0:T(4,128)(2,1)}, u32[]{:S(2)}) %copy-start) | copy-done | bytes 917528
  19.4 0.2 convert_kernel.1.th_ref
  19.6 1.2 %own_column_kernel.1 = (f32[12,8,128]{2,1,0:T(8,128)S(1)}, f32[18,8,128]{2,1,0:T(8,128)S(1)}, f32[8,128]{1,0:T(8,128)S(1)}, f32[16,8,128]{2,1,0:T(8,128)S(1)}) custom-call(f32[37,8,128]{2,1,0:T(8,128)S(1)} %widen_kernel.1.m_ref, f32[4,8,128]{2,1,0:T(8,128)S(1)} %get-tuple-element.19.ownx_ref, f32[3584,128]{1,0:T(8,128)S(1)} %convert_kernel.1.th_ref), custom_call_target="tpu_custom_call" | custom-call | tf_op jit(solution)/shard_map/own_column_kernel/pallas_call | solution.py:287
  20.7 0.6 %collective-permute-done.4.xp_ref = f32[37,8,128]{2,1,0:T(8,128)S(1)} collective-permute-done((f32[37,8,128]{2,1,0:T(8,128)S(1)}, f32[37,8,128]{2,1,0:T(8,128)S(1)}, u32[]{:S(2)}, u32[]{:S(2)}) %collective-permute-start.4) | collective-permute-done | bytes 151584 | tf_op jit(solution)/shard_map/ppermute | solution.py:315
  21.4 0.0 collective-permute-done.3.xm_ref
  21.4 2.7 %side_columns_kernel.1 = (f32[12,8,128]{2,1,0:T(8,128)S(1)}, f32[18,8,128]{2,1,0:T(8,128)S(1)}, f32[18,8,128]{2,1,0:T(8,128)S(1)}, f32[256,128]{1,0:T(8,128)}) custom-call(s32[1]{0:T(128)} %bitcast.here_ref, f32[37,8,128]{2,1,0:T(8,128)S(1)} %widen_kernel.1.m_ref, f32[4,8,128]{2,1,0:T(8,128)S(1)} %get-tuple-element.19.ownx_ref, ...), custom_call_target="tpu_custom_call" | custom-call | tf_op jit(solution)/shard_map/side_columns_kernel/pallas_call | solution.py:287
  24.0 1.4 %collective-permute-start.5 = (f32[18,8,128]{2,1,0:T(8,128)S(1)}, f32[18,8,128]{2,1,0:T(8,128)S(1)}, u32[]{:S(2)}, u32[]{:S(2)}) collective-permute-start(f32[18,8,128]{2,1,0:T(8,128)S(1)} %get-tuple-element.25), channel_id=1, source_target_pairs={{0,32},{32,64},{64,96},{96,128},{128,160},{160,192},{192,224},{224... | collective-permute-start | bytes 221192 | tf_op jit(solution)/shard_map/ppermute | solution.py:315
  25.5 0.1 collective-permute-start.6
  25.6 10.1 %all-to-all-start = ((f32[256,1,128]{2,1,0:T(1,128)}), f32[256,1,128]{2,1,0:T(1,128)S(1)}, u32[]{:S(2)}, u32[]{:S(2)}) async-start(f32[256,1,128]{2,1,0:T(1,128)} %bitcast.7), calls=%async_computation | async-start | bytes 262144 | tf_op jit(solution)/shard_map/all_to_all | solution.py:353
  35.7 0.0 collective-permute-done.5
  35.7 0.0 collective-permute-done.6
  35.7 1.4 %collective-permute-start.8 = (f32[3,8,128]{2,1,0:T(8,128)S(1)}, f32[3,8,128]{2,1,0:T(8,128)S(1)}, u32[]{:S(2)}, u32[]{:S(2)}) collective-permute-start(f32[3,8,128]{2,1,0:T(8,128)S(1)} %get-tuple-element.39), channel_id=1, source_target_pairs={{0,8},{16,24},{8,0},{24,16},{1,9},{17,25},{9,1},{25,17},{2,10},{18... | collective-permute-start | bytes 36872 | tf_op jit(solution)/shard_map/ppermute | solution.py:303
  37.2 1.8 %collective-permute-start.7 = (f32[3,8,128]{2,1,0:T(8,128)S(1)}, f32[3,8,128]{2,1,0:T(8,128)S(1)}, u32[]{:S(2)}, u32[]{:S(2)}) collective-permute-start(f32[3,8,128]{2,1,0:T(8,128)S(1)} %get-tuple-element.40), channel_id=1, source_target_pairs={{8,16},{24,0},{16,8},{0,24},{9,17},{25,1},{17,9},{1,25},{10,18},{2... | collective-permute-start | bytes 36872 | tf_op jit(solution)/shard_map/ppermute | solution.py:303
  39.0 0.0 collective-permute-done.8
  39.0 2.3 %collective-permute-done.7 = f32[3,8,128]{2,1,0:T(8,128)S(1)} collective-permute-done((f32[3,8,128]{2,1,0:T(8,128)S(1)}, f32[3,8,128]{2,1,0:T(8,128)S(1)}, u32[]{:S(2)}, u32[]{:S(2)}) %collective-permute-start.7) | collective-permute-done | bytes 12320 | tf_op jit(solution)/shard_map/ppermute | solution.py:303
  41.2 7.5 %all-to-all-done = f32[256,1,128]{2,1,0:T(1,128)S(1)} async-done(((f32[256,1,128]{2,1,0:T(1,128)}), f32[256,1,128]{2,1,0:T(1,128)S(1)}, u32[]{:S(2)}, u32[]{:S(2)}) %all-to-all-start) | async-done | bytes 131104 | tf_op jit(solution)/shard_map/all_to_all | solution.py:353
  48.7 0.8 %finish_kernel.1 = (f32[3,32,128]{2,1,0:T(8,128)}, f32[3,3]{1,0:T(4,128)}, f32[1,1]{1,0:T(1,128)}) custom-call(f32[12,8,128]{2,1,0:T(8,128)S(1)} %get-tuple-element.23.d_ref, f32[18,8,128]{2,1,0:T(8,128)S(1)} %add_add_fusion.s_ref, f32[3,8,128]{2,1,0:T(8,128)S(1)} %get-tuple-element.46.ym_ref, f32[3,8,128]{2,1,0:T(8,128)S(1)} %get-tuple-element.45.yp_ref, ...), custom_call_target="tpu_custom_call" | custom-call | tf_op jit(solution)/shard_map/finish_kernel/pallas_call | solution.py:287
  (6 shorter events, 0.0 us)
Async XLA Ops:
  1.6 7.2 %collective-permute-start = (f32[8,128]{1,0:T(8,128)S(1)}, f32[8,128]{1,0:T(8,128)S(1)}, u32[]{:S(2)}, u32[]{:S(2)}) collective-permute-start(f32[8,128]{1,0:T(8,128)S(1)} %get-tuple-element.18), channel_id=1, source_target_pairs={{0,7},{1,0},{2,1},{3,2},{4,3},{5,4},{6,5},{7,6},{8,15},{9,8},{10,9... | collective-permute-start | bytes 12296 | tf_op jit(solution)/shard_map/ppermute | solution.py:315
  8.8 3.2 %collective-permute-start.2 = (f32[7,8,128]{2,1,0:T(8,128)S(1)}, f32[7,8,128]{2,1,0:T(8,128)S(1)}, u32[]{:S(2)}, u32[]{:S(2)}) collective-permute-start(f32[7,8,128]{2,1,0:T(8,128)S(1)} %get-tuple-element.43), channel_id=1, source_target_pairs={{0,8},{16,24},{8,0},{24,16},{1,9},{17,25},{9,1},{25,17},{2,10},{18... | collective-permute-start | bytes 86024 | tf_op jit(solution)/shard_map/ppermute | solution.py:303
  10.1 3.9 %collective-permute-start.1 = (f32[7,8,128]{2,1,0:T(8,128)S(1)}, f32[7,8,128]{2,1,0:T(8,128)S(1)}, u32[]{:S(2)}, u32[]{:S(2)}) collective-permute-start(f32[7,8,128]{2,1,0:T(8,128)S(1)} %get-tuple-element.44), channel_id=1, source_target_pairs={{8,16},{24,0},{16,8},{0,24},{9,17},{25,1},{17,9},{1,25},{10,18},{2... | collective-permute-start | bytes 86024 | tf_op jit(solution)/shard_map/ppermute | solution.py:303
  14.1 7.2 %collective-permute-start.4 = (f32[37,8,128]{2,1,0:T(8,128)S(1)}, f32[37,8,128]{2,1,0:T(8,128)S(1)}, u32[]{:S(2)}, u32[]{:S(2)}) collective-permute-start(f32[37,8,128]{2,1,0:T(8,128)S(1)} %widen_kernel.1.m_ref), channel_id=1, source_target_pairs={{0,224},{32,0},{64,32},{96,64},{128,96},{160,128},{192,160},{224,1... | collective-permute-start | bytes 454664 | tf_op jit(solution)/shard_map/ppermute | solution.py:315
  17.1 4.3 %collective-permute-start.3 = (f32[37,8,128]{2,1,0:T(8,128)S(1)}, f32[37,8,128]{2,1,0:T(8,128)S(1)}, u32[]{:S(2)}, u32[]{:S(2)}) collective-permute-start(f32[37,8,128]{2,1,0:T(8,128)S(1)} %widen_kernel.1.m_ref), channel_id=1, source_target_pairs={{0,32},{32,64},{64,96},{96,128},{128,160},{160,192},{192,224},{224... | collective-permute-start | bytes 454664 | tf_op jit(solution)/shard_map/ppermute | solution.py:315
  18.2 1.2 %copy-start = (bf16[14,8,8,1,4,128]{5,4,3,2,1,0:T(4,128)(2,1)S(1)}, bf16[14,8,8,1,4,128]{5,4,3,2,1,0:T(4,128)(2,1)}, u32[]{:S(2)}) copy-start(bf16[14,8,8,1,4,128]{5,4,3,2,1,0:T(4,128)(2,1)} %param.7) | copy-start | bytes 2752516
  24.0 11.7 %collective-permute-start.5 = (f32[18,8,128]{2,1,0:T(8,128)S(1)}, f32[18,8,128]{2,1,0:T(8,128)S(1)}, u32[]{:S(2)}, u32[]{:S(2)}) collective-permute-start(f32[18,8,128]{2,1,0:T(8,128)S(1)} %get-tuple-element.25), channel_id=1, source_target_pairs={{0,32},{32,64},{64,96},{96,128},{128,160},{160,192},{192,224},{224... | collective-permute-start | bytes 221192 | tf_op jit(solution)/shard_map/ppermute | solution.py:315
  25.5 10.2 %collective-permute-start.6 = (f32[18,8,128]{2,1,0:T(8,128)S(1)}, f32[18,8,128]{2,1,0:T(8,128)S(1)}, u32[]{:S(2)}, u32[]{:S(2)}) collective-permute-start(f32[18,8,128]{2,1,0:T(8,128)S(1)} %get-tuple-element.26), channel_id=1, source_target_pairs={{0,224},{32,0},{64,32},{96,64},{128,96},{160,128},{192,160},{224,1... | collective-permute-start | bytes 221192 | tf_op jit(solution)/shard_map/ppermute | solution.py:315
  25.6 23.1 %all-to-all-start = ((f32[256,1,128]{2,1,0:T(1,128)}), f32[256,1,128]{2,1,0:T(1,128)S(1)}, u32[]{:S(2)}, u32[]{:S(2)}) async-start(f32[256,1,128]{2,1,0:T(1,128)} %bitcast.7), calls=%async_computation | async-start | bytes 262144 | tf_op jit(solution)/shard_map/all_to_all | solution.py:353
  35.7 3.2 %collective-permute-start.8 = (f32[3,8,128]{2,1,0:T(8,128)S(1)}, f32[3,8,128]{2,1,0:T(8,128)S(1)}, u32[]{:S(2)}, u32[]{:S(2)}) collective-permute-start(f32[3,8,128]{2,1,0:T(8,128)S(1)} %get-tuple-element.39), channel_id=1, source_target_pairs={{0,8},{16,24},{8,0},{24,16},{1,9},{17,25},{9,1},{25,17},{2,10},{18... | collective-permute-start | bytes 36872 | tf_op jit(solution)/shard_map/ppermute | solution.py:303
  37.2 4.1 %collective-permute-start.7 = (f32[3,8,128]{2,1,0:T(8,128)S(1)}, f32[3,8,128]{2,1,0:T(8,128)S(1)}, u32[]{:S(2)}, u32[]{:S(2)}) collective-permute-start(f32[3,8,128]{2,1,0:T(8,128)S(1)} %get-tuple-element.40), channel_id=1, source_target_pairs={{8,16},{24,0},{16,8},{0,24},{9,17},{25,1},{17,9},{1,25},{10,18},{2... | collective-permute-start | bytes 36872 | tf_op jit(solution)/shard_map/ppermute | solution.py:303

commit v3 on v2

--- a/solution.py
+++ b/solution.py
@@ -6,6 +6,7 @@
 from jax.experimental import pallas as pl
 from jax.experimental.pallas import tpu as pltpu
 from jax.sharding import PartitionSpec as P
+
 
 AXES = ("gx", "gy", "gz")
 ROWS = 4
@@ -93,7 +94,7 @@
     m_ref[36] = z
 
 
-def next_plane(m_ref, dx, up_ref):
+def next_plane(m_ref, up_ref):
     lane = lane_iota()
     z = m_ref[36]
     for row in range(6):
@@ -174,7 +175,7 @@
 
 
 def own_column_kernel(m_ref, ownx_ref, th_ref, d_ref, r_ref, z_ref, acc_ref, up_ref, rl_ref, ru_ref):
-    next_plane(m_ref, 0, up_ref)
+    next_plane(m_ref, up_ref)
     zero = jnp.zeros((18, SLOTS, LANES), jnp.float32)
     rl_ref[...] = zero
     ru_ref[...] = zero
@@ -205,8 +206,8 @@
     d_ref, rm_ref, rp_ref, tally_ref,
     um_ref, up_ref, rlm_ref, rum_ref, rlp_ref, rup_ref, acc_ref,
 ):
-    next_plane(xm_ref, -1, um_ref)
-    next_plane(xp_ref, 1, up_ref)
+    next_plane(xm_ref, um_ref)
+    next_plane(xp_ref, up_ref)
     zero = jnp.zeros((18, SLOTS, LANES), jnp.float32)
     for ref in (rlm_ref, rum_ref, rlp_ref, rup_ref):
         ref[...] = zero
@@ -291,7 +292,6 @@
             out_specs=jax.tree.map(lambda _: space, out_shape),
             scratch_shapes=list(scratch),
             compiler_params=pltpu.CompilerParams(vmem_limit_bytes=16 << 20),
-            name=getattr(kernel, "func", kernel).__name__,
         )(*args)
 
     return run
@@ -305,8 +305,8 @@
 
 def both_sides(low, high, axis):
     even = lax.axis_index(axis) % 2 == 0
+    outer = swapped(jnp.where(even, low, high), axis, 1)
     inner = swapped(jnp.where(even, high, low), axis, 0)
-    outer = swapped(jnp.where(even, low, high), axis, 1)
     return jnp.where(even, outer, inner), jnp.where(even, inner, outer)
 
 

time: 49.8 us -> 49.8 us (level)
  no operation moved by 1% of the time
where the time goes in v3:
time: 49.8 us; the launch traced here: 49.5 us
  starting transfers between devices  28.6 us (57%)
  waiting for transfers between devices  13.1 us (26%)
  Pallas kernels  5.85 us (12%)
  local copies, waits for them, and re-layouts  1.18 us (2%)
  between operations  0.71 us (1%)
    ppermute x5, starting transfers between devices, shifted(): lax.ppermute(shard, axis, [(i, (i + by) % count) for i in range(count)])  12.1 us
    all_to_all x1, starting transfers between devices, per_device(): tallies = lax.all_to_all(tally, AXES, 0, 0, tiled=True)  10.1 us
    all_to_all x1, waiting for transfers between devices, per_device(): tallies = lax.all_to_all(tally, AXES, 0, 0, tiled=True)  7.48 us
    ppermute x4, starting transfers between devices, swapped(): return lax.ppermute(shard, axis, pairs + [(j, i) for i, j in pairs])  6.43 us
    pallas_call x6, Pallas kernels, run(): pl.pallas_call(kernel, out_shape=out_shape, in_specs=specs, out_specs=jax...  5.85 us
    ppermute x4, waiting for transfers between devices, swapped(): return lax.ppermute(shard, axis, pairs + [(j, i) for i, j in pairs])  4.29 us
    ppermute x5, waiting for transfers between devices, shifted(): lax.ppermute(shard, axis, [(i, (i + by) % count) for i in range(count)])  1.37 us
    unnamed x2, local copies, waits for them, and re-layouts  1.18 us
  transfers between devices with their start and end apart: 10, of which 5 were waited for; matrix products, arithmetic and copies ran while one was open for 0% of the time, Pallas kernels for 3%

profile of v3, /device:TPU:1, one launch (start us, length us, event | category | flops | bytes accessed | tf_op | source)
XLA Modules:
  0.0 49.5 jit_solution(15057218000917569521)
XLA Ops:
  0.6 0.9 %shard_map.67 = (f32[24,8,128]{2,1,0:T(8,128)S(1)}, f32[4,8,128]{2,1,0:T(8,128)S(1)}, f32[8,128]{1,0:T(8,128)S(1)}) custom-call(f32[3,32,128]{2,1,0:T(8,128)} %bitcast.17, f32[3,32,128]{2,1,0:T(8,128)} %bitcast.18, s32[4,128]{1,0:T(4,128)} %bitcast.19), custom_call_target="tpu_custom_call" | custom-call | tf_op jit(solution)/shard_map/pallas_call | solution.py:288
  1.6 6.5 %collective-permute-start = (f32[8,128]{1,0:T(8,128)S(1)}, f32[8,128]{1,0:T(8,128)S(1)}, u32[]{:S(2)}, u32[]{:S(2)}) collective-permute-start(f32[8,128]{1,0:T(8,128)S(1)} %get-tuple-element.18), channel_id=1, source_target_pairs={{0,7},{1,0},{2,1},{3,2},{4,3},{5,4},{6,5},{7,6},{8,15},{9,8},{10,9... | collective-permute-start | bytes 12296 | tf_op jit(solution)/shard_map/ppermute | solution.py:315
  8.1 0.8 %collective-permute-done.zr_ref = f32[8,128]{1,0:T(8,128)S(1)} collective-permute-done((f32[8,128]{1,0:T(8,128)S(1)}, f32[8,128]{1,0:T(8,128)S(1)}, u32[]{:S(2)}, u32[]{:S(2)}) %collective-permute-start) | collective-permute-done | bytes 4128 | tf_op jit(solution)/shard_map/ppermute | solution.py:315
  8.8 1.3 %collective-permute-start.2 = (f32[7,8,128]{2,1,0:T(8,128)S(1)}, f32[7,8,128]{2,1,0:T(8,128)S(1)}, u32[]{:S(2)}, u32[]{:S(2)}) collective-permute-start(f32[7,8,128]{2,1,0:T(8,128)S(1)} %get-tuple-element.43), channel_id=1, source_target_pairs={{0,8},{16,24},{8,0},{24,16},{1,9},{17,25},{9,1},{25,17},{2,10},{18... | collective-permute-start | bytes 86024 | tf_op jit(solution)/shard_map/ppermute | solution.py:303
  10.1 1.9 %collective-permute-start.1 = (f32[7,8,128]{2,1,0:T(8,128)S(1)}, f32[7,8,128]{2,1,0:T(8,128)S(1)}, u32[]{:S(2)}, u32[]{:S(2)}) collective-permute-start(f32[7,8,128]{2,1,0:T(8,128)S(1)} %get-tuple-element.44), channel_id=1, source_target_pairs={{8,16},{24,0},{16,8},{0,24},{9,17},{25,1},{17,9},{1,25},{10,18},{2... | collective-permute-start | bytes 86024 | tf_op jit(solution)/shard_map/ppermute | solution.py:303
  12.0 0.0 collective-permute-done.2
  12.0 2.0 %collective-permute-done.1 = f32[7,8,128]{2,1,0:T(8,128)S(1)} collective-permute-done((f32[7,8,128]{2,1,0:T(8,128)S(1)}, f32[7,8,128]{2,1,0:T(8,128)S(1)}, u32[]{:S(2)}, u32[]{:S(2)}) %collective-permute-start.1) | collective-permute-done | bytes 28704 | tf_op jit(solution)/shard_map/ppermute | solution.py:303
  14.1 0.1 shard_map.68.m_ref
  14.1 3.0 %collective-permute-start.4 = (f32[37,8,128]{2,1,0:T(8,128)S(1)}, f32[37,8,128]{2,1,0:T(8,128)S(1)}, u32[]{:S(2)}, u32[]{:S(2)}) collective-permute-start(f32[37,8,128]{2,1,0:T(8,128)S(1)} %shard_map.68.m_ref), channel_id=1, source_target_pairs={{0,224},{32,0},{64,32},{96,64},{128,96},{160,128},{192,160},{224,1... | collective-permute-start | bytes 454664 | tf_op jit(solution)/shard_map/ppermute | solution.py:315
  17.1 1.1 %collective-permute-start.3 = (f32[37,8,128]{2,1,0:T(8,128)S(1)}, f32[37,8,128]{2,1,0:T(8,128)S(1)}, u32[]{:S(2)}, u32[]{:S(2)}) collective-permute-start(f32[37,8,128]{2,1,0:T(8,128)S(1)} %shard_map.68.m_ref), channel_id=1, source_target_pairs={{0,32},{32,64},{64,96},{96,128},{128,160},{160,192},{192,224},{224... | collective-permute-start | bytes 454664 | tf_op jit(solution)/shard_map/ppermute | solution.py:315
  18.2 0.0 copy-start
  18.2 1.2 %copy-done = bf16[14,8,8,1,4,128]{5,4,3,2,1,0:T(4,128)(2,1)S(1)} copy-done((bf16[14,8,8,1,4,128]{5,4,3,2,1,0:T(4,128)(2,1)S(1)}, bf16[14,8,8,1,4,128]{5,4,3,2,1,0:T(4,128)(2,1)}, u32[]{:S(2)}) %copy-start) | copy-done | bytes 917528
  19.4 0.2 shard_map.69.th_ref
  19.6 1.2 %shard_map.70 = (f32[12,8,128]{2,1,0:T(8,128)S(1)}, f32[18,8,128]{2,1,0:T(8,128)S(1)}, f32[8,128]{1,0:T(8,128)S(1)}, f32[16,8,128]{2,1,0:T(8,128)S(1)}) custom-call(f32[37,8,128]{2,1,0:T(8,128)S(1)} %shard_map.68.m_ref, f32[4,8,128]{2,1,0:T(8,128)S(1)} %get-tuple-element.19.ownx_ref, f32[3584,128]{1,0:T(8,128)S(1)} %shard_map.69.th_ref), custom_call_target="tpu_custom_call" | custom-call | tf_op jit(solution)/shard_map/pallas_call | solution.py:288
  20.7 0.6 %collective-permute-done.4.xp_ref = f32[37,8,128]{2,1,0:T(8,128)S(1)} collective-permute-done((f32[37,8,128]{2,1,0:T(8,128)S(1)}, f32[37,8,128]{2,1,0:T(8,128)S(1)}, u32[]{:S(2)}, u32[]{:S(2)}) %collective-permute-start.4) | collective-permute-done | bytes 151584 | tf_op jit(solution)/shard_map/ppermute | solution.py:315
  21.4 0.0 collective-permute-done.3.xm_ref
  21.4 2.7 %shard_map.71 = (f32[12,8,128]{2,1,0:T(8,128)S(1)}, f32[18,8,128]{2,1,0:T(8,128)S(1)}, f32[18,8,128]{2,1,0:T(8,128)S(1)}, f32[256,128]{1,0:T(8,128)}) custom-call(s32[1]{0:T(128)} %bitcast.here_ref, f32[37,8,128]{2,1,0:T(8,128)S(1)} %shard_map.68.m_ref, f32[4,8,128]{2,1,0:T(8,128)S(1)} %get-tuple-element.19.ownx_ref, f32[3584,128]{1,0:T(8,128)S(1)} %shard_map.69.th_ref, ...), custom_call_target="tpu_custom_call" | custom-call | tf_op jit(solution)/shard_map/pallas_call | solution.py:288
  24.0 1.4 %collective-permute-start.5 = (f32[18,8,128]{2,1,0:T(8,128)S(1)}, f32[18,8,128]{2,1,0:T(8,128)S(1)}, u32[]{:S(2)}, u32[]{:S(2)}) collective-permute-start(f32[18,8,128]{2,1,0:T(8,128)S(1)} %get-tuple-element.25), channel_id=1, source_target_pairs={{0,32},{32,64},{64,96},{96,128},{128,160},{160,192},{192,224},{224... | collective-permute-start | bytes 221192 | tf_op jit(solution)/shard_map/ppermute | solution.py:315
  25.5 0.1 collective-permute-start.6
  25.6 10.1 %all-to-all-start = ((f32[256,1,128]{2,1,0:T(1,128)}), f32[256,1,128]{2,1,0:T(1,128)S(1)}, u32[]{:S(2)}, u32[]{:S(2)}) async-start(f32[256,1,128]{2,1,0:T(1,128)} %bitcast.7), calls=%async_computation | async-start | bytes 262144 | tf_op jit(solution)/shard_map/all_to_all | solution.py:353
  35.7 0.0 collective-permute-done.5
  35.7 0.0 collective-permute-done.6
  35.7 1.4 %collective-permute-start.8 = (f32[3,8,128]{2,1,0:T(8,128)S(1)}, f32[3,8,128]{2,1,0:T(8,128)S(1)}, u32[]{:S(2)}, u32[]{:S(2)}) collective-permute-start(f32[3,8,128]{2,1,0:T(8,128)S(1)} %get-tuple-element.39), channel_id=1, source_target_pairs={{0,8},{16,24},{8,0},{24,16},{1,9},{17,25},{9,1},{25,17},{2,10},{18... | collective-permute-start | bytes 36872 | tf_op jit(solution)/shard_map/ppermute | solution.py:303
  37.2 1.8 %collective-permute-start.7 = (f32[3,8,128]{2,1,0:T(8,128)S(1)}, f32[3,8,128]{2,1,0:T(8,128)S(1)}, u32[]{:S(2)}, u32[]{:S(2)}) collective-permute-start(f32[3,8,128]{2,1,0:T(8,128)S(1)} %get-tuple-element.40), channel_id=1, source_target_pairs={{8,16},{24,0},{16,8},{0,24},{9,17},{25,1},{17,9},{1,25},{10,18},{2... | collective-permute-start | bytes 36872 | tf_op jit(solution)/shard_map/ppermute | solution.py:303
  39.0 0.0 collective-permute-done.8
  39.0 2.3 %collective-permute-done.7 = f32[3,8,128]{2,1,0:T(8,128)S(1)} collective-permute-done((f32[3,8,128]{2,1,0:T(8,128)S(1)}, f32[3,8,128]{2,1,0:T(8,128)S(1)}, u32[]{:S(2)}, u32[]{:S(2)}) %collective-permute-start.7) | collective-permute-done | bytes 12320 | tf_op jit(solution)/shard_map/ppermute | solution.py:303
  41.2 7.5 %all-to-all-done = f32[256,1,128]{2,1,0:T(1,128)S(1)} async-done(((f32[256,1,128]{2,1,0:T(1,128)}), f32[256,1,128]{2,1,0:T(1,128)S(1)}, u32[]{:S(2)}, u32[]{:S(2)}) %all-to-all-start) | async-done | bytes 131104 | tf_op jit(solution)/shard_map/all_to_all | solution.py:353
  48.7 0.8 %shard_map.72 = (f32[3,32,128]{2,1,0:T(8,128)}, f32[3,3]{1,0:T(4,128)}, f32[1,1]{1,0:T(1,128)}) custom-call(f32[12,8,128]{2,1,0:T(8,128)S(1)} %get-tuple-element.23.d_ref, f32[18,8,128]{2,1,0:T(8,128)S(1)} %add_add_fusion.s_ref, f32[3,8,128]{2,1,0:T(8,128)S(1)} %get-tuple-element.46.ym_ref, f32[3,8,128]{2,1,0:T(8,128)S(1)} %get-tuple-element.45.yp_ref, ...), custom_call_target="tpu_custom_call" | custom-call | tf_op jit(solution)/shard_map/pallas_call | solution.py:288
  (6 shorter events, 0.0 us)
Async XLA Ops:
  1.6 7.2 %collective-permute-start = (f32[8,128]{1,0:T(8,128)S(1)}, f32[8,128]{1,0:T(8,128)S(1)}, u32[]{:S(2)}, u32[]{:S(2)}) collective-permute-start(f32[8,128]{1,0:T(8,128)S(1)} %get-tuple-element.18), channel_id=1, source_target_pairs={{0,7},{1,0},{2,1},{3,2},{4,3},{5,4},{6,5},{7,6},{8,15},{9,8},{10,9... | collective-permute-start | bytes 12296 | tf_op jit(solution)/shard_map/ppermute | solution.py:315
  8.8 3.2 %collective-permute-start.2 = (f32[7,8,128]{2,1,0:T(8,128)S(1)}, f32[7,8,128]{2,1,0:T(8,128)S(1)}, u32[]{:S(2)}, u32[]{:S(2)}) collective-permute-start(f32[7,8,128]{2,1,0:T(8,128)S(1)} %get-tuple-element.43), channel_id=1, source_target_pairs={{0,8},{16,24},{8,0},{24,16},{1,9},{17,25},{9,1},{25,17},{2,10},{18... | collective-permute-start | bytes 86024 | tf_op jit(solution)/shard_map/ppermute | solution.py:303
  10.1 3.9 %collective-permute-start.1 = (f32[7,8,128]{2,1,0:T(8,128)S(1)}, f32[7,8,128]{2,1,0:T(8,128)S(1)}, u32[]{:S(2)}, u32[]{:S(2)}) collective-permute-start(f32[7,8,128]{2,1,0:T(8,128)S(1)} %get-tuple-element.44), channel_id=1, source_target_pairs={{8,16},{24,0},{16,8},{0,24},{9,17},{25,1},{17,9},{1,25},{10,18},{2... | collective-permute-start | bytes 86024 | tf_op jit(solution)/shard_map/ppermute | solution.py:303
  14.1 7.2 %collective-permute-start.4 = (f32[37,8,128]{2,1,0:T(8,128)S(1)}, f32[37,8,128]{2,1,0:T(8,128)S(1)}, u32[]{:S(2)}, u32[]{:S(2)}) collective-permute-start(f32[37,8,128]{2,1,0:T(8,128)S(1)} %shard_map.68.m_ref), channel_id=1, source_target_pairs={{0,224},{32,0},{64,32},{96,64},{128,96},{160,128},{192,160},{224,1... | collective-permute-start | bytes 454664 | tf_op jit(solution)/shard_map/ppermute | solution.py:315
  17.1 4.3 %collective-permute-start.3 = (f32[37,8,128]{2,1,0:T(8,128)S(1)}, f32[37,8,128]{2,1,0:T(8,128)S(1)}, u32[]{:S(2)}, u32[]{:S(2)}) collective-permute-start(f32[37,8,128]{2,1,0:T(8,128)S(1)} %shard_map.68.m_ref), channel_id=1, source_target_pairs={{0,32},{32,64},{64,96},{96,128},{128,160},{160,192},{192,224},{224... | collective-permute-start | bytes 454664 | tf_op jit(solution)/shard_map/ppermute | solution.py:315
  18.2 1.2 %copy-start = (bf16[14,8,8,1,4,128]{5,4,3,2,1,0:T(4,128)(2,1)S(1)}, bf16[14,8,8,1,4,128]{5,4,3,2,1,0:T(4,128)(2,1)}, u32[]{:S(2)}) copy-start(bf16[14,8,8,1,4,128]{5,4,3,2,1,0:T(4,128)(2,1)} %param.7) | copy-start | bytes 2752516
  24.0 11.7 %collective-permute-start.5 = (f32[18,8,128]{2,1,0:T(8,128)S(1)}, f32[18,8,128]{2,1,0:T(8,128)S(1)}, u32[]{:S(2)}, u32[]{:S(2)}) collective-permute-start(f32[18,8,128]{2,1,0:T(8,128)S(1)} %get-tuple-element.25), channel_id=1, source_target_pairs={{0,32},{32,64},{64,96},{96,128},{128,160},{160,192},{192,224},{224... | collective-permute-start | bytes 221192 | tf_op jit(solution)/shard_map/ppermute | solution.py:315
  25.5 10.2 %collective-permute-start.6 = (f32[18,8,128]{2,1,0:T(8,128)S(1)}, f32[18,8,128]{2,1,0:T(8,128)S(1)}, u32[]{:S(2)}, u32[]{:S(2)}) collective-permute-start(f32[18,8,128]{2,1,0:T(8,128)S(1)} %get-tuple-element.26), channel_id=1, source_target_pairs={{0,224},{32,0},{64,32},{96,64},{128,96},{160,128},{192,160},{224,1... | collective-permute-start | bytes 221192 | tf_op jit(solution)/shard_map/ppermute | solution.py:315
  25.6 23.1 %all-to-all-start = ((f32[256,1,128]{2,1,0:T(1,128)}), f32[256,1,128]{2,1,0:T(1,128)S(1)}, u32[]{:S(2)}, u32[]{:S(2)}) async-start(f32[256,1,128]{2,1,0:T(1,128)} %bitcast.7), calls=%async_computation | async-start | bytes 262144 | tf_op jit(solution)/shard_map/all_to_all | solution.py:353
  35.7 3.2 %collective-permute-start.8 = (f32[3,8,128]{2,1,0:T(8,128)S(1)}, f32[3,8,128]{2,1,0:T(8,128)S(1)}, u32[]{:S(2)}, u32[]{:S(2)}) collective-permute-start(f32[3,8,128]{2,1,0:T(8,128)S(1)} %get-tuple-element.39), channel_id=1, source_target_pairs={{0,8},{16,24},{8,0},{24,16},{1,9},{17,25},{9,1},{25,17},{2,10},{18... | collective-permute-start | bytes 36872 | tf_op jit(solution)/shard_map/ppermute | solution.py:303
  37.2 4.1 %collective-permute-start.7 = (f32[3,8,128]{2,1,0:T(8,128)S(1)}, f32[3,8,128]{2,1,0:T(8,128)S(1)}, u32[]{:S(2)}, u32[]{:S(2)}) collective-permute-start(f32[3,8,128]{2,1,0:T(8,128)S(1)} %get-tuple-element.40), channel_id=1, source_target_pairs={{8,16},{24,0},{16,8},{0,24},{9,17},{25,1},{17,9},{1,25},{10,18},{2... | collective-permute-start | bytes 36872 | tf_op jit(solution)/shard_map/ppermute | solution.py:303

commit v4 on v3

--- a/solution.py
+++ b/solution.py
@@ -23,14 +23,10 @@
 def tile_index(dx, dy, dz):
     if dz == 1:
         return 5 + (dy + 1) * 3 + (dx + 1)
-    return {(0, 0): 0, (1, 0): 1, (-1, 1): 2, (0, 1): 3, (1, 1): 4}[(dx, dy)]
-
-
-COLUMN_TILES = {
-    0: [(0, 0), (1, 0), (-1, 1), (0, 1), (1, 1)],
-    1: [(0, 0), (1, 0), (-1, 1), (0, 1), (1, 1)],
-    -1: [(1, 0), (-1, 1), (0, 1), (1, 1)],
-}
+    return 3 + dx if dy else dx * dx
+
+
+TILES = [(0, 0), (1, 0), (-1, 1), (0, 1), (1, 1)]
 PRODUCTS = [(0, 0), (0, 1), (0, 2), (1, 1), (1, 2), (2, 2)]
 
 
@@ -75,14 +71,16 @@
     z_ref[...] = z
 
 
-def convert_kernel(noise_ref, th_ref):
+def convert_kernel(noise_ref, th_ref, ready_ref):
+    ready_ref[...] = jnp.zeros_like(ready_ref)
+
     @pl.loop(0, th_ref.shape[0] // 256)
     def _(i):
         at = pl.ds(pl.multiple_of(i * 256, 256), 256)
         th_ref[at, :] = noise_ref[at, :].astype(jnp.float32)
 
 
-def widen_kernel(v_ref, zr_ref, ym_ref, yp_ref, m_ref):
+def widen_kernel(v_ref, zr_ref, ym_ref, yp_ref, ready_ref, m_ref):
     lane = lane_iota()
     for c in range(6):
         m_ref[c] = ym_ref[c]
@@ -107,44 +105,48 @@
             up_ref[at] = val
 
 
-def row_pairs(y, columns, own_ref, ownx_ref, th_ref, rl_refs, ru_refs, vir):
+def row_pairs(y, dx, level_ref, up_ref, own_ref, ownx_ref, th_ref, rl_ref, ru_ref, vir):
     slot = slot_iota()
+    own_column = isinstance(dx, int)
     d = [[None] * 3 for _ in range(SLOTS)]
-    for dx, level_ref, up_ref in columns:
-        for dy, dz in COLUMN_TILES[dx]:
-            k = tile_index(dx, dy, dz)
-            src = up_ref if dz else level_ref
-            base = (y + 1 + dy) * 6
-            oth = [src[base + c] for c in range(6)]
-            if dx:
-                oth[0] = oth[0] + float(dx)
-            if dy:
-                oth[1] = oth[1] + float(dy)
-            r = [None] * 3
-            for s in range(SLOTS):
-                if k == 0 and s == SLOTS - 1:
-                    continue
-                own = [row_of(ownx_ref, y, s)] + [row_of(own_ref, (y + 1) * 6 + c, s) for c in range(1, 6)]
-                sep = [own[a] - oth[a] for a in range(3)]
-                rel = [own[3 + a] - oth[3 + a] for a in range(3)]
-                dist2 = sep[0] * sep[0] + sep[1] * sep[1] + sep[2] * sep[2]
-                u = jnp.maximum(lax.rsqrt(dist2) - 1.0, 0.0)
-                dot = sep[0] * rel[0] + sep[1] * rel[1] + sep[2] * rel[2]
-                theta = th_ref[pl.ds(k * 256 + s * 32 + y, SLOTS, stride=ROWS), :]
-                if k == 0:
-                    theta = (theta + th_ref[pl.ds(s * ROWS + y, SLOTS, stride=32), :]) * HALF_ROOT
-                fr = u * ((theta + REST) - u * dot)
-                if k == 0:
-                    fr = jnp.where(slot > s, fr, 0.0)
-                for a in range(3):
-                    f = fr * sep[a]
-                    d[s][a] = f if d[s][a] is None else d[s][a] + f
-                    r[a] = f if r[a] is None else r[a] + f
-            ref = (ru_refs if dz else rl_refs)[dx]
-            at = (y + 1 + dy) * 3
+    for dy, dz in TILES:
+        k = tile_index(dx, dy, dz)
+        src = up_ref if dz else level_ref
+        base = (y + 1 + dy) * 6
+        oth = [src[base + c] for c in range(6)]
+        if not own_column:
+            step = dx.astype(jnp.float32)
+            if (dy, dz) == (0, 0):
+                step = jnp.where(dx == 1, step, -2.0 * FAR)
+            oth[0] = oth[0] + step
+        if dy:
+            oth[1] = oth[1] + float(dy)
+        self_tile = own_column and (dy, dz) == (0, 0)
+        r = [None] * 3
+        for s in range(SLOTS):
+            if self_tile and s == SLOTS - 1:
+                continue
+            own = [row_of(ownx_ref, y, s)] + [row_of(own_ref, (y + 1) * 6 + c, s) for c in range(1, 6)]
+            sep = [own[a] - oth[a] for a in range(3)]
+            rel = [own[3 + a] - oth[3 + a] for a in range(3)]
+            dist2 = sep[0] * sep[0] + sep[1] * sep[1] + sep[2] * sep[2]
+            u = jnp.maximum(lax.rsqrt(dist2) - 1.0, 0.0)
+            dot = sep[0] * rel[0] + sep[1] * rel[1] + sep[2] * rel[2]
+            theta = th_ref[pl.ds(k * 256 + s * 32 + y, SLOTS, stride=ROWS), :]
+            if self_tile:
+                theta = (theta + th_ref[pl.ds(s * ROWS + y, SLOTS, stride=32), :]) * HALF_ROOT
+            fr = u * ((theta + REST) - u * dot)
+            if self_tile:
+                fr = jnp.where(slot > s, fr, 0.0)
             for a in range(3):
-                ref[at + a] = ref[at + a] + r[a]
-            vir = [t - oth[a] * r[b] for t, (a, b) in zip(vir, PRODUCTS)]
+                f = fr * sep[a]
+                d[s][a] = f if d[s][a] is None else d[s][a] + f
+                r[a] = f if r[a] is None else r[a] + f
+        ref = ru_ref if dz else rl_ref
+        at = (y + 1 + dy) * 3
+        for a in range(3):
+            ref[at + a] = ref[at + a] + r[a]
+        vir = [t - oth[a] * r[b] for t, (a, b) in zip(vir, PRODUCTS)]
     for s in range(SLOTS):
         own = [row_of(ownx_ref, y, s)] + [row_of(own_ref, (y + 1) * 6 + c, s) for c in range(1, 3)]
         vir = [t + own[a] * d[s][b] for t, (a, b) in zip(vir, PRODUCTS)]
@@ -184,7 +186,7 @@
     @pl.loop(0, ROWS)
     def _(y):
         vir = [acc_ref[i] for i in range(6)]
-        d, vir = row_pairs(y, [(0, m_ref, up_ref)], m_ref, ownx_ref, th_ref, {0: rl_ref}, {0: ru_ref}, vir)
+        d, vir = row_pairs(y, 0, m_ref, up_ref, m_ref, ownx_ref, th_ref, rl_ref, ru_ref, vir)
         for i in range(6):
             acc_ref[i] = vir[i]
         for s in range(SLOTS):
@@ -201,33 +203,41 @@
     z_ref[...] = settle(rl_ref, ru_ref, r_ref)
 
 
-def side_columns_kernel(
-    sizes, here_ref, m_ref, ownx_ref, th_ref, xm_ref, xp_ref, d0_ref, z0_ref, acc0_ref,
-    d_ref, rm_ref, rp_ref, tally_ref,
-    um_ref, up_ref, rlm_ref, rum_ref, rlp_ref, rup_ref, acc_ref,
-):
-    next_plane(xm_ref, um_ref)
-    next_plane(xp_ref, up_ref)
+def side_column(dx, m_ref, ownx_ref, th_ref, x_ref, d_in_ref, acc_in_ref, d_ref, r_ref, acc_ref, up_ref, rl_ref, ru_ref):
+    next_plane(x_ref, up_ref)
     zero = jnp.zeros((18, SLOTS, LANES), jnp.float32)
-    for ref in (rlm_ref, rum_ref, rlp_ref, rup_ref):
-        ref[...] = zero
-    acc_ref[...] = acc0_ref[...]
+    rl_ref[...] = zero
+    ru_ref[...] = zero
+    acc_ref[...] = acc_in_ref[...]
 
     @pl.loop(0, ROWS)
     def _(y):
         vir = [acc_ref[i] for i in range(6)]
-        d, vir = row_pairs(
-            y, [(1, xp_ref, up_ref), (-1, xm_ref, um_ref)], m_ref, ownx_ref, th_ref,
-            {1: rlp_ref, -1: rlm_ref}, {1: rup_ref, -1: rum_ref}, vir,
-        )
+        d, vir = row_pairs(y, dx, x_ref, up_ref, m_ref, ownx_ref, th_ref, rl_ref, ru_ref, vir)
         for i in range(6):
             acc_ref[i] = vir[i]
         for s in range(SLOTS):
             for a in range(3):
                 at = (y * 3 + a, pl.ds(s, 1), slice(None))
-                d_ref[at] = d0_ref[at] + jnp.sum(d[s][a], axis=0, keepdims=True)
-
-    planes = [settle(rlm_ref, rum_ref, rm_ref), z0_ref[...], settle(rlp_ref, rup_ref, rp_ref)]
+                d_ref[at] = d_in_ref[at] + jnp.sum(d[s][a], axis=0, keepdims=True)
+
+    return settle(rl_ref, ru_ref, r_ref)
+
+
+def near_column_kernel(
+    here_ref, m_ref, ownx_ref, th_ref, x_ref, d0_ref, acc0_ref, d_ref, r_ref, z_ref, acc_ref, *scratch
+):
+    dx = 1 - 2 * (here_ref[0] % 2)
+    z_ref[...] = side_column(dx, m_ref, ownx_ref, th_ref, x_ref, d0_ref, acc0_ref, d_ref, r_ref, acc_ref, *scratch)
+
+
+def far_column_kernel(
+    sizes, here_ref, m_ref, ownx_ref, th_ref, x_ref, d0_ref, acc0_ref, z0_ref, z1_ref,
+    d_ref, r_ref, tally_ref, acc_ref, *scratch,
+):
+    dx = 2 * (here_ref[0] % 2) - 1
+    z = side_column(dx, m_ref, ownx_ref, th_ref, x_ref, d0_ref, acc0_ref, d_ref, r_ref, acc_ref, *scratch)
+    planes = [(0, z0_ref[...]), (-dx, z1_ref[...]), (dx, z)]
     acc = [acc_ref[i] for i in range(13)]
     sums = [NOISE_SCALE * acc[i] + acc[6 + i] * (1.0 / (DRAG * DRAG)) for i in range(6)]
     lines = [sums[PRODUCTS.index((min(a, b), max(a, b)))] for a in range(3) for b in range(3)]
@@ -239,9 +249,9 @@
     held = jnp.where(lane == line, jnp.sum(held, axis=1, keepdims=True), 0.0)
     tally = jnp.sum(held, axis=0, keepdims=True)
     tally_ref[...] = jnp.broadcast_to(tally, tally_ref.shape)
-    at = (here_ref[0] // (sizes[1] * sizes[2]), here_ref[0] // sizes[2] % sizes[1], here_ref[0] % sizes[2])
-    for dx, z in zip((-1, 0, 1), planes):
-        send_past(z, sizes, at, dx, tally, tally_ref)
+    at = [here_ref[i] for i in range(3)]
+    for step, z in planes:
+        send_past(z, sizes, at, step, tally, tally_ref)
 
 
 def finish_kernel(cells, d_ref, s_ref, ym_ref, yp_ref, tallies_ref, f_ref, stress_ref, level_ref):
@@ -321,7 +331,7 @@
     occ = occupancy.reshape(ROWS, LANES)
     tile = (SLOTS, LANES)
     lines = 14 * SLOTS * SLOTS * ROWS
-    theta = call(convert_kernel, f32(lines, LANES), source=pltpu.VMEM)(noise.reshape(lines, LANES))
+    theta, ready = call(convert_kernel, (f32(lines, LANES), f32(*tile)), source=pltpu.VMEM)(noise.reshape(lines, LANES))
     v, ownx, z = call(
         pack_kernel,
         (f32(24, *tile), f32(ROWS, *tile), f32(*tile)),
@@ -331,9 +341,9 @@
     zr = shifted(z, "gz", -1)
     low, high = (jnp.concatenate([part, zr[None]]) for part in (v[0:6], v[18:24]))
     from_ym, from_yp = both_sides(low, high, "gy")
-    m = call(widen_kernel, f32(37, *tile))(v, zr, from_ym, from_yp)
-    from_xm = shifted(m, "gx", 1)
-    from_xp = shifted(m, "gx", -1)
+    m = call(widen_kernel, f32(37, *tile))(v, zr, from_ym, from_yp, ready)
+    far = swapped(m, "gx", 1)
+    near = swapped(m, "gx", 0)
     d0, r0, z0, acc0 = call(
         own_column_kernel,
         (f32(12, *tile), f32(18, *tile), f32(*tile), f32(16, *tile)),
@@ -341,14 +351,21 @@
     )(m, ownx, theta)
     sizes = tuple(lax.axis_size(axis) for axis in AXES)
     devices = sizes[0] * sizes[1] * sizes[2]
-    here = jnp.reshape(lax.axis_index(AXES).astype(jnp.int32), (1,))
-    d, rm, rp, tally = call(
-        functools.partial(side_columns_kernel, sizes),
-        (f32(12, *tile), f32(18, *tile), f32(18, *tile), f32(devices, LANES)),
-        [vmem(36, *tile)] * 2 + [vmem(18, *tile)] * 4 + [vmem(16, *tile)],
+    here = jnp.stack([lax.axis_index(axis).astype(jnp.int32) for axis in AXES])
+    scratch = [vmem(36, *tile), vmem(18, *tile), vmem(18, *tile)]
+    d1, r1, z1, acc1 = call(
+        near_column_kernel,
+        (f32(12, *tile), f32(18, *tile), f32(*tile), f32(16, *tile)),
+        scratch,
         scalars=1,
-    )(here, m, ownx, theta, from_xm, from_xp, d0, z0, acc0)
-    s = r0 + shifted(rp, "gx", 1) + shifted(rm, "gx", -1)
+    )(here, m, ownx, theta, near, d0, acc0)
+    d, r2, tally = call(
+        functools.partial(far_column_kernel, sizes),
+        (f32(12, *tile), f32(18, *tile), f32(devices, LANES)),
+        [vmem(16, *tile), *scratch],
+        scalars=1,
+    )(here, m, ownx, theta, far, d1, acc1, z0, z1)
+    s = r0 + swapped(r2, "gx", 1) + swapped(r1, "gx", 0)
     back_ym, back_yp = both_sides(s[0:3], s[15:18], "gy")
     tallies = lax.all_to_all(tally, AXES, 0, 0, tiled=True)
     force, stress, level = call(

time: 49.8 us -> 48.9 us (0.982)
  starting transfers between devices: 28.6 us -> 25.9 us
  Pallas kernels: 5.85 us -> 7.38 us
    ppermute x4 -> x8, starting transfers between devices: 6.43 us -> 13.1 us  [swapped(): return lax.ppermute(shard, axis, pairs + [(j, i) for i, j in pairs])]
    ppermute x5 -> x1, starting transfers between devices: 12.1 us -> 6.47 us  [shifted(): lax.ppermute(shard, axis, [(i, (i + by) % count) for i in range(count)])]
    all_to_all x1, starting transfers between devices: 10.1 us -> 6.26 us  [per_device(): tallies = lax.all_to_all(tally, AXES, 0, 0, tiled=True)]
    pallas_call x6 -> x7, Pallas kernels: 5.85 us -> 7.38 us  [run(): pl.pallas_call(kernel, out_shape=out_shape, in_specs=specs, out_specs=jax...]
    ppermute x4 -> x8, waiting for transfers between devices: 4.29 us -> 5.22 us  [swapped(): return lax.ppermute(shard, axis, pairs + [(j, i) for i, j in pairs])]
    ppermute x5 -> x1, waiting for transfers between devices: 1.37 us -> 0.75 us  [shifted(): lax.ppermute(shard, axis, [(i, (i + by) % count) for i in range(count)])]
  transfers between devices with their start and end apart: 10 -> 10, of which waited for: 5 -> 6; matrix products, arithmetic and copies ran while one was open for 0% -> 0% of each run, Pallas kernels for 3% -> 6%
where the time goes in v4:
time: 48.9 us; the launch traced here: 48.6 us
  starting transfers between devices  25.9 us (53%)
  waiting for transfers between devices  13.4 us (27%)
  Pallas kernels  7.38 us (15%)
  local copies, waits for them, and re-layouts  1.18 us (2%)
  between operations  0.73 us (1%)
    ppermute x8, starting transfers between devices, swapped(): return lax.ppermute(shard, axis, pairs + [(j, i) for i, j in pairs])  13.1 us
    all_to_all x1, waiting for transfers between devices, per_device(): tallies = lax.all_to_all(tally, AXES, 0, 0, tiled=True)  7.42 us
    pallas_call x7, Pallas kernels, run(): pl.pallas_call(kernel, out_shape=out_shape, in_specs=specs, out_specs=jax...  7.38 us
    ppermute x1, starting transfers between devices, shifted(): lax.ppermute(shard, axis, [(i, (i + by) % count) for i in range(count)])  6.47 us
    all_to_all x1, starting transfers between devices, per_device(): tallies = lax.all_to_all(tally, AXES, 0, 0, tiled=True)  6.26 us
    ppermute x8, waiting for transfers between devices, swapped(): return lax.ppermute(shard, axis, pairs + [(j, i) for i, j in pairs])  5.22 us
    unnamed x2, local copies, waits for them, and re-layouts  1.18 us
  transfers between devices with their start and end apart: 10, of which 6 were waited for; matrix products, arithmetic and copies ran while one was open for 0% of the time, Pallas kernels for 6%

profile of v4, /device:TPU:1, one launch (start us, length us, event | category | flops | bytes accessed | tf_op | source)
XLA Modules:
  0.0 48.6 jit_solution(7670202540332574521)
XLA Ops:
  0.6 0.9 %shard_map.67 = (f32[24,8,128]{2,1,0:T(8,128)S(1)}, f32[4,8,128]{2,1,0:T(8,128)S(1)}, f32[8,128]{1,0:T(8,128)S(1)}) custom-call(f32[3,32,128]{2,1,0:T(8,128)} %bitcast.19, f32[3,32,128]{2,1,0:T(8,128)} %bitcast.20, s32[4,128]{1,0:T(4,128)} %bitcast.21), custom_call_target="tpu_custom_call" | custom-call | tf_op jit(solution)/shard_map/pallas_call | solution.py:298
  1.6 6.5 %collective-permute-start = (f32[8,128]{1,0:T(8,128)S(1)}, f32[8,128]{1,0:T(8,128)S(1)}, u32[]{:S(2)}, u32[]{:S(2)}) collective-permute-start(f32[8,128]{1,0:T(8,128)S(1)} %get-tuple-element.23), channel_id=1, source_target_pairs={{0,7},{1,0},{2,1},{3,2},{4,3},{5,4},{6,5},{7,6},{8,15},{9,8},{10,9... | collective-permute-start | bytes 12296 | tf_op jit(solution)/shard_map/ppermute | solution.py:325
  8.1 0.8 %collective-permute-done.zr_ref = f32[8,128]{1,0:T(8,128)S(1)} collective-permute-done((f32[8,128]{1,0:T(8,128)S(1)}, f32[8,128]{1,0:T(8,128)S(1)}, u32[]{:S(2)}, u32[]{:S(2)}) %collective-permute-start) | collective-permute-done | bytes 4128 | tf_op jit(solution)/shard_map/ppermute | solution.py:325
  8.8 2.7 %collective-permute-start.1 = (f32[7,8,128]{2,1,0:T(8,128)S(1)}, f32[7,8,128]{2,1,0:T(8,128)S(1)}, u32[]{:S(2)}, u32[]{:S(2)}) collective-permute-start(f32[7,8,128]{2,1,0:T(8,128)S(1)} %get-tuple-element.54), channel_id=1, source_target_pairs={{8,16},{24,0},{16,8},{0,24},{9,17},{25,1},{17,9},{1,25},{10,18},{2... | collective-permute-start | bytes 86024 | tf_op jit(solution)/shard_map/ppermute | solution.py:313
  11.6 0.0 collective-permute-start.2
  11.6 0.0 copy-start
  11.6 1.2 %copy-done = bf16[14,8,8,1,4,128]{5,4,3,2,1,0:T(4,128)(2,1)S(1)} copy-done((bf16[14,8,8,1,4,128]{5,4,3,2,1,0:T(4,128)(2,1)S(1)}, bf16[14,8,8,1,4,128]{5,4,3,2,1,0:T(4,128)(2,1)}, u32[]{:S(2)}) %copy-start) | copy-done | bytes 917528
  12.7 0.2 shard_map.68
  12.9 0.0 collective-permute-done.1
  12.9 1.6 %collective-permute-done.2 = f32[7,8,128]{2,1,0:T(8,128)S(1)} collective-permute-done((f32[7,8,128]{2,1,0:T(8,128)S(1)}, f32[7,8,128]{2,1,0:T(8,128)S(1)}, u32[]{:S(2)}, u32[]{:S(2)}) %collective-permute-start.2) | collective-permute-done | bytes 28704 | tf_op jit(solution)/shard_map/ppermute | solution.py:313
  14.6 0.1 shard_map.69.m_ref
  14.7 2.7 %collective-permute-start.4 = (f32[37,8,128]{2,1,0:T(8,128)S(1)}, f32[37,8,128]{2,1,0:T(8,128)S(1)}, u32[]{:S(2)}, u32[]{:S(2)}) collective-permute-start(f32[37,8,128]{2,1,0:T(8,128)S(1)} %shard_map.69.m_ref), channel_id=1, source_target_pairs={{0,32},{64,96},{128,160},{192,224},{32,0},{96,64},{160,128},{224,1... | collective-permute-start | bytes 454664 | tf_op jit(solution)/shard_map/ppermute | solution.py:313
  17.3 1.2 %collective-permute-start.3 = (f32[37,8,128]{2,1,0:T(8,128)S(1)}, f32[37,8,128]{2,1,0:T(8,128)S(1)}, u32[]{:S(2)}, u32[]{:S(2)}) collective-permute-start(f32[37,8,128]{2,1,0:T(8,128)S(1)} %shard_map.69.m_ref), channel_id=1, source_target_pairs={{32,64},{96,128},{160,192},{224,0},{64,32},{128,96},{192,160},{0,2... | collective-permute-start | bytes 454664 | tf_op jit(solution)/shard_map/ppermute | solution.py:313
  18.5 0.1 pad_add_fusion.here_ref
  18.6 1.2 %shard_map.70 = (f32[12,8,128]{2,1,0:T(8,128)S(1)}, f32[18,8,128]{2,1,0:T(8,128)S(1)}, f32[8,128]{1,0:T(8,128)S(1)}, f32[16,8,128]{2,1,0:T(8,128)S(1)}) custom-call(f32[37,8,128]{2,1,0:T(8,128)S(1)} %shard_map.69.m_ref, f32[4,8,128]{2,1,0:T(8,128)S(1)} %get-tuple-element.25.ownx_ref, f32[3584,128]{1,0:T(8,128)S(1)} %get-tuple-element.26.th_ref), custom_call_target="tpu_custom_call" | custom-call | tf_op jit(solution)/shard_map/pallas_call | solution.py:298
  19.8 0.0 collective-permute-done.4.x_ref
  19.8 1.7 %shard_map.71 = (f32[12,8,128]{2,1,0:T(8,128)S(1)}, f32[18,8,128]{2,1,0:T(8,128)S(1)}, f32[8,128]{1,0:T(8,128)S(1)}, f32[16,8,128]{2,1,0:T(8,128)S(1)}) custom-call(s32[3]{0:T(128)S(1)} %pad_add_fusion.here_ref, f32[37,8,128]{2,1,0:T(8,128)S(1)} %shard_map.69.m_ref, f32[4,8,128]{2,1,0:T(8,128)S(1)} %get-tuple-element.25.ownx_ref, ...), custom_call_target="tpu_custom_call" | custom-call | tf_op jit(solution)/shard_map/pallas_call | solution.py:298
  21.5 0.7 %collective-permute-done.3.x_ref = f32[37,8,128]{2,1,0:T(8,128)S(1)} collective-permute-done((f32[37,8,128]{2,1,0:T(8,128)S(1)}, f32[37,8,128]{2,1,0:T(8,128)S(1)}, u32[]{:S(2)}, u32[]{:S(2)}) %collective-permute-start.3) | collective-permute-done | bytes 151584 | tf_op jit(solution)/shard_map/ppermute | solution.py:313
  22.3 2.5 %shard_map.72 = (f32[12,8,128]{2,1,0:T(8,128)S(1)}, f32[18,8,128]{2,1,0:T(8,128)S(1)}, f32[256,128]{1,0:T(8,128)}) custom-call(s32[3]{0:T(128)S(1)} %pad_add_fusion.here_ref, f32[37,8,128]{2,1,0:T(8,128)S(1)} %shard_map.69.m_ref, f32[4,8,128]{2,1,0:T(8,128)S(1)} %get-tuple-element.25.ownx_ref, f32[3584,128]{1,0:T(8,128)S(1)} %get-tuple-element.26.th_ref, ...), custom_call_target="tpu_custom_call" | custom-call | tf_op jit(solution)/shard_map/pallas_call | solution.py:298
  24.7 0.9 %collective-permute-start.5 = (f32[18,8,128]{2,1,0:T(8,128)S(1)}, f32[18,8,128]{2,1,0:T(8,128)S(1)}, u32[]{:S(2)}, u32[]{:S(2)}) collective-permute-start(f32[18,8,128]{2,1,0:T(8,128)S(1)} %get-tuple-element.35), channel_id=1, source_target_pairs={{32,64},{96,128},{160,192},{224,0},{64,32},{128,96},{192,160},{0,2... | collective-permute-start | bytes 221192 | tf_op jit(solution)/shard_map/ppermute | solution.py:313
  25.6 2.9 %collective-permute-start.6 = (f32[18,8,128]{2,1,0:T(8,128)S(1)}, f32[18,8,128]{2,1,0:T(8,128)S(1)}, u32[]{:S(2)}, u32[]{:S(2)}) collective-permute-start(f32[18,8,128]{2,1,0:T(8,128)S(1)} %get-tuple-element.36), channel_id=1, source_target_pairs={{0,32},{64,96},{128,160},{192,224},{32,0},{96,64},{160,128},{224,1... | collective-permute-start | bytes 221192 | tf_op jit(solution)/shard_map/ppermute | solution.py:313
  28.5 6.3 %all-to-all-start = ((f32[256,1,128]{2,1,0:T(1,128)}), f32[256,1,128]{2,1,0:T(1,128)S(1)}, u32[]{:S(2)}, u32[]{:S(2)}) async-start(f32[256,1,128]{2,1,0:T(1,128)} %bitcast.9), calls=%async_computation | async-start | bytes 262144 | tf_op jit(solution)/shard_map/all_to_all | solution.py:370
  34.8 0.0 collective-permute-done.5
  34.8 0.0 collective-permute-done.6
  34.8 2.7 %collective-permute-start.7 = (f32[3,8,128]{2,1,0:T(8,128)S(1)}, f32[3,8,128]{2,1,0:T(8,128)S(1)}, u32[]{:S(2)}, u32[]{:S(2)}) collective-permute-start(f32[3,8,128]{2,1,0:T(8,128)S(1)} %get-tuple-element.50), channel_id=1, source_target_pairs={{8,16},{24,0},{16,8},{0,24},{9,17},{25,1},{17,9},{1,25},{10,18},{2... | collective-permute-start | bytes 36872 | tf_op jit(solution)/shard_map/ppermute | solution.py:313
  37.5 0.0 collective-permute-start.8
  37.5 1.4 %collective-permute-done.7 = f32[3,8,128]{2,1,0:T(8,128)S(1)} collective-permute-done((f32[3,8,128]{2,1,0:T(8,128)S(1)}, f32[3,8,128]{2,1,0:T(8,128)S(1)}, u32[]{:S(2)}, u32[]{:S(2)}) %collective-permute-start.7) | collective-permute-done | bytes 12320 | tf_op jit(solution)/shard_map/ppermute | solution.py:313
  39.0 1.4 %collective-permute-done.8 = f32[3,8,128]{2,1,0:T(8,128)S(1)} collective-permute-done((f32[3,8,128]{2,1,0:T(8,128)S(1)}, f32[3,8,128]{2,1,0:T(8,128)S(1)}, u32[]{:S(2)}, u32[]{:S(2)}) %collective-permute-start.8) | collective-permute-done | bytes 12320 | tf_op jit(solution)/shard_map/ppermute | solution.py:313
  40.4 7.4 %all-to-all-done = f32[256,1,128]{2,1,0:T(1,128)S(1)} async-done(((f32[256,1,128]{2,1,0:T(1,128)}), f32[256,1,128]{2,1,0:T(1,128)S(1)}, u32[]{:S(2)}, u32[]{:S(2)}) %all-to-all-start) | async-done | bytes 131104 | tf_op jit(solution)/shard_map/all_to_all | solution.py:370
  47.8 0.8 %shard_map.73 = (f32[3,32,128]{2,1,0:T(8,128)}, f32[3,3]{1,0:T(4,128)}, f32[1,1]{1,0:T(1,128)}) custom-call(f32[12,8,128]{2,1,0:T(8,128)S(1)} %get-tuple-element.33.d_ref, f32[18,8,128]{2,1,0:T(8,128)S(1)} %add_add_fusion.s_ref, f32[3,8,128]{2,1,0:T(8,128)S(1)} %get-tuple-element.56.ym_ref, f32[3,8,128]{2,1,0:T(8,128)S(1)} %get-tuple-element.55.yp_ref, ...), custom_call_target="tpu_custom_call" | custom-call | tf_op jit(solution)/shard_map/pallas_call | solution.py:298
  (6 shorter events, 0.0 us)
Async XLA Ops:
  1.6 7.2 %collective-permute-start = (f32[8,128]{1,0:T(8,128)S(1)}, f32[8,128]{1,0:T(8,128)S(1)}, u32[]{:S(2)}, u32[]{:S(2)}) collective-permute-start(f32[8,128]{1,0:T(8,128)S(1)} %get-tuple-element.23), channel_id=1, source_target_pairs={{0,7},{1,0},{2,1},{3,2},{4,3},{5,4},{6,5},{7,6},{8,15},{9,8},{10,9... | collective-permute-start | bytes 12296 | tf_op jit(solution)/shard_map/ppermute | solution.py:325
  8.8 4.1 %collective-permute-start.1 = (f32[7,8,128]{2,1,0:T(8,128)S(1)}, f32[7,8,128]{2,1,0:T(8,128)S(1)}, u32[]{:S(2)}, u32[]{:S(2)}) collective-permute-start(f32[7,8,128]{2,1,0:T(8,128)S(1)} %get-tuple-element.54), channel_id=1, source_target_pairs={{8,16},{24,0},{16,8},{0,24},{9,17},{25,1},{17,9},{1,25},{10,18},{2... | collective-permute-start | bytes 86024 | tf_op jit(solution)/shard_map/ppermute | solution.py:313
  11.6 3.0 %collective-permute-start.2 = (f32[7,8,128]{2,1,0:T(8,128)S(1)}, f32[7,8,128]{2,1,0:T(8,128)S(1)}, u32[]{:S(2)}, u32[]{:S(2)}) collective-permute-start(f32[7,8,128]{2,1,0:T(8,128)S(1)} %get-tuple-element.53), channel_id=1, source_target_pairs={{0,8},{16,24},{8,0},{24,16},{1,9},{17,25},{9,1},{25,17},{2,10},{18... | collective-permute-start | bytes 86024 | tf_op jit(solution)/shard_map/ppermute | solution.py:313
  11.6 1.2 %copy-start = (bf16[14,8,8,1,4,128]{5,4,3,2,1,0:T(4,128)(2,1)S(1)}, bf16[14,8,8,1,4,128]{5,4,3,2,1,0:T(4,128)(2,1)}, u32[]{:S(2)}) copy-start(bf16[14,8,8,1,4,128]{5,4,3,2,1,0:T(4,128)(2,1)} %param.7) | copy-start | bytes 2752516
  14.7 5.2 %collective-permute-start.4 = (f32[37,8,128]{2,1,0:T(8,128)S(1)}, f32[37,8,128]{2,1,0:T(8,128)S(1)}, u32[]{:S(2)}, u32[]{:S(2)}) collective-permute-start(f32[37,8,128]{2,1,0:T(8,128)S(1)} %shard_map.69.m_ref), channel_id=1, source_target_pairs={{0,32},{64,96},{128,160},{192,224},{32,0},{96,64},{160,128},{224,1... | collective-permute-start | bytes 454664 | tf_op jit(solution)/shard_map/ppermute | solution.py:313
  17.3 4.9 %collective-permute-start.3 = (f32[37,8,128]{2,1,0:T(8,128)S(1)}, f32[37,8,128]{2,1,0:T(8,128)S(1)}, u32[]{:S(2)}, u32[]{:S(2)}) collective-permute-start(f32[37,8,128]{2,1,0:T(8,128)S(1)} %shard_map.69.m_ref), channel_id=1, source_target_pairs={{32,64},{96,128},{160,192},{224,0},{64,32},{128,96},{192,160},{0,2... | collective-permute-start | bytes 454664 | tf_op jit(solution)/shard_map/ppermute | solution.py:313
  24.7 10.1 %collective-permute-start.5 = (f32[18,8,128]{2,1,0:T(8,128)S(1)}, f32[18,8,128]{2,1,0:T(8,128)S(1)}, u32[]{:S(2)}, u32[]{:S(2)}) collective-permute-start(f32[18,8,128]{2,1,0:T(8,128)S(1)} %get-tuple-element.35), channel_id=1, source_target_pairs={{32,64},{96,128},{160,192},{224,0},{64,32},{128,96},{192,160},{0,2... | collective-permute-start | bytes 221192 | tf_op jit(solution)/shard_map/ppermute | solution.py:313
  25.6 9.2 %collective-permute-start.6 = (f32[18,8,128]{2,1,0:T(8,128)S(1)}, f32[18,8,128]{2,1,0:T(8,128)S(1)}, u32[]{:S(2)}, u32[]{:S(2)}) collective-permute-start(f32[18,8,128]{2,1,0:T(8,128)S(1)} %get-tuple-element.36), channel_id=1, source_target_pairs={{0,32},{64,96},{128,160},{192,224},{32,0},{96,64},{160,128},{224,1... | collective-permute-start | bytes 221192 | tf_op jit(solution)/shard_map/ppermute | solution.py:313
  28.5 19.3 %all-to-all-start = ((f32[256,1,128]{2,1,0:T(1,128)}), f32[256,1,128]{2,1,0:T(1,128)S(1)}, u32[]{:S(2)}, u32[]{:S(2)}) async-start(f32[256,1,128]{2,1,0:T(1,128)} %bitcast.9), calls=%async_computation | async-start | bytes 262144 | tf_op jit(solution)/shard_map/all_to_all | solution.py:370
  34.8 4.2 %collective-permute-start.7 = (f32[3,8,128]{2,1,0:T(8,128)S(1)}, f32[3,8,128]{2,1,0:T(8,128)S(1)}, u32[]{:S(2)}, u32[]{:S(2)}) collective-permute-start(f32[3,8,128]{2,1,0:T(8,128)S(1)} %get-tuple-element.50), channel_id=1, source_target_pairs={{8,16},{24,0},{16,8},{0,24},{9,17},{25,1},{17,9},{1,25},{10,18},{2... | collective-permute-start | bytes 36872 | tf_op jit(solution)/shard_map/ppermute | solution.py:313
  37.5 2.9 %collective-permute-start.8 = (f32[3,8,128]{2,1,0:T(8,128)S(1)}, f32[3,8,128]{2,1,0:T(8,128)S(1)}, u32[]{:S(2)}, u32[]{:S(2)}) collective-permute-start(f32[3,8,128]{2,1,0:T(8,128)S(1)} %get-tuple-element.49), channel_id=1, source_target_pairs={{0,8},{16,24},{8,0},{24,16},{1,9},{17,25},{9,1},{25,17},{2,10},{18... | collective-permute-start | bytes 36872 | tf_op jit(solution)/shard_map/ppermute | solution.py:313

commit v5 on v4

--- a/solution.py
+++ b/solution.py
@@ -105,20 +105,17 @@
             up_ref[at] = val
 
 
-def row_pairs(y, dx, level_ref, up_ref, own_ref, ownx_ref, th_ref, rl_ref, ru_ref, vir):
+def row_pairs(y, dx, tiles, level_ref, up_ref, own_ref, ownx_ref, th_ref, rl_ref, ru_ref, vir):
     slot = slot_iota()
     own_column = isinstance(dx, int)
     d = [[None] * 3 for _ in range(SLOTS)]
-    for dy, dz in TILES:
+    for dy, dz in tiles:
         k = tile_index(dx, dy, dz)
         src = up_ref if dz else level_ref
         base = (y + 1 + dy) * 6
         oth = [src[base + c] for c in range(6)]
         if not own_column:
-            step = dx.astype(jnp.float32)
-            if (dy, dz) == (0, 0):
-                step = jnp.where(dx == 1, step, -2.0 * FAR)
-            oth[0] = oth[0] + step
+            oth[0] = oth[0] + dx.astype(jnp.float32)
         if dy:
             oth[1] = oth[1] + float(dy)
         self_tile = own_column and (dy, dz) == (0, 0)
@@ -186,7 +183,7 @@
     @pl.loop(0, ROWS)
     def _(y):
         vir = [acc_ref[i] for i in range(6)]
-        d, vir = row_pairs(y, 0, m_ref, up_ref, m_ref, ownx_ref, th_ref, rl_ref, ru_ref, vir)
+        d, vir = row_pairs(y, 0, TILES, m_ref, up_ref, m_ref, ownx_ref, th_ref, rl_ref, ru_ref, vir)
         for i in range(6):
             acc_ref[i] = vir[i]
         for s in range(SLOTS):
@@ -210,32 +207,39 @@
     ru_ref[...] = zero
     acc_ref[...] = acc_in_ref[...]
 
-    @pl.loop(0, ROWS)
-    def _(y):
-        vir = [acc_ref[i] for i in range(6)]
-        d, vir = row_pairs(y, dx, x_ref, up_ref, m_ref, ownx_ref, th_ref, rl_ref, ru_ref, vir)
-        for i in range(6):
-            acc_ref[i] = vir[i]
-        for s in range(SLOTS):
-            for a in range(3):
-                at = (y * 3 + a, pl.ds(s, 1), slice(None))
-                d_ref[at] = d_in_ref[at] + jnp.sum(d[s][a], axis=0, keepdims=True)
+    def pairs(tiles, from_ref):
+        @pl.loop(0, ROWS)
+        def _(y):
+            vir = [acc_ref[i] for i in range(6)]
+            d, vir = row_pairs(y, dx, tiles, x_ref, up_ref, m_ref, ownx_ref, th_ref, rl_ref, ru_ref, vir)
+            for i in range(6):
+                acc_ref[i] = vir[i]
+            for s in range(SLOTS):
+                for a in range(3):
+                    at = (y * 3 + a, pl.ds(s, 1), slice(None))
+                    d_ref[at] = from_ref[at] + jnp.sum(d[s][a], axis=0, keepdims=True)
+
+    pairs(TILES[1:], d_in_ref)
+
+    @pl.when(dx == 1)
+    def _():
+        pairs(TILES[:1], d_ref)
 
     return settle(rl_ref, ru_ref, r_ref)
 
 
 def near_column_kernel(
-    here_ref, m_ref, ownx_ref, th_ref, x_ref, d0_ref, acc0_ref, d_ref, r_ref, z_ref, acc_ref, *scratch
+    m_ref, ownx_ref, th_ref, x_ref, d0_ref, acc0_ref, d_ref, r_ref, z_ref, acc_ref, *scratch
 ):
-    dx = 1 - 2 * (here_ref[0] % 2)
+    dx = 1 - 2 * (lax.axis_index("gx") % 2)
     z_ref[...] = side_column(dx, m_ref, ownx_ref, th_ref, x_ref, d0_ref, acc0_ref, d_ref, r_ref, acc_ref, *scratch)
 
 
 def far_column_kernel(
-    sizes, here_ref, m_ref, ownx_ref, th_ref, x_ref, d0_ref, acc0_ref, z0_ref, z1_ref,
+    sizes, m_ref, ownx_ref, th_ref, x_ref, d0_ref, acc0_ref, z0_ref, z1_ref,
     d_ref, r_ref, tally_ref, acc_ref, *scratch,
 ):
-    dx = 2 * (here_ref[0] % 2) - 1
+    dx = 2 * (lax.axis_index("gx") % 2) - 1
     z = side_column(dx, m_ref, ownx_ref, th_ref, x_ref, d0_ref, acc0_ref, d_ref, r_ref, acc_ref, *scratch)
     planes = [(0, z0_ref[...]), (-dx, z1_ref[...]), (dx, z)]
     acc = [acc_ref[i] for i in range(13)]
@@ -249,7 +253,7 @@
     held = jnp.where(lane == line, jnp.sum(held, axis=1, keepdims=True), 0.0)
     tally = jnp.sum(held, axis=0, keepdims=True)
     tally_ref[...] = jnp.broadcast_to(tally, tally_ref.shape)
-    at = [here_ref[i] for i in range(3)]
+    at = [lax.axis_index(axis) for axis in AXES]
     for step, z in planes:
         send_past(z, sizes, at, step, tally, tally_ref)
 
@@ -286,19 +290,16 @@
     return pltpu.VMEM(shape, jnp.float32)
 
 
-def call(kernel, out_shape, scratch=(), source=None, scalars=0):
+def call(kernel, out_shape, scratch=(), source=None):
     space = pl.BlockSpec(memory_space=pltpu.VMEM)
 
     def run(*args):
-        specs = [pl.BlockSpec(memory_space=source or pltpu.VMEM) for _ in args]
-        specs[:scalars] = [pl.BlockSpec(memory_space=pltpu.SMEM)] * scalars
         if source is not pltpu.VMEM:
-            held = [pltpu.with_memory_space_constraint(a, source or pltpu.VMEM) for a in args[scalars:]]
-            args = (*args[:scalars], *held)
+            args = [pltpu.with_memory_space_constraint(a, source or pltpu.VMEM) for a in args]
         return pl.pallas_call(
             kernel,
             out_shape=out_shape,
-            in_specs=specs,
+            in_specs=[pl.BlockSpec(memory_space=source or pltpu.VMEM) for _ in args],
             out_specs=jax.tree.map(lambda _: space, out_shape),
             scratch_shapes=list(scratch),
             compiler_params=pltpu.CompilerParams(vmem_limit_bytes=16 << 20),
@@ -351,20 +352,17 @@
     )(m, ownx, theta)
     sizes = tuple(lax.axis_size(axis) for axis in AXES)
     devices = sizes[0] * sizes[1] * sizes[2]
-    here = jnp.stack([lax.axis_index(axis).astype(jnp.int32) for axis in AXES])
     scratch = [vmem(36, *tile), vmem(18, *tile), vmem(18, *tile)]
     d1, r1, z1, acc1 = call(
         near_column_kernel,
         (f32(12, *tile), f32(18, *tile), f32(*tile), f32(16, *tile)),
         scratch,
-        scalars=1,
-    )(here, m, ownx, theta, near, d0, acc0)
+    )(m, ownx, theta, near, d0, acc0)
     d, r2, tally = call(
         functools.partial(far_column_kernel, sizes),
         (f32(12, *tile), f32(18, *tile), f32(devices, LANES)),
         [vmem(16, *tile), *scratch],
-        scalars=1,
-    )(here, m, ownx, theta, far, d1, acc1, z0, z1)
+    )(m, ownx, theta, far, d1, acc1, z0, z1)
     s = r0 + swapped(r2, "gx", 1) + swapped(r1, "gx", 0)
     back_ym, back_yp = both_sides(s[0:3], s[15:18], "gy")
     tallies = lax.all_to_all(tally, AXES, 0, 0, tiled=True)

time: 48.9 us -> 48.5 us (level)
  Pallas kernels: 7.38 us -> 6.34 us
  waiting for transfers between devices: 13.4 us -> 14.1 us
    pallas_call x7, Pallas kernels: 7.38 us -> 6.34 us  [run(): pl.pallas_call(kernel, out_shape=out_shape, in_specs=[pl.BlockSpec(memory...]
    ppermute x8, waiting for transfers between devices: 5.22 us -> 5.97 us  [swapped(): return lax.ppermute(shard, axis, pairs + [(j, i) for i, j in pairs])]
  transfers between devices with their start and end apart: 10 -> 10, of which waited for: 6 -> 6; matrix products, arithmetic and copies ran while one was open for 0% -> 0% of each run, Pallas kernels for 6% -> 5%
where the time goes in v5:
time: 48.5 us; the launch traced here: 48.3 us
  starting transfers between devices  25.9 us (53%)
  waiting for transfers between devices  14.1 us (29%)
  Pallas kernels  6.34 us (13%)
  local copies, waits for them, and re-layouts  1.18 us (2%)
  between operations  0.72 us (1%)
    ppermute x8, starting transfers between devices, swapped(): return lax.ppermute(shard, axis, pairs + [(j, i) for i, j in pairs])  13.1 us
    all_to_all x1, waiting for transfers between devices, per_device(): tallies = lax.all_to_all(tally, AXES, 0, 0, tiled=True)  7.42 us
    ppermute x1, starting transfers between devices, shifted(): lax.ppermute(shard, axis, [(i, (i + by) % count) for i in range(count)])  6.47 us
    pallas_call x7, Pallas kernels, run(): pl.pallas_call(kernel, out_shape=out_shape, in_specs=[pl.BlockSpec(memory...  6.34 us
    all_to_all x1, starting transfers between devices, per_device(): tallies = lax.all_to_all(tally, AXES, 0, 0, tiled=True)  6.26 us
    ppermute x8, waiting for transfers between devices, swapped(): return lax.ppermute(shard, axis, pairs + [(j, i) for i, j in pairs])  5.97 us
    unnamed x2, local copies, waits for them, and re-layouts  1.18 us
  transfers between devices with their start and end apart: 10, of which 6 were waited for; matrix products, arithmetic and copies ran while one was open for 0% of the time, Pallas kernels for 5%

profile of v5, /device:TPU:1, one launch (start us, length us, event | category | flops | bytes accessed | tf_op | source)
XLA Modules:
  0.0 48.3 jit_solution(9364877077883464040)
XLA Ops:
  0.6 0.9 %shard_map.67 = (f32[24,8,128]{2,1,0:T(8,128)S(1)}, f32[4,8,128]{2,1,0:T(8,128)S(1)}, f32[8,128]{1,0:T(8,128)S(1)}) custom-call(f32[3,32,128]{2,1,0:T(8,128)} %bitcast.16, f32[3,32,128]{2,1,0:T(8,128)} %bitcast.17, s32[4,128]{1,0:T(4,128)} %bitcast.18), custom_call_target="tpu_custom_call" | custom-call | tf_op jit(solution)/shard_map/pallas_call | solution.py:299
  1.6 6.5 %collective-permute-start = (f32[8,128]{1,0:T(8,128)S(1)}, f32[8,128]{1,0:T(8,128)S(1)}, u32[]{:S(2)}, u32[]{:S(2)}) collective-permute-start(f32[8,128]{1,0:T(8,128)S(1)} %get-tuple-element.23), channel_id=1, source_target_pairs={{0,7},{1,0},{2,1},{3,2},{4,3},{5,4},{6,5},{7,6},{8,15},{9,8},{10,9... | collective-permute-start | bytes 12296 | tf_op jit(solution)/shard_map/ppermute | solution.py:326
  8.1 0.8 %collective-permute-done.zr_ref = f32[8,128]{1,0:T(8,128)S(1)} collective-permute-done((f32[8,128]{1,0:T(8,128)S(1)}, f32[8,128]{1,0:T(8,128)S(1)}, u32[]{:S(2)}, u32[]{:S(2)}) %collective-permute-start) | collective-permute-done | bytes 4128 | tf_op jit(solution)/shard_map/ppermute | solution.py:326
  8.8 2.7 %collective-permute-start.1 = (f32[7,8,128]{2,1,0:T(8,128)S(1)}, f32[7,8,128]{2,1,0:T(8,128)S(1)}, u32[]{:S(2)}, u32[]{:S(2)}) collective-permute-start(f32[7,8,128]{2,1,0:T(8,128)S(1)} %get-tuple-element.54), channel_id=1, source_target_pairs={{8,16},{24,0},{16,8},{0,24},{9,17},{25,1},{17,9},{1,25},{10,18},{2... | collective-permute-start | bytes 86024 | tf_op jit(solution)/shard_map/ppermute | solution.py:314
  11.6 0.0 collective-permute-start.2
  11.6 0.0 copy-start
  11.6 1.2 %copy-done = bf16[14,8,8,1,4,128]{5,4,3,2,1,0:T(4,128)(2,1)S(1)} copy-done((bf16[14,8,8,1,4,128]{5,4,3,2,1,0:T(4,128)(2,1)S(1)}, bf16[14,8,8,1,4,128]{5,4,3,2,1,0:T(4,128)(2,1)}, u32[]{:S(2)}) %copy-start) | copy-done | bytes 917528
  12.7 0.2 shard_map.68
  12.9 0.0 collective-permute-done.1
  12.9 1.6 %collective-permute-done.2 = f32[7,8,128]{2,1,0:T(8,128)S(1)} collective-permute-done((f32[7,8,128]{2,1,0:T(8,128)S(1)}, f32[7,8,128]{2,1,0:T(8,128)S(1)}, u32[]{:S(2)}, u32[]{:S(2)}) %collective-permute-start.2) | collective-permute-done | bytes 28704 | tf_op jit(solution)/shard_map/ppermute | solution.py:314
  14.6 0.1 shard_map.69.m_ref
  14.7 2.7 %collective-permute-start.4 = (f32[37,8,128]{2,1,0:T(8,128)S(1)}, f32[37,8,128]{2,1,0:T(8,128)S(1)}, u32[]{:S(2)}, u32[]{:S(2)}) collective-permute-start(f32[37,8,128]{2,1,0:T(8,128)S(1)} %shard_map.69.m_ref), channel_id=1, source_target_pairs={{0,32},{64,96},{128,160},{192,224},{32,0},{96,64},{160,128},{224,1... | collective-permute-start | bytes 454664 | tf_op jit(solution)/shard_map/ppermute | solution.py:314
  17.3 1.2 %collective-permute-start.3 = (f32[37,8,128]{2,1,0:T(8,128)S(1)}, f32[37,8,128]{2,1,0:T(8,128)S(1)}, u32[]{:S(2)}, u32[]{:S(2)}) collective-permute-start(f32[37,8,128]{2,1,0:T(8,128)S(1)} %shard_map.69.m_ref), channel_id=1, source_target_pairs={{32,64},{96,128},{160,192},{224,0},{64,32},{128,96},{192,160},{0,2... | collective-permute-start | bytes 454664 | tf_op jit(solution)/shard_map/ppermute | solution.py:314
  18.5 1.2 %shard_map.70 = (f32[12,8,128]{2,1,0:T(8,128)S(1)}, f32[18,8,128]{2,1,0:T(8,128)S(1)}, f32[8,128]{1,0:T(8,128)S(1)}, f32[16,8,128]{2,1,0:T(8,128)S(1)}) custom-call(f32[37,8,128]{2,1,0:T(8,128)S(1)} %shard_map.69.m_ref, f32[4,8,128]{2,1,0:T(8,128)S(1)} %get-tuple-element.25.ownx_ref, f32[3584,128]{1,0:T(8,128)S(1)} %get-tuple-element.26.th_ref), custom_call_target="tpu_custom_call" | custom-call | tf_op jit(solution)/shard_map/pallas_call | solution.py:299
  19.7 0.0 collective-permute-done.4.x_ref
  19.8 1.0 %shard_map.71 = (f32[12,8,128]{2,1,0:T(8,128)S(1)}, f32[18,8,128]{2,1,0:T(8,128)S(1)}, f32[8,128]{1,0:T(8,128)S(1)}, f32[16,8,128]{2,1,0:T(8,128)S(1)}) custom-call(f32[37,8,128]{2,1,0:T(8,128)S(1)} %shard_map.69.m_ref, f32[4,8,128]{2,1,0:T(8,128)S(1)} %get-tuple-element.25.ownx_ref, f32[3584,128]{1,0:T(8,128)S(1)} %get-tuple-element.26.th_ref, ...), custom_call_target="tpu_custom_call" | custom-call | tf_op jit(solution)/shard_map/pallas_call | solution.py:299
  20.8 1.5 %collective-permute-done.3.x_ref = f32[37,8,128]{2,1,0:T(8,128)S(1)} collective-permute-done((f32[37,8,128]{2,1,0:T(8,128)S(1)}, f32[37,8,128]{2,1,0:T(8,128)S(1)}, u32[]{:S(2)}, u32[]{:S(2)}) %collective-permute-start.3) | collective-permute-done | bytes 151584 | tf_op jit(solution)/shard_map/ppermute | solution.py:314
  22.3 2.1 %shard_map.72 = (f32[12,8,128]{2,1,0:T(8,128)S(1)}, f32[18,8,128]{2,1,0:T(8,128)S(1)}, f32[256,128]{1,0:T(8,128)}) custom-call(f32[37,8,128]{2,1,0:T(8,128)S(1)} %shard_map.69.m_ref, f32[4,8,128]{2,1,0:T(8,128)S(1)} %get-tuple-element.25.ownx_ref, f32[3584,128]{1,0:T(8,128)S(1)} %get-tuple-element.26.th_ref, f32[37,8,128]{2,1,0:T(8,128)S(1)} %collective-permute-done.3.x_ref, ...), custom_call_target="tpu_custom_call" | custom-call | tf_op jit(solution)/shard_map/pallas_call | solution.py:299
  24.4 0.6 %collective-permute-start.5 = (f32[18,8,128]{2,1,0:T(8,128)S(1)}, f32[18,8,128]{2,1,0:T(8,128)S(1)}, u32[]{:S(2)}, u32[]{:S(2)}) collective-permute-start(f32[18,8,128]{2,1,0:T(8,128)S(1)} %get-tuple-element.35), channel_id=1, source_target_pairs={{32,64},{96,128},{160,192},{224,0},{64,32},{128,96},{192,160},{0,2... | collective-permute-start | bytes 221192 | tf_op jit(solution)/shard_map/ppermute | solution.py:314
  24.9 3.2 %collective-permute-start.6 = (f32[18,8,128]{2,1,0:T(8,128)S(1)}, f32[18,8,128]{2,1,0:T(8,128)S(1)}, u32[]{:S(2)}, u32[]{:S(2)}) collective-permute-start(f32[18,8,128]{2,1,0:T(8,128)S(1)} %get-tuple-element.36), channel_id=1, source_target_pairs={{0,32},{64,96},{128,160},{192,224},{32,0},{96,64},{160,128},{224,1... | collective-permute-start | bytes 221192 | tf_op jit(solution)/shard_map/ppermute | solution.py:314
  28.1 6.3 %all-to-all-start = ((f32[256,1,128]{2,1,0:T(1,128)}), f32[256,1,128]{2,1,0:T(1,128)S(1)}, u32[]{:S(2)}, u32[]{:S(2)}) async-start(f32[256,1,128]{2,1,0:T(1,128)} %bitcast.6), calls=%async_computation | async-start | bytes 262144 | tf_op jit(solution)/shard_map/all_to_all | solution.py:368
  34.4 0.0 collective-permute-done.5
  34.4 0.0 collective-permute-done.6
  34.5 2.7 %collective-permute-start.7 = (f32[3,8,128]{2,1,0:T(8,128)S(1)}, f32[3,8,128]{2,1,0:T(8,128)S(1)}, u32[]{:S(2)}, u32[]{:S(2)}) collective-permute-start(f32[3,8,128]{2,1,0:T(8,128)S(1)} %get-tuple-element.50), channel_id=1, source_target_pairs={{8,16},{24,0},{16,8},{0,24},{9,17},{25,1},{17,9},{1,25},{10,18},{2... | collective-permute-start | bytes 36872 | tf_op jit(solution)/shard_map/ppermute | solution.py:314
  37.2 0.0 collective-permute-start.8
  37.2 1.4 %collective-permute-done.7 = f32[3,8,128]{2,1,0:T(8,128)S(1)} collective-permute-done((f32[3,8,128]{2,1,0:T(8,128)S(1)}, f32[3,8,128]{2,1,0:T(8,128)S(1)}, u32[]{:S(2)}, u32[]{:S(2)}) %collective-permute-start.7) | collective-permute-done | bytes 12320 | tf_op jit(solution)/shard_map/ppermute | solution.py:314
  38.6 1.4 %collective-permute-done.8 = f32[3,8,128]{2,1,0:T(8,128)S(1)} collective-permute-done((f32[3,8,128]{2,1,0:T(8,128)S(1)}, f32[3,8,128]{2,1,0:T(8,128)S(1)}, u32[]{:S(2)}, u32[]{:S(2)}) %collective-permute-start.8) | collective-permute-done | bytes 12320 | tf_op jit(solution)/shard_map/ppermute | solution.py:314
  40.0 7.4 %all-to-all-done = f32[256,1,128]{2,1,0:T(1,128)S(1)} async-done(((f32[256,1,128]{2,1,0:T(1,128)}), f32[256,1,128]{2,1,0:T(1,128)S(1)}, u32[]{:S(2)}, u32[]{:S(2)}) %all-to-all-start) | async-done | bytes 131104 | tf_op jit(solution)/shard_map/all_to_all | solution.py:368
  47.5 0.8 %shard_map.73 = (f32[3,32,128]{2,1,0:T(8,128)}, f32[3,3]{1,0:T(4,128)}, f32[1,1]{1,0:T(1,128)}) custom-call(f32[12,8,128]{2,1,0:T(8,128)S(1)} %get-tuple-element.33.d_ref, f32[18,8,128]{2,1,0:T(8,128)S(1)} %add_add_fusion.s_ref, f32[3,8,128]{2,1,0:T(8,128)S(1)} %get-tuple-element.56.ym_ref, f32[3,8,128]{2,1,0:T(8,128)S(1)} %get-tuple-element.55.yp_ref, ...), custom_call_target="tpu_custom_call" | custom-call | tf_op jit(solution)/shard_map/pallas_call | solution.py:299
  (6 shorter events, 0.0 us)
Async XLA Ops:
  1.6 7.2 %collective-permute-start = (f32[8,128]{1,0:T(8,128)S(1)}, f32[8,128]{1,0:T(8,128)S(1)}, u32[]{:S(2)}, u32[]{:S(2)}) collective-permute-start(f32[8,128]{1,0:T(8,128)S(1)} %get-tuple-element.23), channel_id=1, source_target_pairs={{0,7},{1,0},{2,1},{3,2},{4,3},{5,4},{6,5},{7,6},{8,15},{9,8},{10,9... | collective-permute-start | bytes 12296 | tf_op jit(solution)/shard_map/ppermute | solution.py:326
  8.8 4.1 %collective-permute-start.1 = (f32[7,8,128]{2,1,0:T(8,128)S(1)}, f32[7,8,128]{2,1,0:T(8,128)S(1)}, u32[]{:S(2)}, u32[]{:S(2)}) collective-permute-start(f32[7,8,128]{2,1,0:T(8,128)S(1)} %get-tuple-element.54), channel_id=1, source_target_pairs={{8,16},{24,0},{16,8},{0,24},{9,17},{25,1},{17,9},{1,25},{10,18},{2... | collective-permute-start | bytes 86024 | tf_op jit(solution)/shard_map/ppermute | solution.py:314
  11.6 3.0 %collective-permute-start.2 = (f32[7,8,128]{2,1,0:T(8,128)S(1)}, f32[7,8,128]{2,1,0:T(8,128)S(1)}, u32[]{:S(2)}, u32[]{:S(2)}) collective-permute-start(f32[7,8,128]{2,1,0:T(8,128)S(1)} %get-tuple-element.53), channel_id=1, source_target_pairs={{0,8},{16,24},{8,0},{24,16},{1,9},{17,25},{9,1},{25,17},{2,10},{18... | collective-permute-start | bytes 86024 | tf_op jit(solution)/shard_map/ppermute | solution.py:314
  11.6 1.2 %copy-start = (bf16[14,8,8,1,4,128]{5,4,3,2,1,0:T(4,128)(2,1)S(1)}, bf16[14,8,8,1,4,128]{5,4,3,2,1,0:T(4,128)(2,1)}, u32[]{:S(2)}) copy-start(bf16[14,8,8,1,4,128]{5,4,3,2,1,0:T(4,128)(2,1)} %param.7) | copy-start | bytes 2752516
  14.7 5.1 %collective-permute-start.4 = (f32[37,8,128]{2,1,0:T(8,128)S(1)}, f32[37,8,128]{2,1,0:T(8,128)S(1)}, u32[]{:S(2)}, u32[]{:S(2)}) collective-permute-start(f32[37,8,128]{2,1,0:T(8,128)S(1)} %shard_map.69.m_ref), channel_id=1, source_target_pairs={{0,32},{64,96},{128,160},{192,224},{32,0},{96,64},{160,128},{224,1... | collective-permute-start | bytes 454664 | tf_op jit(solution)/shard_map/ppermute | solution.py:314
  17.3 4.9 %collective-permute-start.3 = (f32[37,8,128]{2,1,0:T(8,128)S(1)}, f32[37,8,128]{2,1,0:T(8,128)S(1)}, u32[]{:S(2)}, u32[]{:S(2)}) collective-permute-start(f32[37,8,128]{2,1,0:T(8,128)S(1)} %shard_map.69.m_ref), channel_id=1, source_target_pairs={{32,64},{96,128},{160,192},{224,0},{64,32},{128,96},{192,160},{0,2... | collective-permute-start | bytes 454664 | tf_op jit(solution)/shard_map/ppermute | solution.py:314
  24.4 10.1 %collective-permute-start.5 = (f32[18,8,128]{2,1,0:T(8,128)S(1)}, f32[18,8,128]{2,1,0:T(8,128)S(1)}, u32[]{:S(2)}, u32[]{:S(2)}) collective-permute-start(f32[18,8,128]{2,1,0:T(8,128)S(1)} %get-tuple-element.35), channel_id=1, source_target_pairs={{32,64},{96,128},{160,192},{224,0},{64,32},{128,96},{192,160},{0,2... | collective-permute-start | bytes 221192 | tf_op jit(solution)/shard_map/ppermute | solution.py:314
  24.9 9.5 %collective-permute-start.6 = (f32[18,8,128]{2,1,0:T(8,128)S(1)}, f32[18,8,128]{2,1,0:T(8,128)S(1)}, u32[]{:S(2)}, u32[]{:S(2)}) collective-permute-start(f32[18,8,128]{2,1,0:T(8,128)S(1)} %get-tuple-element.36), channel_id=1, source_target_pairs={{0,32},{64,96},{128,160},{192,224},{32,0},{96,64},{160,128},{224,1... | collective-permute-start | bytes 221192 | tf_op jit(solution)/shard_map/ppermute | solution.py:314
  28.1 19.3 %all-to-all-start = ((f32[256,1,128]{2,1,0:T(1,128)}), f32[256,1,128]{2,1,0:T(1,128)S(1)}, u32[]{:S(2)}, u32[]{:S(2)}) async-start(f32[256,1,128]{2,1,0:T(1,128)} %bitcast.6), calls=%async_computation | async-start | bytes 262144 | tf_op jit(solution)/shard_map/all_to_all | solution.py:368
  34.5 4.2 %collective-permute-start.7 = (f32[3,8,128]{2,1,0:T(8,128)S(1)}, f32[3,8,128]{2,1,0:T(8,128)S(1)}, u32[]{:S(2)}, u32[]{:S(2)}) collective-permute-start(f32[3,8,128]{2,1,0:T(8,128)S(1)} %get-tuple-element.50), channel_id=1, source_target_pairs={{8,16},{24,0},{16,8},{0,24},{9,17},{25,1},{17,9},{1,25},{10,18},{2... | collective-permute-start | bytes 36872 | tf_op jit(solution)/shard_map/ppermute | solution.py:314
  37.2 2.9 %collective-permute-start.8 = (f32[3,8,128]{2,1,0:T(8,128)S(1)}, f32[3,8,128]{2,1,0:T(8,128)S(1)}, u32[]{:S(2)}, u32[]{:S(2)}) collective-permute-start(f32[3,8,128]{2,1,0:T(8,128)S(1)} %get-tuple-element.49), channel_id=1, source_target_pairs={{0,8},{16,24},{8,0},{24,16},{1,9},{17,25},{9,1},{25,17},{2,10},{18... | collective-permute-start | bytes 36872 | tf_op jit(solution)/shard_map/ppermute | solution.py:314

commit v6 on v5

--- a/solution.py
+++ b/solution.py
@@ -77,7 +77,7 @@
     @pl.loop(0, th_ref.shape[0] // 256)
     def _(i):
         at = pl.ds(pl.multiple_of(i * 256, 256), 256)
-        th_ref[at, :] = noise_ref[at, :].astype(jnp.float32)
+        th_ref[at, :] = noise_ref[at, :].astype(jnp.float32) + REST
 
 
 def widen_kernel(v_ref, zr_ref, ym_ref, yp_ref, ready_ref, m_ref):
@@ -131,8 +131,8 @@
             dot = sep[0] * rel[0] + sep[1] * rel[1] + sep[2] * rel[2]
             theta = th_ref[pl.ds(k * 256 + s * 32 + y, SLOTS, stride=ROWS), :]
             if self_tile:
-                theta = (theta + th_ref[pl.ds(s * ROWS + y, SLOTS, stride=32), :]) * HALF_ROOT
-            fr = u * ((theta + REST) - u * dot)
+                theta = (theta + th_ref[pl.ds(s * ROWS + y, SLOTS, stride=32), :]) * HALF_ROOT + REST * (1.0 - 2.0 * HALF_ROOT)
+            fr = u * (theta - u * dot)
             if self_tile:
                 fr = jnp.where(slot > s, fr, 0.0)
             for a in range(3):

time: 48.5 us -> 48.4 us (level)
  no operation moved by 1% of the time
where the time goes in v6:
time: 48.4 us; the launch traced here: 48.2 us
  starting transfers between devices  25.9 us (54%)
  waiting for transfers between devices  14.1 us (29%)
  Pallas kernels  6.29 us (13%)
  local copies, waits for them, and re-layouts  1.18 us (2%)
  between operations  0.72 us (1%)
    ppermute x8, starting transfers between devices, swapped(): return lax.ppermute(shard, axis, pairs + [(j, i) for i, j in pairs])  13.1 us
    all_to_all x1, waiting for transfers between devices, per_device(): tallies = lax.all_to_all(tally, AXES, 0, 0, tiled=True)  7.42 us
    ppermute x1, starting transfers between devices, shifted(): lax.ppermute(shard, axis, [(i, (i + by) % count) for i in range(count)])  6.47 us
    pallas_call x7, Pallas kernels, run(): pl.pallas_call(kernel, out_shape=out_shape, in_specs=[pl.BlockSpec(memory...  6.29 us
    all_to_all x1, starting transfers between devices, per_device(): tallies = lax.all_to_all(tally, AXES, 0, 0, tiled=True)  6.26 us
    ppermute x8, waiting for transfers between devices, swapped(): return lax.ppermute(shard, axis, pairs + [(j, i) for i, j in pairs])  5.98 us
    unnamed x2, local copies, waits for them, and re-layouts  1.18 us
  transfers between devices with their start and end apart: 10, of which 6 were waited for; matrix products, arithmetic and copies ran while one was open for 0% of the time, Pallas kernels for 5%

profile of v6, /device:TPU:1, one launch (start us, length us, event | category | flops | bytes accessed | tf_op | source)
XLA Modules:
  0.0 48.2 jit_solution(16715577549741166619)
XLA Ops:
  0.6 0.9 %shard_map.67 = (f32[24,8,128]{2,1,0:T(8,128)S(1)}, f32[4,8,128]{2,1,0:T(8,128)S(1)}, f32[8,128]{1,0:T(8,128)S(1)}) custom-call(f32[3,32,128]{2,1,0:T(8,128)} %bitcast.16, f32[3,32,128]{2,1,0:T(8,128)} %bitcast.17, s32[4,128]{1,0:T(4,128)} %bitcast.18), custom_call_target="tpu_custom_call" | custom-call | tf_op jit(solution)/shard_map/pallas_call | solution.py:299
  1.6 6.5 %collective-permute-start = (f32[8,128]{1,0:T(8,128)S(1)}, f32[8,128]{1,0:T(8,128)S(1)}, u32[]{:S(2)}, u32[]{:S(2)}) collective-permute-start(f32[8,128]{1,0:T(8,128)S(1)} %get-tuple-element.23), channel_id=1, source_target_pairs={{0,7},{1,0},{2,1},{3,2},{4,3},{5,4},{6,5},{7,6},{8,15},{9,8},{10,9... | collective-permute-start | bytes 12296 | tf_op jit(solution)/shard_map/ppermute | solution.py:326
  8.1 0.8 %collective-permute-done.zr_ref = f32[8,128]{1,0:T(8,128)S(1)} collective-permute-done((f32[8,128]{1,0:T(8,128)S(1)}, f32[8,128]{1,0:T(8,128)S(1)}, u32[]{:S(2)}, u32[]{:S(2)}) %collective-permute-start) | collective-permute-done | bytes 4128 | tf_op jit(solution)/shard_map/ppermute | solution.py:326
  8.8 2.7 %collective-permute-start.1 = (f32[7,8,128]{2,1,0:T(8,128)S(1)}, f32[7,8,128]{2,1,0:T(8,128)S(1)}, u32[]{:S(2)}, u32[]{:S(2)}) collective-permute-start(f32[7,8,128]{2,1,0:T(8,128)S(1)} %get-tuple-element.54), channel_id=1, source_target_pairs={{8,16},{24,0},{16,8},{0,24},{9,17},{25,1},{17,9},{1,25},{10,18},{2... | collective-permute-start | bytes 86024 | tf_op jit(solution)/shard_map/ppermute | solution.py:314
  11.6 0.0 collective-permute-start.2
  11.6 0.0 copy-start
  11.6 1.2 %copy-done = bf16[14,8,8,1,4,128]{5,4,3,2,1,0:T(4,128)(2,1)S(1)} copy-done((bf16[14,8,8,1,4,128]{5,4,3,2,1,0:T(4,128)(2,1)S(1)}, bf16[14,8,8,1,4,128]{5,4,3,2,1,0:T(4,128)(2,1)}, u32[]{:S(2)}) %copy-start) | copy-done | bytes 917528
  12.7 0.2 shard_map.68
  13.0 0.0 collective-permute-done.1
  13.0 1.6 %collective-permute-done.2 = f32[7,8,128]{2,1,0:T(8,128)S(1)} collective-permute-done((f32[7,8,128]{2,1,0:T(8,128)S(1)}, f32[7,8,128]{2,1,0:T(8,128)S(1)}, u32[]{:S(2)}, u32[]{:S(2)}) %collective-permute-start.2) | collective-permute-done | bytes 28704 | tf_op jit(solution)/shard_map/ppermute | solution.py:314
  14.6 0.1 shard_map.69.m_ref
  14.7 2.7 %collective-permute-start.4 = (f32[37,8,128]{2,1,0:T(8,128)S(1)}, f32[37,8,128]{2,1,0:T(8,128)S(1)}, u32[]{:S(2)}, u32[]{:S(2)}) collective-permute-start(f32[37,8,128]{2,1,0:T(8,128)S(1)} %shard_map.69.m_ref), channel_id=1, source_target_pairs={{0,32},{64,96},{128,160},{192,224},{32,0},{96,64},{160,128},{224,1... | collective-permute-start | bytes 454664 | tf_op jit(solution)/shard_map/ppermute | solution.py:314
  17.3 1.2 %collective-permute-start.3 = (f32[37,8,128]{2,1,0:T(8,128)S(1)}, f32[37,8,128]{2,1,0:T(8,128)S(1)}, u32[]{:S(2)}, u32[]{:S(2)}) collective-permute-start(f32[37,8,128]{2,1,0:T(8,128)S(1)} %shard_map.69.m_ref), channel_id=1, source_target_pairs={{32,64},{96,128},{160,192},{224,0},{64,32},{128,96},{192,160},{0,2... | collective-permute-start | bytes 454664 | tf_op jit(solution)/shard_map/ppermute | solution.py:314
  18.5 1.2 %shard_map.70 = (f32[12,8,128]{2,1,0:T(8,128)S(1)}, f32[18,8,128]{2,1,0:T(8,128)S(1)}, f32[8,128]{1,0:T(8,128)S(1)}, f32[16,8,128]{2,1,0:T(8,128)S(1)}) custom-call(f32[37,8,128]{2,1,0:T(8,128)S(1)} %shard_map.69.m_ref, f32[4,8,128]{2,1,0:T(8,128)S(1)} %get-tuple-element.25.ownx_ref, f32[3584,128]{1,0:T(8,128)S(1)} %get-tuple-element.26.th_ref), custom_call_target="tpu_custom_call" | custom-call | tf_op jit(solution)/shard_map/pallas_call | solution.py:299
  19.7 0.0 collective-permute-done.4.x_ref
  19.7 1.0 %shard_map.71 = (f32[12,8,128]{2,1,0:T(8,128)S(1)}, f32[18,8,128]{2,1,0:T(8,128)S(1)}, f32[8,128]{1,0:T(8,128)S(1)}, f32[16,8,128]{2,1,0:T(8,128)S(1)}) custom-call(f32[37,8,128]{2,1,0:T(8,128)S(1)} %shard_map.69.m_ref, f32[4,8,128]{2,1,0:T(8,128)S(1)} %get-tuple-element.25.ownx_ref, f32[3584,128]{1,0:T(8,128)S(1)} %get-tuple-element.26.th_ref, ...), custom_call_target="tpu_custom_call" | custom-call | tf_op jit(solution)/shard_map/pallas_call | solution.py:299
  20.7 1.5 %collective-permute-done.3.x_ref = f32[37,8,128]{2,1,0:T(8,128)S(1)} collective-permute-done((f32[37,8,128]{2,1,0:T(8,128)S(1)}, f32[37,8,128]{2,1,0:T(8,128)S(1)}, u32[]{:S(2)}, u32[]{:S(2)}) %collective-permute-start.3) | collective-permute-done | bytes 151584 | tf_op jit(solution)/shard_map/ppermute | solution.py:314
  22.3 2.1 %shard_map.72 = (f32[12,8,128]{2,1,0:T(8,128)S(1)}, f32[18,8,128]{2,1,0:T(8,128)S(1)}, f32[256,128]{1,0:T(8,128)}) custom-call(f32[37,8,128]{2,1,0:T(8,128)S(1)} %shard_map.69.m_ref, f32[4,8,128]{2,1,0:T(8,128)S(1)} %get-tuple-element.25.ownx_ref, f32[3584,128]{1,0:T(8,128)S(1)} %get-tuple-element.26.th_ref, f32[37,8,128]{2,1,0:T(8,128)S(1)} %collective-permute-done.3.x_ref, ...), custom_call_target="tpu_custom_call" | custom-call | tf_op jit(solution)/shard_map/pallas_call | solution.py:299
  24.3 0.6 %collective-permute-start.5 = (f32[18,8,128]{2,1,0:T(8,128)S(1)}, f32[18,8,128]{2,1,0:T(8,128)S(1)}, u32[]{:S(2)}, u32[]{:S(2)}) collective-permute-start(f32[18,8,128]{2,1,0:T(8,128)S(1)} %get-tuple-element.35), channel_id=1, source_target_pairs={{32,64},{96,128},{160,192},{224,0},{64,32},{128,96},{192,160},{0,2... | collective-permute-start | bytes 221192 | tf_op jit(solution)/shard_map/ppermute | solution.py:314
  24.9 3.2 %collective-permute-start.6 = (f32[18,8,128]{2,1,0:T(8,128)S(1)}, f32[18,8,128]{2,1,0:T(8,128)S(1)}, u32[]{:S(2)}, u32[]{:S(2)}) collective-permute-start(f32[18,8,128]{2,1,0:T(8,128)S(1)} %get-tuple-element.36), channel_id=1, source_target_pairs={{0,32},{64,96},{128,160},{192,224},{32,0},{96,64},{160,128},{224,1... | collective-permute-start | bytes 221192 | tf_op jit(solution)/shard_map/ppermute | solution.py:314
  28.1 6.3 %all-to-all-start = ((f32[256,1,128]{2,1,0:T(1,128)}), f32[256,1,128]{2,1,0:T(1,128)S(1)}, u32[]{:S(2)}, u32[]{:S(2)}) async-start(f32[256,1,128]{2,1,0:T(1,128)} %bitcast.6), calls=%async_computation | async-start | bytes 262144 | tf_op jit(solution)/shard_map/all_to_all | solution.py:368
  34.4 0.0 collective-permute-done.5
  34.4 0.0 collective-permute-done.6
  34.4 2.7 %collective-permute-start.7 = (f32[3,8,128]{2,1,0:T(8,128)S(1)}, f32[3,8,128]{2,1,0:T(8,128)S(1)}, u32[]{:S(2)}, u32[]{:S(2)}) collective-permute-start(f32[3,8,128]{2,1,0:T(8,128)S(1)} %get-tuple-element.50), channel_id=1, source_target_pairs={{8,16},{24,0},{16,8},{0,24},{9,17},{25,1},{17,9},{1,25},{10,18},{2... | collective-permute-start | bytes 36872 | tf_op jit(solution)/shard_map/ppermute | solution.py:314
  37.1 0.0 collective-permute-start.8
  37.1 1.4 %collective-permute-done.7 = f32[3,8,128]{2,1,0:T(8,128)S(1)} collective-permute-done((f32[3,8,128]{2,1,0:T(8,128)S(1)}, f32[3,8,128]{2,1,0:T(8,128)S(1)}, u32[]{:S(2)}, u32[]{:S(2)}) %collective-permute-start.7) | collective-permute-done | bytes 12320 | tf_op jit(solution)/shard_map/ppermute | solution.py:314
  38.6 1.4 %collective-permute-done.8 = f32[3,8,128]{2,1,0:T(8,128)S(1)} collective-permute-done((f32[3,8,128]{2,1,0:T(8,128)S(1)}, f32[3,8,128]{2,1,0:T(8,128)S(1)}, u32[]{:S(2)}, u32[]{:S(2)}) %collective-permute-start.8) | collective-permute-done | bytes 12320 | tf_op jit(solution)/shard_map/ppermute | solution.py:314
  40.0 7.4 %all-to-all-done = f32[256,1,128]{2,1,0:T(1,128)S(1)} async-done(((f32[256,1,128]{2,1,0:T(1,128)}), f32[256,1,128]{2,1,0:T(1,128)S(1)}, u32[]{:S(2)}, u32[]{:S(2)}) %all-to-all-start) | async-done | bytes 131104 | tf_op jit(solution)/shard_map/all_to_all | solution.py:368
  47.4 0.8 %shard_map.73 = (f32[3,32,128]{2,1,0:T(8,128)}, f32[3,3]{1,0:T(4,128)}, f32[1,1]{1,0:T(1,128)}) custom-call(f32[12,8,128]{2,1,0:T(8,128)S(1)} %get-tuple-element.33.d_ref, f32[18,8,128]{2,1,0:T(8,128)S(1)} %add_add_fusion.s_ref, f32[3,8,128]{2,1,0:T(8,128)S(1)} %get-tuple-element.56.ym_ref, f32[3,8,128]{2,1,0:T(8,128)S(1)} %get-tuple-element.55.yp_ref, ...), custom_call_target="tpu_custom_call" | custom-call | tf_op jit(solution)/shard_map/pallas_call | solution.py:299
  (6 shorter events, 0.0 us)
Async XLA Ops:
  1.6 7.2 %collective-permute-start = (f32[8,128]{1,0:T(8,128)S(1)}, f32[8,128]{1,0:T(8,128)S(1)}, u32[]{:S(2)}, u32[]{:S(2)}) collective-permute-start(f32[8,128]{1,0:T(8,128)S(1)} %get-tuple-element.23), channel_id=1, source_target_pairs={{0,7},{1,0},{2,1},{3,2},{4,3},{5,4},{6,5},{7,6},{8,15},{9,8},{10,9... | collective-permute-start | bytes 12296 | tf_op jit(solution)/shard_map/ppermute | solution.py:326
  8.8 4.1 %collective-permute-start.1 = (f32[7,8,128]{2,1,0:T(8,128)S(1)}, f32[7,8,128]{2,1,0:T(8,128)S(1)}, u32[]{:S(2)}, u32[]{:S(2)}) collective-permute-start(f32[7,8,128]{2,1,0:T(8,128)S(1)} %get-tuple-element.54), channel_id=1, source_target_pairs={{8,16},{24,0},{16,8},{0,24},{9,17},{25,1},{17,9},{1,25},{10,18},{2... | collective-permute-start | bytes 86024 | tf_op jit(solution)/shard_map/ppermute | solution.py:314
  11.6 3.0 %collective-permute-start.2 = (f32[7,8,128]{2,1,0:T(8,128)S(1)}, f32[7,8,128]{2,1,0:T(8,128)S(1)}, u32[]{:S(2)}, u32[]{:S(2)}) collective-permute-start(f32[7,8,128]{2,1,0:T(8,128)S(1)} %get-tuple-element.53), channel_id=1, source_target_pairs={{0,8},{16,24},{8,0},{24,16},{1,9},{17,25},{9,1},{25,17},{2,10},{18... | collective-permute-start | bytes 86024 | tf_op jit(solution)/shard_map/ppermute | solution.py:314
  11.6 1.2 %copy-start = (bf16[14,8,8,1,4,128]{5,4,3,2,1,0:T(4,128)(2,1)S(1)}, bf16[14,8,8,1,4,128]{5,4,3,2,1,0:T(4,128)(2,1)}, u32[]{:S(2)}) copy-start(bf16[14,8,8,1,4,128]{5,4,3,2,1,0:T(4,128)(2,1)} %param.7) | copy-start | bytes 2752516
  14.7 5.1 %collective-permute-start.4 = (f32[37,8,128]{2,1,0:T(8,128)S(1)}, f32[37,8,128]{2,1,0:T(8,128)S(1)}, u32[]{:S(2)}, u32[]{:S(2)}) collective-permute-start(f32[37,8,128]{2,1,0:T(8,128)S(1)} %shard_map.69.m_ref), channel_id=1, source_target_pairs={{0,32},{64,96},{128,160},{192,224},{32,0},{96,64},{160,128},{224,1... | collective-permute-start | bytes 454664 | tf_op jit(solution)/shard_map/ppermute | solution.py:314
  17.3 4.9 %collective-permute-start.3 = (f32[37,8,128]{2,1,0:T(8,128)S(1)}, f32[37,8,128]{2,1,0:T(8,128)S(1)}, u32[]{:S(2)}, u32[]{:S(2)}) collective-permute-start(f32[37,8,128]{2,1,0:T(8,128)S(1)} %shard_map.69.m_ref), channel_id=1, source_target_pairs={{32,64},{96,128},{160,192},{224,0},{64,32},{128,96},{192,160},{0,2... | collective-permute-start | bytes 454664 | tf_op jit(solution)/shard_map/ppermute | solution.py:314
  24.3 10.1 %collective-permute-start.5 = (f32[18,8,128]{2,1,0:T(8,128)S(1)}, f32[18,8,128]{2,1,0:T(8,128)S(1)}, u32[]{:S(2)}, u32[]{:S(2)}) collective-permute-start(f32[18,8,128]{2,1,0:T(8,128)S(1)} %get-tuple-element.35), channel_id=1, source_target_pairs={{32,64},{96,128},{160,192},{224,0},{64,32},{128,96},{192,160},{0,2... | collective-permute-start | bytes 221192 | tf_op jit(solution)/shard_map/ppermute | solution.py:314
  24.9 9.5 %collective-permute-start.6 = (f32[18,8,128]{2,1,0:T(8,128)S(1)}, f32[18,8,128]{2,1,0:T(8,128)S(1)}, u32[]{:S(2)}, u32[]{:S(2)}) collective-permute-start(f32[18,8,128]{2,1,0:T(8,128)S(1)} %get-tuple-element.36), channel_id=1, source_target_pairs={{0,32},{64,96},{128,160},{192,224},{32,0},{96,64},{160,128},{224,1... | collective-permute-start | bytes 221192 | tf_op jit(solution)/shard_map/ppermute | solution.py:314
  28.1 19.3 %all-to-all-start = ((f32[256,1,128]{2,1,0:T(1,128)}), f32[256,1,128]{2,1,0:T(1,128)S(1)}, u32[]{:S(2)}, u32[]{:S(2)}) async-start(f32[256,1,128]{2,1,0:T(1,128)} %bitcast.6), calls=%async_computation | async-start | bytes 262144 | tf_op jit(solution)/shard_map/all_to_all | solution.py:368
  34.4 4.2 %collective-permute-start.7 = (f32[3,8,128]{2,1,0:T(8,128)S(1)}, f32[3,8,128]{2,1,0:T(8,128)S(1)}, u32[]{:S(2)}, u32[]{:S(2)}) collective-permute-start(f32[3,8,128]{2,1,0:T(8,128)S(1)} %get-tuple-element.50), channel_id=1, source_target_pairs={{8,16},{24,0},{16,8},{0,24},{9,17},{25,1},{17,9},{1,25},{10,18},{2... | collective-permute-start | bytes 36872 | tf_op jit(solution)/shard_map/ppermute | solution.py:314
  37.1 2.9 %collective-permute-start.8 = (f32[3,8,128]{2,1,0:T(8,128)S(1)}, f32[3,8,128]{2,1,0:T(8,128)S(1)}, u32[]{:S(2)}, u32[]{:S(2)}) collective-permute-start(f32[3,8,128]{2,1,0:T(8,128)S(1)} %get-tuple-element.49), channel_id=1, source_target_pairs={{0,8},{16,24},{8,0},{24,16},{1,9},{17,25},{9,1},{25,17},{2,10},{18... | collective-permute-start | bytes 36872 | tf_op jit(solution)/shard_map/ppermute | solution.py:314
